TPU v7x, 32 devices: a whole 2x2x4 slice. The times are simulated.
32 devices in a mesh: row: 4 (over y, x), col: 8 (over z, core).
Axes of the slice: x: 2, y: 2, z: 4, core: 2. Of those that a mesh axis runs over, the one named last changes fastest.
Arguments:
- object_field: float32 [2, 1024, 2048], P(None, 'row', 'col'), may hold values from -5 to 5
- velocity: float32 [2, 1024, 2048], P(None, 'row', 'col'), may hold values from -5 to 5
- positions: int32 [4, 8, 1, 2], P('row', 'col'), may hold values from 0 to 128
- measured: float32 [4, 8, 1, 256, 256], P('row', 'col'), may hold values from 0 to 2
- probe: float32 [2, 256, 256], replicated, may hold values from -5 to 5
Outputs:
- object_out: float32 [2, 1024, 2048], P(None, 'row', 'col')
- velocity_out: float32 [2, 1024, 2048], P(None, 'row', 'col')
All inputs are finite; a program needn't handle non-finite values.
Results may differ from a plain program's by a relative error of at most 0.00018.
Values sent between devices are 32-bit elements; how exact they have to be, the bound alone decides.
No kernel may reach another device: no remote copies, remote signals or barrier semaphores. Data moves between devices by JAX's collectives and lax.ppermute only.
A program may use at most 64 MiB of HBM per device.

v0:
```python
import math

import jax
import jax.numpy as jnp
import numpy as np
from jax import lax
from jax.experimental import pallas as pl
from jax.experimental.pallas import tpu as pltpu
from jax.sharding import PartitionSpec as P


P_SIZE = 256
W = 128
ITERS = 2

step_size = 0.1
momentum_rate = 0.8

VMEM = pl.BlockSpec(memory_space=pltpu.VMEM)
SMEM = pl.BlockSpec(memory_space=pltpu.SMEM)
N = P_SIZE
H = P_SIZE // 2


def shifted(value, row_steps, col_steps):
    rows, cols = lax.axis_size("row"), lax.axis_size("col")
    pairs = []
    for r in range(rows):
        for c in range(cols):
            to_r, to_c = r + row_steps, c + col_steps
            if 0 <= to_r < rows and 0 <= to_c < cols:
                pairs.append((r * cols + c, to_r * cols + to_c))
    return lax.ppermute(value, ("row", "col"), pairs)


def constants():
    index = np.arange(H)
    angle = -2.0 * math.pi * (index[:, None] * index[None, :] % H) / H
    scale = 1.0 / math.sqrt(P_SIZE)
    c, s = np.cos(angle) * scale, np.sin(angle) * scale
    pairs = []
    for block in (np.block([[c, s], [-s, c]]), np.block([[c, -s], [s, c]])):
        block = block.astype(np.float32)
        high = block.astype(jnp.bfloat16)
        pairs += [high, (block - high.astype(np.float32)).astype(jnp.bfloat16)]
    turn = -2.0 * math.pi * index / P_SIZE
    twiddle = np.stack([np.cos(turn), np.sin(turn)]).astype(np.float32)
    along_cols = np.broadcast_to(twiddle[:, None, :], (2, 8, H))
    along_rows = np.broadcast_to(twiddle[:, :, None], (2, H, H))
    return np.stack(pairs), np.ascontiguousarray(along_cols), np.ascontiguousarray(along_rows)


def halves(x):
    high = x.astype(jnp.bfloat16)
    return high, (x - high.astype(jnp.float32)).astype(jnp.bfloat16)


def dot(a, b):
    return jnp.dot(a, b, preferred_element_type=jnp.float32)


def times(a, b):
    return dot(a[0], b[0]) + dot(a[0], b[1]) + dot(a[1], b[0])


def quads(q00, q01, q10, q11):
    return jnp.concatenate(
        [jnp.concatenate([q00, q01], axis=1), jnp.concatenate([q10, q11], axis=1)], axis=0
    )


def block_transpose(x):
    return quads(x[:H, :H], x[H:, :H], x[:H, H:], x[H:, H:])


def plus(table_ref):
    return table_ref[0], table_ref[1]


def minus(table_ref):
    return table_ref[2], table_ref[3]


def prep_kernel(pos_ref, probe_ref, meas_ref, table_ref, cols_ref, rows_ref, probe_out, meas_out, table_out, cols_out, rows_out):
    p0 = pos_ref[0]
    p1 = pos_ref[1]
    for part in range(2):
        x = pltpu.roll(probe_ref[part], p0, 0)
        probe_out[part] = pltpu.roll(x, p1, 1)
    first = lax.broadcasted_iota(jnp.int32, (N, N), 0)
    second = lax.broadcasted_iota(jnp.int32, (N, N), 1)

    def evens_first(place):
        return jnp.where(place < H, 2 * place, 2 * (place - H) + 1)

    def moved(x, move):
        high, rest = halves(x)
        mid = x - high.astype(jnp.float32)
        low = (mid - rest.astype(jnp.float32)).astype(jnp.bfloat16)
        return move(high) + (move(rest) + move(low))

    rows_move = jnp.where(second == evens_first(first), 1.0, 0.0).astype(jnp.bfloat16)
    cols_move = jnp.where(first == evens_first(second), 1.0, 0.0).astype(jnp.bfloat16)
    x = moved(meas_ref[...], lambda part: dot(rows_move, part))
    meas_out[...] = moved(x, lambda part: dot(part, cols_move))
    table_out[...] = table_ref[...]
    cols_out[...] = cols_ref[...]
    rows_out[...] = rows_ref[...]


def row_stage(patch, pr, pi, table, w_ref):
    er = pr * patch[0] - pi * patch[1]
    ei = pr * patch[1] + pi * patch[0]
    wr, wi = w_ref[0, 0:1], w_ref[1, 0:1]
    dr, di = er[:, :H] - er[:, H:], ei[:, :H] - ei[:, H:]
    x = quads(
        er[:, :H] + er[:, H:], ei[:, :H] + ei[:, H:], dr * wr - di * wi, dr * wi + di * wr
    )
    return times(halves(x), table)


def back_stage(x, pr, pi, table, w_ref):
    y = times(halves(block_transpose(x)), table)
    wr, wi = w_ref[0, 0:1], w_ref[1, 0:1]
    qr, qi = y[H:, :H], y[H:, H:]
    tr, ti = qr * wr + qi * wi, qi * wr - qr * wi
    br = jnp.concatenate([y[:H, :H] + tr, y[:H, :H] - tr], axis=1)
    bi = jnp.concatenate([y[:H, H:] + ti, y[:H, H:] - ti], axis=1)
    return pr * br + pi * bi, pr * bi - pi * br


def masks(pos_ref):
    row_id = lax.broadcasted_iota(jnp.int32, (H, H), 0)
    col_id = lax.broadcasted_iota(jnp.int32, (H, H), 1)
    return row_id < pos_ref[0], col_id < pos_ref[1]


def pre_kernel(pos_ref, left_ref, right_ref, beside_ref, probe_ref, table_ref, cols_ref, y_ref):
    _, beyond = masks(pos_ref)
    patch = [
        jnp.concatenate(
            [jnp.where(beyond, beside_ref[part, H:], left_ref[part, H:]), right_ref[part, H:]], axis=1
        )
        for part in range(2)
    ]
    y_ref[...] = row_stage(patch, probe_ref[0, H:], probe_ref[1, H:], plus(table_ref), cols_ref)


def main_kernel(split, *refs):
    if split:
        (pos_ref, left_ref, right_ref, lower_ref, beside_ref, corner_ref, probe_ref, meas_ref, yb_ref,
         table_ref, cols_ref, rows_ref, own_out, d00_out, d01_out, diag_out, r00_out, xb_out) = refs
        lower = [[lower_ref[part, :, :H], lower_ref[part, :, H:]] for part in range(2)]
    else:
        (pos_ref, below_ref, left_ref, right_ref, up00_ref, up01_ref, mine01_ref, beside_ref, corner_ref,
         probe_ref, meas_ref, yb_ref, table_ref, cols_ref, rows_ref,
         own_out, down_out, diag_out, r00_out, xb_out) = refs
        scale = jnp.where(below_ref[0] > 0, step_size, 0.0)
        lower = [[up00_ref[part], up01_ref[part] - scale * mine01_ref[part]] for part in range(2)]
    below, beyond = masks(pos_ref)
    pr, pi = probe_ref[0, :H], probe_ref[1, :H]
    patch = []
    for part in range(2):
        q00 = jnp.where(
            below,
            jnp.where(beyond, corner_ref[part], lower[part][0]),
            jnp.where(beyond, beside_ref[part, :H], left_ref[part, :H]),
        )
        q01 = jnp.where(below, lower[part][1], right_ref[part, :H])
        patch.append(jnp.concatenate([q00, q01], axis=1))
    yt = row_stage(patch, pr, pi, plus(table_ref), cols_ref)
    yb = yb_ref[...]
    wr = jnp.concatenate([rows_ref[0], rows_ref[0]], axis=0)
    wi = jnp.concatenate([rows_ref[1], rows_ref[1]], axis=0)
    diff = yt - yb
    dr, di = diff[:, :H], diff[:, H:]
    odd = jnp.concatenate([dr * wr - di * wi, dr * wi + di * wr], axis=1)
    back = []
    for parity, x in enumerate((yt + yb, odd)):
        z = times(minus(table_ref), halves(block_transpose(x)))
        zr, zi = z[:H], z[H:]
        misfit = zr * zr + zi * zi - meas_ref[parity * H : (parity + 1) * H]
        g = jnp.concatenate([misfit * zr, misfit * zi], axis=0)
        back.append(times(plus(table_ref), halves(g)))
    qr, qi = back[1][:H], back[1][H:]
    wr = jnp.concatenate([rows_ref[0], rows_ref[0]], axis=1)
    wi = jnp.concatenate([rows_ref[1], rows_ref[1]], axis=1)
    turned = jnp.concatenate([qr * wr + qi * wi, qi * wr - qr * wi], axis=0)
    xb_out[...] = back[0] - turned
    out = back_stage(back[0] + turned, pr, pi, minus(table_ref), cols_ref)
    for part in range(2):
        g00, g01 = out[part][:, :H], out[part][:, H:]
        own_out[part, :, :H] = jnp.where(jnp.logical_or(below, beyond), 0.0, g00)
        own_out[part, :, H:] = jnp.where(below, 0.0, g01)
        d00 = jnp.where(jnp.logical_and(below, ~beyond), g00, 0.0)
        d01 = jnp.where(below, g01, 0.0)
        if split:
            d00_out[part] = d00
            d01_out[part] = d01
        else:
            down_out[part, :, :H] = d00
            down_out[part, :, H:] = d01
        diag_out[part] = jnp.where(jnp.logical_and(below, beyond), g00, 0.0)
        r00_out[part] = jnp.where(jnp.logical_and(~below, beyond), g00, 0.0)


def post_kernel(pos_ref, xb_ref, r00_ref, probe_ref, table_ref, cols_ref, own_out, right_out):
    _, beyond = masks(pos_ref)
    out = back_stage(xb_ref[...], probe_ref[0, H:], probe_ref[1, H:], minus(table_ref), cols_ref)
    for part in range(2):
        g10, g11 = out[part][:, :H], out[part][:, H:]
        own_out[part, :, :H] = jnp.where(beyond, 0.0, g10)
        own_out[part, :, H:] = g11
        right_out[part, :H] = r00_ref[part]
        right_out[part, H:] = jnp.where(beyond, g10, 0.0)


def stepped(obj, vel, g):
    vel = momentum_rate * vel + g
    return obj - step_size * vel, vel


def ahead_kernel(right_ref, vel_ref, own_ref, up_out):
    for part in range(2):
        up_out[part], _ = stepped(right_ref[part, :H], vel_ref[part, :H, H:], own_ref[part, :, H:])


def left_update_kernel(left_ref, vel_ref, top_ref, bottom_ref, d00_ref, before_ref, diag_ref, obj_out, q00_out, vel_out):
    for part in range(2):
        g00 = (top_ref[part, :, :H] + d00_ref[part]) + (before_ref[part, :H] + diag_ref[part])
        g10 = bottom_ref[part, :, :H] + before_ref[part, H:]
        obj, vel = stepped(left_ref[part, :H], vel_ref[part, :H, :H], g00)
        obj_out[part, :H] = obj
        q00_out[part] = obj
        vel_out[part, :H] = vel
        obj_out[part, H:], vel_out[part, H:] = stepped(left_ref[part, H:], vel_ref[part, H:, :H], g10)


def right_update_kernel(right_ref, vel_ref, top_ref, bottom_ref, d01_ref, obj_out, vel_out):
    for part in range(2):
        g01 = top_ref[part, :, H:] + d01_ref[part]
        obj_out[part, :H], vel_out[part, :H] = stepped(right_ref[part, :H], vel_ref[part, :H, H:], g01)
        obj_out[part, H:], vel_out[part, H:] = stepped(
            right_ref[part, H:], vel_ref[part, H:, H:], bottom_ref[part, :, H:]
        )


def final_kernel(left_ref, right_ref, vl_ref, vr_ref, top_ref, bottom_ref, above_ref, before_ref, diag_ref, obj_out, vel_out):
    for part in range(2):
        g00 = (top_ref[part, :, :H] + above_ref[part, :, :H]) + (before_ref[part, :H] + diag_ref[part])
        g01 = top_ref[part, :, H:] + above_ref[part, :, H:]
        g10 = bottom_ref[part, :, :H] + before_ref[part, H:]
        g11 = bottom_ref[part, :, H:]
        for rows, g_left, g_right in ((slice(0, H), g00, g01), (slice(H, N), g10, g11)):
            obj_out[part, rows, :H], vel_out[part, rows, :H] = stepped(left_ref[part, rows], vl_ref[part, rows], g_left)
            obj_out[part, rows, H:], vel_out[part, rows, H:] = stepped(right_ref[part, rows], vr_ref[part, rows], g_right)


def shape(*dims, dtype=jnp.float32):
    return jax.ShapeDtypeStruct(dims, dtype)


def kernel(body, name, flops, scalars, arrays, outs):
    return pl.pallas_call(
        body,
        out_shape=outs,
        in_specs=[SMEM] * scalars + [VMEM] * arrays,
        out_specs=(VMEM,) * len(outs),
        compiler_params=pltpu.CompilerParams(vmem_limit_bytes=16 * 1024 * 1024),
        cost_estimate=pl.CostEstimate(flops=flops, bytes_accessed=10**6, transcendentals=0),
        name=name,
    )


def on_device(object_field, velocity, positions, measured, probe):
    tables, along_cols, along_rows = (jnp.asarray(x) for x in constants())
    offsets = positions[0, 0, 0]
    intensity = measured[0, 0, 0]
    has_below = (lax.axis_index("row") < lax.axis_size("row") - 1).astype(jnp.int32).reshape(1)
    half, strip, quad, rows = shape(2, N, H), shape(2, H, N), shape(2, H, H), shape(N, N)

    left, right = object_field[:, :, :H], object_field[:, :, H:]
    lower = shifted(object_field[:, :H, :], -1, 0)
    corner = shifted(object_field[:, :H, :H], -1, -1)
    beside = shifted(left, 0, -1)
    turned, intensity, tables, along_cols, along_rows = kernel(
        prep_kernel, "prep", 10**8, 1, 5,
        (shape(2, N, N), rows, shape(4, N, N, dtype=jnp.bfloat16), shape(2, 8, H), shape(2, H, H)),
    )(offsets, probe, intensity, tables, along_cols, along_rows)
    pre = kernel(pre_kernel, "pre", 10**8, 1, 6, (rows,))
    post = kernel(post_kernel, "post", 10**8, 1, 5, (strip, half))

    (yb,) = pre(offsets, left, right, beside, turned, tables, along_cols)
    top, d00, d01, diag, r00, xb = kernel(
        lambda *refs: main_kernel(True, *refs), "main_first", 10**9, 1, 11, (strip, quad, quad, quad, quad, rows)
    )(offsets, left, right, lower, beside, corner, turned, intensity, yb, tables, along_cols, along_rows)
    from_above = shifted(d00, 1, 0)
    from_corner = shifted(diag, 1, 1)
    bottom, right_part = post(offsets, xb, r00, turned, tables, along_cols)
    before = shifted(right_part, 0, 1)
    above01 = shifted(d01, 1, 0)
    (ahead,) = kernel(ahead_kernel, "ahead", 10**6, 0, 3, (quad,))(right, velocity, top)
    up01 = shifted(ahead, -1, 0)

    left, q00, vel_left = kernel(left_update_kernel, "left_update", 10**6, 0, 7, (half, quad, half))(
        left, velocity, top, bottom, from_above, before, from_corner
    )
    up00 = shifted(q00, -1, 0)
    corner = shifted(q00, -1, -1)
    beside = shifted(left, 0, -1)
    right, vel_right = kernel(right_update_kernel, "right_update", 10**6, 0, 5, (half, half))(
        right, velocity, top, bottom, above01
    )

    (yb,) = pre(offsets, left, right, beside, turned, tables, along_cols)
    top, down, diag, r00, xb = kernel(
        lambda *refs: main_kernel(False, *refs), "main_last", 10**9, 2, 13, (strip, strip, quad, quad, rows)
    )(offsets, has_below, left, right, up00, up01, d01, beside, corner, turned, intensity, yb, tables, along_cols, along_rows)
    above = shifted(down, 1, 0)
    from_corner = shifted(diag, 1, 1)
    bottom, right_part = post(offsets, xb, r00, turned, tables, along_cols)
    before = shifted(right_part, 0, 1)
    return kernel(final_kernel, "final", 10**6, 0, 9, (shape(2, N, N), shape(2, N, N)))(
        left, right, vel_left, vel_right, top, bottom, above, before, from_corner
    )


def solution(mesh):
    placed = (
        P(None, "row", "col"),
        P(None, "row", "col"),
        P("row", "col", None, None),
        P("row", "col", None, None, None),
        P(),
    )
    return jax.shard_map(
        on_device,
        mesh=mesh,
        in_specs=placed,
        out_specs=(P(None, "row", "col"), P(None, "row", "col")),
        check_vma=False,
    )
```

profile of v0, /device:TPU:11, one launch (start us, length us, event | category | flops | bytes accessed | tf_op | source)
XLA Modules:
  0.0 76.4 jit_solution(16350123444080705209)
XLA Ops:
  0.7 1.1 %fusion = (f32[2,256,128]{2,1,0:T(8,128)S(1)}, f32[2,256,128]{2,1,0:T(8,128)S(1)}) fusion(f32[2,256,256]{2,1,0:T(8,128)} %param.8), kind=kLoop, calls=%fused_computation | loop fusion | bytes 1048576 | tf_op jit(solution)/shard_map/slice | solution.py:282
  1.8 2.7 %collective-permute-start.1 = (f32[2,256,128]{2,1,0:T(8,128)S(1)}, f32[2,256,128]{2,1,0:T(8,128)S(1)}, u32[]{:S(2)}, u32[]{:S(2)}) collective-permute-start(f32[2,256,128]{2,1,0:T(8,128)S(1)} %get-tuple-element.53.left_ref.refs_1_), channel_id=1, source_target_pairs={{1,0},{2,1},{3,2},{4,3},{5,4},{6,5},{7,6},{9,8},{10,9},{11,10},{12... | collective-permute-start | bytes 786440 | tf_op jit(solution)/shard_map/ppermute | solution.py:33
  4.5 1.0 %slice.14 = f32[2,128,256]{2,1,0:T(8,128)S(1)} slice(f32[2,256,256]{2,1,0:T(8,128)} %param.8), slice={[0:2], [0:128], [0:256]} | slice | bytes 524288 | tf_op jit(solution)/shard_map/slice | solution.py:283
  5.5 2.3 %collective-permute-start = (f32[2,128,256]{2,1,0:T(8,128)S(1)}, f32[2,128,256]{2,1,0:T(8,128)S(1)}, u32[]{:S(2)}, u32[]{:S(2)}) collective-permute-start(f32[2,128,256]{2,1,0:T(8,128)S(1)} %slice.14), channel_id=1, source_target_pairs={{8,0},{9,1},{10,2},{11,3},{12,4},{13,5},{14,6},{15,7},{16,8},{17,9... | collective-permute-start | bytes 786440 | tf_op jit(solution)/shard_map/ppermute | solution.py:33
  7.8 0.9 %slice.15 = f32[2,128,128]{2,1,0:T(8,128)S(1)} slice(f32[2,256,256]{2,1,0:T(8,128)} %param.8), slice={[0:2], [0:128], [0:128]} | slice | bytes 262144 | tf_op jit(solution)/shard_map/slice | solution.py:284
  8.8 1.9 %collective-permute-start.2 = (f32[2,128,128]{2,1,0:T(8,128)S(1)}, f32[2,128,128]{2,1,0:T(8,128)S(1)}, u32[]{:S(2)}, u32[]{:S(2)}) collective-permute-start(f32[2,128,128]{2,1,0:T(8,128)S(1)} %slice.15), channel_id=1, source_target_pairs={{9,0},{10,1},{11,2},{12,3},{13,4},{14,5},{15,6},{17,8},{18,9},{19,... | collective-permute-start | bytes 393224 | tf_op jit(solution)/shard_map/ppermute | solution.py:33
  11.3 1.3 %prep.1 = (f32[2,256,256]{2,1,0:T(8,128)S(1)}, f32[256,256]{1,0:T(8,128)S(1)}, bf16[4,256,256]{2,1,0:T(8,128)(2,1)S(1)}, f32[2,8,128]{2,1,0:T(8,128)S(1)}, f32[2,128,128]{2,1,0:T(8,128)S(1)}) custom-call(s32[2]{0:T(128)S(1)} %bitcast.4, f32[2,256,256]{2,1,0:T(8,128)S(1)} %copy-done.1, f32[256,256]{1,0:T(8,128)S(1)} %bitcast.3, ...), custom_call_target="tpu_custom_call" | custom-call | flops 100000000 | bytes 1000000 | tf_op jit(solution)/shard_map/prep/pallas_call | solution.py:286
  12.7 0.8 %pre.2.refs_8_ = f32[256,256]{1,0:T(8,128)S(1)} custom-call(s32[2]{0:T(128)S(1)} %bitcast.5, f32[2,256,128]{2,1,0:T(8,128)S(1)} %get-tuple-element.53.left_ref.refs_1_, f32[2,256,128]{2,1,0:T(8,128)S(1)} %get-tuple-element.52.right_ref.refs_2_, f32[2,256,128]{2,1,0:T(8,128)S(1)} %collective-permute-done.1.beside_ref.refs_4_, ...), custom_call_target="tpu_custom_call" | custom-call | flops 100000000 | bytes 1000000 | tf_op jit(solution)/shard_map/pre/pallas_call | solution.py:293
  13.5 3.4 %collective-permute-done.2.refs_5_ = f32[2,128,128]{2,1,0:T(8,128)S(1)} collective-permute-done((f32[2,128,128]{2,1,0:T(8,128)S(1)}, f32[2,128,128]{2,1,0:T(8,128)S(1)}, u32[]{:S(2)}, u32[]{:S(2)}) %collective-permute-start.2) | collective-permute-done | bytes 131104 | tf_op jit(solution)/shard_map/ppermute | solution.py:33
  17.7 2.8 %main_first.1 = (f32[2,128,256]{2,1,0:T(8,128)S(1)}, f32[2,128,128]{2,1,0:T(8,128)S(1)}, f32[2,128,128]{2,1,0:T(8,128)}, f32[2,128,128]{2,1,0:T(8,128)S(1)}, f32...) custom-call(s32[2]{0:T(128)S(1)} %bitcast.6, f32[2,256,128]{2,1,0:T(8,128)S(1)} %get-tuple-element.53.left_ref.refs_1_, ...), custom_call_target="tpu_custom_call" | custom-call | flops 1000000000 | bytes 1000000 | tf_op jit(solution)/shard_map/main_first/pallas_call | solution.py:294
  20.5 0.8 %post.2 = (f32[2,128,256]{2,1,0:T(8,128)S(1)}, f32[2,256,128]{2,1,0:T(8,128)S(1)}) custom-call(s32[2]{0:T(128)S(1)} %bitcast.7, f32[256,256]{1,0:T(8,128)S(1)} %get-tuple-element.33.xb_ref, f32[2,128,128]{2,1,0:T(8,128)S(1)} %get-tuple-element.34.r00_ref, f32[2,256,256]{2,1,0:T(8,128)S(1)} %get-tuple-element.27.probe_ref.refs_6_.refs_9_, ...), custom_call_target="tpu_custom_call" | custom-call | flops 100000000 | bytes 1000000 | tf_op jit(solution)/shard_map/post/pallas_call | solution.py:299
  21.4 5.4 %collective-permute-start.4 = (f32[2,256,128]{2,1,0:T(8,128)S(1)}, f32[2,256,128]{2,1,0:T(8,128)S(1)}, u32[]{:S(2)}, u32[]{:S(2)}) collective-permute-start(f32[2,256,128]{2,1,0:T(8,128)S(1)} %get-tuple-element.37), channel_id=1, source_target_pairs={{0,1},{1,2},{2,3},{3,4},{4,5},{5,6},{6,7},{8,9},{9,10},{10,11},{11... | collective-permute-start | bytes 786440 | tf_op jit(solution)/shard_map/ppermute | solution.py:33
  26.8 2.2 %collective-permute-start.3 = (f32[2,128,128]{2,1,0:T(8,128)S(1)}, f32[2,128,128]{2,1,0:T(8,128)S(1)}, u32[]{:S(2)}, u32[]{:S(2)}) collective-permute-start(f32[2,128,128]{2,1,0:T(8,128)S(1)} %get-tuple-element.36), channel_id=1, source_target_pairs={{0,8},{1,9},{2,10},{3,11},{4,12},{5,13},{6,14},{7,15},{8,16},{9,17... | collective-permute-start | bytes 393224 | tf_op jit(solution)/shard_map/ppermute | solution.py:33
  29.0 1.9 %collective-permute-start.5 = (f32[2,128,128]{2,1,0:T(8,128)S(1)}, f32[2,128,128]{2,1,0:T(8,128)S(1)}, u32[]{:S(2)}, u32[]{:S(2)}) collective-permute-start(f32[2,128,128]{2,1,0:T(8,128)S(1)} %get-tuple-element.38), channel_id=1, source_target_pairs={{0,9},{1,10},{2,11},{3,12},{4,13},{5,14},{6,15},{8,17},{9,18},{10,... | collective-permute-start | bytes 393224 | tf_op jit(solution)/shard_map/ppermute | solution.py:33
  30.9 2.2 %collective-permute-done.3.d00_ref = f32[2,128,128]{2,1,0:T(8,128)S(1)} collective-permute-done((f32[2,128,128]{2,1,0:T(8,128)S(1)}, f32[2,128,128]{2,1,0:T(8,128)S(1)}, u32[]{:S(2)}, u32[]{:S(2)}) %collective-permute-start.3) | collective-permute-done | bytes 131104 | tf_op jit(solution)/shard_map/ppermute | solution.py:33
  33.2 2.8 %collective-permute-done.5.diag_ref = f32[2,128,128]{2,1,0:T(8,128)S(1)} collective-permute-done((f32[2,128,128]{2,1,0:T(8,128)S(1)}, f32[2,128,128]{2,1,0:T(8,128)S(1)}, u32[]{:S(2)}, u32[]{:S(2)}) %collective-permute-start.5) | collective-permute-done | bytes 131104 | tf_op jit(solution)/shard_map/ppermute | solution.py:33
  36.8 1.9 %collective-permute-start.9 = (f32[2,256,128]{2,1,0:T(8,128)S(1)}, f32[2,256,128]{2,1,0:T(8,128)S(1)}, u32[]{:S(2)}, u32[]{:S(2)}) collective-permute-start(f32[2,256,128]{2,1,0:T(8,128)S(1)} %get-tuple-element.39.left_ref.refs_2_), channel_id=1, source_target_pairs={{1,0},{2,1},{3,2},{4,3},{5,4},{6,5},{7,6},{9,8},{10,9},{11,10},{12... | collective-permute-start | bytes 786440 | tf_op jit(solution)/shard_map/ppermute | solution.py:33
  38.7 3.1 %collective-permute-start.6 = (f32[2,128,128]{2,1,0:T(8,128)}, f32[2,128,128]{2,1,0:T(8,128)S(1)}, u32[]{:S(2)}, u32[]{:S(2)}) collective-permute-start(f32[2,128,128]{2,1,0:T(8,128)} %get-tuple-element.40.refs_6_), channel_id=1, source_target_pairs={{0,8},{1,9},{2,10},{3,11},{4,12},{5,13},{6,14},{7,15},{8,16},{9,17... | collective-permute-start | bytes 393224 | tf_op jit(solution)/shard_map/ppermute | solution.py:33
  41.8 2.2 %collective-permute-start.8 = (f32[2,128,128]{2,1,0:T(8,128)S(1)}, f32[2,128,128]{2,1,0:T(8,128)}, u32[]{:S(2)}, u32[]{:S(2)}) collective-permute-start(f32[2,128,128]{2,1,0:T(8,128)S(1)} %ahead.1), channel_id=1, source_target_pairs={{8,0},{9,1},{10,2},{11,3},{12,4},{13,5},{14,6},{15,7},{16,8},{17,9... | collective-permute-start | bytes 393224 | tf_op jit(solution)/shard_map/ppermute | solution.py:33
  44.0 1.9 %collective-permute-start.10 = (f32[2,128,128]{2,1,0:T(8,128)}, f32[2,128,128]{2,1,0:T(8,128)}, u32[]{:S(2)}, u32[]{:S(2)}) collective-permute-start(f32[2,128,128]{2,1,0:T(8,128)} %get-tuple-element.44), channel_id=1, source_target_pairs={{9,0},{10,1},{11,2},{12,3},{13,4},{14,5},{15,6},{17,8},{18,9},{19,... | collective-permute-start | bytes 393224 | tf_op jit(solution)/shard_map/ppermute | solution.py:33
  45.9 1.9 %collective-permute-start.7 = (f32[2,128,128]{2,1,0:T(8,128)}, f32[2,128,128]{2,1,0:T(8,128)}, u32[]{:S(2)}, u32[]{:S(2)}) collective-permute-start(f32[2,128,128]{2,1,0:T(8,128)} %get-tuple-element.44), channel_id=1, source_target_pairs={{8,0},{9,1},{10,2},{11,3},{12,4},{13,5},{14,6},{15,7},{16,8},{17,9... | collective-permute-start | bytes 393224 | tf_op jit(solution)/shard_map/ppermute | solution.py:33
  48.0 0.8 %pre.3.refs_11_ = f32[256,256]{1,0:T(8,128)S(1)} custom-call(s32[2]{0:T(128)S(1)} %bitcast.8, f32[2,256,128]{2,1,0:T(8,128)S(1)} %get-tuple-element.39.left_ref.refs_2_, f32[2,256,128]{2,1,0:T(8,128)S(1)} %get-tuple-element.41.right_ref.refs_3_, f32[2,256,128]{2,1,0:T(8,128)S(1)} %collective-permute-done.9.beside_ref.refs_7_, ...), custom_call_target="tpu_custom_call" | custom-call | flops 100000000 | bytes 1000000 | tf_op jit(solution)/shard_map/pre/pallas_call | solution.py:315
  48.8 1.1 %collective-permute-done.8.refs_5_ = f32[2,128,128]{2,1,0:T(8,128)} collective-permute-done((f32[2,128,128]{2,1,0:T(8,128)S(1)}, f32[2,128,128]{2,1,0:T(8,128)}, u32[]{:S(2)}, u32[]{:S(2)}) %collective-permute-start.8) | collective-permute-done | bytes 131104 | tf_op jit(solution)/shard_map/ppermute | solution.py:33
  49.9 3.1 %collective-permute-done.10.refs_8_ = f32[2,128,128]{2,1,0:T(8,128)} collective-permute-done((f32[2,128,128]{2,1,0:T(8,128)}, f32[2,128,128]{2,1,0:T(8,128)}, u32[]{:S(2)}, u32[]{:S(2)}) %collective-permute-start.10) | collective-permute-done | bytes 131104 | tf_op jit(solution)/shard_map/ppermute | solution.py:33
  53.1 2.9 %collective-permute-done.7.refs_4_ = f32[2,128,128]{2,1,0:T(8,128)} collective-permute-done((f32[2,128,128]{2,1,0:T(8,128)}, f32[2,128,128]{2,1,0:T(8,128)}, u32[]{:S(2)}, u32[]{:S(2)}) %collective-permute-start.7) | collective-permute-done | bytes 131104 | tf_op jit(solution)/shard_map/ppermute | solution.py:33
  56.0 2.7 %main_last.1 = (f32[2,128,256]{2,1,0:T(8,128)S(1)}, f32[2,128,256]{2,1,0:T(8,128)S(1)}, f32[2,128,128]{2,1,0:T(8,128)S(1)}, f32[2,128,128]{2,1,0:T(8,128)S(1)}, f32[256,256]{1,0:T(8,128)S(1)}) custom-call(s32[2]{0:T(128)S(1)} %bitcast.9, s32[1]{0:T(128)} %bitcast.2.refs_1_, f32[2,256,128]{2,1,0:T(8,128)S(1)} %get-tuple-element.39.left_ref.refs_2_, ...), custom_call_target="tpu_custom_call" | custom-call | flops 1000000000 | bytes 1000000 | tf_op jit(solution)/shard_map/main_last/pallas_call | solution.py:316
  58.8 0.8 %post.3 = (f32[2,128,256]{2,1,0:T(8,128)S(1)}, f32[2,256,128]{2,1,0:T(8,128)S(1)}) custom-call(s32[2]{0:T(128)S(1)} %bitcast.10, f32[256,256]{1,0:T(8,128)S(1)} %get-tuple-element.46.xb_ref, f32[2,128,128]{2,1,0:T(8,128)S(1)} %get-tuple-element.47.r00_ref, f32[2,256,256]{2,1,0:T(8,128)S(1)} %get-tuple-element.27.probe_ref.refs_6_.refs_9_, ...), custom_call_target="tpu_custom_call" | custom-call | flops 100000000 | bytes 1000000 | tf_op jit(solution)/shard_map/post/pallas_call | solution.py:321
  59.6 3.6 %collective-permute-start.12 = (f32[2,256,128]{2,1,0:T(8,128)S(1)}, f32[2,256,128]{2,1,0:T(8,128)S(1)}, u32[]{:S(2)}, u32[]{:S(2)}) collective-permute-start(f32[2,256,128]{2,1,0:T(8,128)S(1)} %get-tuple-element.50), channel_id=1, source_target_pairs={{0,1},{1,2},{2,3},{3,4},{4,5},{5,6},{6,7},{8,9},{9,10},{10,11},{11... | collective-permute-start | bytes 786440 | tf_op jit(solution)/shard_map/ppermute | solution.py:33
  63.2 3.1 %collective-permute-start.11 = (f32[2,128,256]{2,1,0:T(8,128)S(1)}, f32[2,128,256]{2,1,0:T(8,128)S(1)}, u32[]{:S(2)}, u32[]{:S(2)}) collective-permute-start(f32[2,128,256]{2,1,0:T(8,128)S(1)} %get-tuple-element.49), channel_id=1, source_target_pairs={{0,8},{1,9},{2,10},{3,11},{4,12},{5,13},{6,14},{7,15},{8,16},{9,17... | collective-permute-start | bytes 786440 | tf_op jit(solution)/shard_map/ppermute | solution.py:33
  66.3 1.9 %collective-permute-start.13 = (f32[2,128,128]{2,1,0:T(8,128)S(1)}, f32[2,128,128]{2,1,0:T(8,128)S(1)}, u32[]{:S(2)}, u32[]{:S(2)}) collective-permute-start(f32[2,128,128]{2,1,0:T(8,128)S(1)} %get-tuple-element.51), channel_id=1, source_target_pairs={{0,9},{1,10},{2,11},{3,12},{4,13},{5,14},{6,15},{8,17},{9,18},{10,... | collective-permute-start | bytes 393224 | tf_op jit(solution)/shard_map/ppermute | solution.py:33
  68.3 7.0 %collective-permute-done.13.diag_ref = f32[2,128,128]{2,1,0:T(8,128)S(1)} collective-permute-done((f32[2,128,128]{2,1,0:T(8,128)S(1)}, f32[2,128,128]{2,1,0:T(8,128)S(1)}, u32[]{:S(2)}, u32[]{:S(2)}) %collective-permute-start.13) | collective-permute-done | bytes 131104 | tf_op jit(solution)/shard_map/ppermute | solution.py:33
  75.2 1.1 %final.1 = (f32[2,256,256]{2,1,0:T(8,128)}, f32[2,256,256]{2,1,0:T(8,128)}) custom-call(f32[2,256,128]{2,1,0:T(8,128)S(1)} %get-tuple-element.39.left_ref.refs_2_, f32[2,256,128]{2,1,0:T(8,128)S(1)} %get-tuple-element.41.right_ref.refs_3_, f32[2,256,128]{2,1,0:T(8,128)S(1)} %get-tuple-element.42.vl_ref, f32[2,256,128]{2,1,0:T(8,128)S(1)} %get-tuple-element.43.vr_ref, ...), custom_call_target="tpu_custom_call" | custom-call | flops 1000000 | bytes 1000000 | tf_op jit(solution)/shard_map/final/pallas_call | solution.py:323
  (28 shorter events, 2.3 us)
Async XLA Ops:
  0.6 10.1 %copy-start.2 = (bf16[4,256,256]{2,1,0:T(8,128)(2,1)S(1)}, bf16[4,256,256]{2,1,0:T(8,128)(2,1)}, u32[]{:S(2)}) copy-start(bf16[4,256,256]{2,1,0:T(8,128)(2,1)} %constant.13.clone.table_ref) | copy-start | bytes 1572868
  0.6 10.1 %copy-start.4 = (f32[2,128,128]{2,1,0:T(8,128)S(1)}, f32[2,128,128]{2,1,0:T(8,128)}, u32[]{:S(2)}) copy-start(f32[2,128,128]{2,1,0:T(8,128)} %constant.15.clone.rows_ref) | copy-start | bytes 393220
  0.7 10.1 %copy-start.6 = (f32[2,8,128]{2,1,0:T(8,128)S(1)}, f32[2,8,128]{2,1,0:T(8,128)}, u32[]{:S(2)}) copy-start(f32[2,8,128]{2,1,0:T(8,128)} %constant.14.clone.cols_ref) | copy-start | bytes 24580
  1.8 8.9 %copy-start.1 = (f32[2,256,256]{2,1,0:T(8,128)S(1)}, f32[2,256,256]{2,1,0:T(8,128)}, u32[]{:S(2)}) copy-start(f32[2,256,256]{2,1,0:T(8,128)} %probe_ref.1) | copy-start | bytes 1572868
  1.8 10.9 %collective-permute-start.1 = (f32[2,256,128]{2,1,0:T(8,128)S(1)}, f32[2,256,128]{2,1,0:T(8,128)S(1)}, u32[]{:S(2)}, u32[]{:S(2)}) collective-permute-start(f32[2,256,128]{2,1,0:T(8,128)S(1)} %get-tuple-element.53.left_ref.refs_1_), channel_id=1, source_target_pairs={{1,0},{2,1},{3,2},{4,3},{5,4},{6,5},{7,6},{9,8},{10,9},{11,10},{12... | collective-permute-start | bytes 786440 | tf_op jit(solution)/shard_map/ppermute | solution.py:33
  5.5 5.2 %copy-start.3 = (f32[1,1,1,256,256]{4,3,2,1,0:T(8,128)S(1)}, f32[1,1,1,256,256]{4,3,2,1,0:T(8,128)}, u32[]{:S(2)}) copy-start(f32[1,1,1,256,256]{4,3,2,1,0:T(8,128)} %param.11) | copy-start | bytes 786436
  5.5 12.2 %collective-permute-start = (f32[2,128,256]{2,1,0:T(8,128)S(1)}, f32[2,128,256]{2,1,0:T(8,128)S(1)}, u32[]{:S(2)}, u32[]{:S(2)}) collective-permute-start(f32[2,128,256]{2,1,0:T(8,128)S(1)} %slice.14), channel_id=1, source_target_pairs={{8,0},{9,1},{10,2},{11,3},{12,4},{13,5},{14,6},{15,7},{16,8},{17,9... | collective-permute-start | bytes 786440 | tf_op jit(solution)/shard_map/ppermute | solution.py:33
  8.8 8.2 %collective-permute-start.2 = (f32[2,128,128]{2,1,0:T(8,128)S(1)}, f32[2,128,128]{2,1,0:T(8,128)S(1)}, u32[]{:S(2)}, u32[]{:S(2)}) collective-permute-start(f32[2,128,128]{2,1,0:T(8,128)S(1)} %slice.15), channel_id=1, source_target_pairs={{9,0},{10,1},{11,2},{12,3},{13,4},{14,5},{15,6},{17,8},{18,9},{19,... | collective-permute-start | bytes 393224 | tf_op jit(solution)/shard_map/ppermute | solution.py:33
  10.7 0.7 copy-start.5
  12.7 5.0 %copy-start.7 = (f32[256,256]{1,0:T(8,128)}, f32[256,256]{1,0:T(8,128)S(1)}, u32[]{:S(2)}) copy-start(f32[256,256]{1,0:T(8,128)S(1)} %get-tuple-element.28.refs_7_.refs_10_) | copy-start | bytes 786436
  20.5 15.5 %copy-start = (f32[2,256,256]{2,1,0:T(8,128)S(1)}, f32[2,256,256]{2,1,0:T(8,128)}, u32[]{:S(2)}) copy-start(f32[2,256,256]{2,1,0:T(8,128)} %vel_ref.5) | copy-start | bytes 1572868
  21.4 14.6 %collective-permute-start.4 = (f32[2,256,128]{2,1,0:T(8,128)S(1)}, f32[2,256,128]{2,1,0:T(8,128)S(1)}, u32[]{:S(2)}, u32[]{:S(2)}) collective-permute-start(f32[2,256,128]{2,1,0:T(8,128)S(1)} %get-tuple-element.37), channel_id=1, source_target_pairs={{0,1},{1,2},{2,3},{3,4},{4,5},{5,6},{6,7},{8,9},{9,10},{10,11},{11... | collective-permute-start | bytes 786440 | tf_op jit(solution)/shard_map/ppermute | solution.py:33
  26.8 6.4 %collective-permute-start.3 = (f32[2,128,128]{2,1,0:T(8,128)S(1)}, f32[2,128,128]{2,1,0:T(8,128)S(1)}, u32[]{:S(2)}, u32[]{:S(2)}) collective-permute-start(f32[2,128,128]{2,1,0:T(8,128)S(1)} %get-tuple-element.36), channel_id=1, source_target_pairs={{0,8},{1,9},{2,10},{3,11},{4,12},{5,13},{6,14},{7,15},{8,16},{9,17... | collective-permute-start | bytes 393224 | tf_op jit(solution)/shard_map/ppermute | solution.py:33
  29.0 7.0 %collective-permute-start.5 = (f32[2,128,128]{2,1,0:T(8,128)S(1)}, f32[2,128,128]{2,1,0:T(8,128)S(1)}, u32[]{:S(2)}, u32[]{:S(2)}) collective-permute-start(f32[2,128,128]{2,1,0:T(8,128)S(1)} %get-tuple-element.38), channel_id=1, source_target_pairs={{0,9},{1,10},{2,11},{3,12},{4,13},{5,14},{6,15},{8,17},{9,18},{10,... | collective-permute-start | bytes 393224 | tf_op jit(solution)/shard_map/ppermute | solution.py:33
  36.8 11.2 %collective-permute-start.9 = (f32[2,256,128]{2,1,0:T(8,128)S(1)}, f32[2,256,128]{2,1,0:T(8,128)S(1)}, u32[]{:S(2)}, u32[]{:S(2)}) collective-permute-start(f32[2,256,128]{2,1,0:T(8,128)S(1)} %get-tuple-element.39.left_ref.refs_2_), channel_id=1, source_target_pairs={{1,0},{2,1},{3,2},{4,3},{5,4},{6,5},{7,6},{9,8},{10,9},{11,10},{12... | collective-permute-start | bytes 786440 | tf_op jit(solution)/shard_map/ppermute | solution.py:33
  38.7 9.2 %collective-permute-start.6 = (f32[2,128,128]{2,1,0:T(8,128)}, f32[2,128,128]{2,1,0:T(8,128)S(1)}, u32[]{:S(2)}, u32[]{:S(2)}) collective-permute-start(f32[2,128,128]{2,1,0:T(8,128)} %get-tuple-element.40.refs_6_), channel_id=1, source_target_pairs={{0,8},{1,9},{2,10},{3,11},{4,12},{5,13},{6,14},{7,15},{8,16},{9,17... | collective-permute-start | bytes 393224 | tf_op jit(solution)/shard_map/ppermute | solution.py:33
  41.8 8.1 %collective-permute-start.8 = (f32[2,128,128]{2,1,0:T(8,128)S(1)}, f32[2,128,128]{2,1,0:T(8,128)}, u32[]{:S(2)}, u32[]{:S(2)}) collective-permute-start(f32[2,128,128]{2,1,0:T(8,128)S(1)} %ahead.1), channel_id=1, source_target_pairs={{8,0},{9,1},{10,2},{11,3},{12,4},{13,5},{14,6},{15,7},{16,8},{17,9... | collective-permute-start | bytes 393224 | tf_op jit(solution)/shard_map/ppermute | solution.py:33
  44.0 9.1 %collective-permute-start.10 = (f32[2,128,128]{2,1,0:T(8,128)}, f32[2,128,128]{2,1,0:T(8,128)}, u32[]{:S(2)}, u32[]{:S(2)}) collective-permute-start(f32[2,128,128]{2,1,0:T(8,128)} %get-tuple-element.44), channel_id=1, source_target_pairs={{9,0},{10,1},{11,2},{12,3},{13,4},{14,5},{15,6},{17,8},{18,9},{19,... | collective-permute-start | bytes 393224 | tf_op jit(solution)/shard_map/ppermute | solution.py:33
  45.9 10.1 %collective-permute-start.7 = (f32[2,128,128]{2,1,0:T(8,128)}, f32[2,128,128]{2,1,0:T(8,128)}, u32[]{:S(2)}, u32[]{:S(2)}) collective-permute-start(f32[2,128,128]{2,1,0:T(8,128)} %get-tuple-element.44), channel_id=1, source_target_pairs={{8,0},{9,1},{10,2},{11,3},{12,4},{13,5},{14,6},{15,7},{16,8},{17,9... | collective-permute-start | bytes 393224 | tf_op jit(solution)/shard_map/ppermute | solution.py:33
  48.0 8.1 %copy-start.8 = (f32[256,256]{1,0:T(8,128)S(1)}, f32[256,256]{1,0:T(8,128)}, u32[]{:S(2)}) copy-start(f32[256,256]{1,0:T(8,128)} %copy-done.7) | copy-start | bytes 786436
  59.6 15.6 %collective-permute-start.12 = (f32[2,256,128]{2,1,0:T(8,128)S(1)}, f32[2,256,128]{2,1,0:T(8,128)S(1)}, u32[]{:S(2)}, u32[]{:S(2)}) collective-permute-start(f32[2,256,128]{2,1,0:T(8,128)S(1)} %get-tuple-element.50), channel_id=1, source_target_pairs={{0,1},{1,2},{2,3},{3,4},{4,5},{5,6},{6,7},{8,9},{9,10},{10,11},{11... | collective-permute-start | bytes 786440 | tf_op jit(solution)/shard_map/ppermute | solution.py:33
  63.2 12.0 %collective-permute-start.11 = (f32[2,128,256]{2,1,0:T(8,128)S(1)}, f32[2,128,256]{2,1,0:T(8,128)S(1)}, u32[]{:S(2)}, u32[]{:S(2)}) collective-permute-start(f32[2,128,256]{2,1,0:T(8,128)S(1)} %get-tuple-element.49), channel_id=1, source_target_pairs={{0,8},{1,9},{2,10},{3,11},{4,12},{5,13},{6,14},{7,15},{8,16},{9,17... | collective-permute-start | bytes 786440 | tf_op jit(solution)/shard_map/ppermute | solution.py:33
  66.3 8.9 %collective-permute-start.13 = (f32[2,128,128]{2,1,0:T(8,128)S(1)}, f32[2,128,128]{2,1,0:T(8,128)S(1)}, u32[]{:S(2)}, u32[]{:S(2)}) collective-permute-start(f32[2,128,128]{2,1,0:T(8,128)S(1)} %get-tuple-element.51), channel_id=1, source_target_pairs={{0,9},{1,10},{2,11},{3,12},{4,13},{5,14},{6,15},{8,17},{9,18},{10,... | collective-permute-start | bytes 393224 | tf_op jit(solution)/shard_map/ppermute | solution.py:33
where the time goes:
time: 77.6 us; the launch traced here: 76.4 us
  starting transfers between devices  36.1 us (47%)
  waiting for transfers between devices  23.5 us (30%)
  Pallas kernels  12.2 us (16%)
  local copies, waits for them, and re-layouts  3.67 us (5%)
  between operations  0.95 us (1%)
    ppermute x14, starting transfers between devices, shifted(): return lax.ppermute(value, ('row', 'col'), pairs)  36.1 us
    ppermute x14, waiting for transfers between devices, shifted(): return lax.ppermute(value, ('row', 'col'), pairs)  23.5 us
    pallas_call x1, Pallas kernels, on_device(): kernel(lambda *refs: main_kernel(True, *refs), 'main_first', 10 ** 9, 1,...  2.83 us
    pallas_call x1, Pallas kernels, on_device(): kernel(lambda *refs: main_kernel(False, *refs), 'main_last', 10 ** 9, 2,...  2.73 us
    pallas_call x2, Pallas kernels, on_device(): bottom, right_part = post(offsets, xb, r00, turned, tables, along_cols)  1.69 us
    pallas_call x2, Pallas kernels, on_device(): yb, = pre(offsets, left, right, beside, turned, tables, along_cols)  1.65 us
  transfers between devices with their start and end apart: 14, of which 8 were waited for; matrix products, arithmetic and copies ran while one was open for 2% of the time, Pallas kernels for 4%

commit v1 on v0

--- a/solution.py
+++ b/solution.py
@@ -10,8 +10,6 @@
 
 
 P_SIZE = 256
-W = 128
-ITERS = 2
 
 step_size = 0.1
 momentum_rate = 0.8
@@ -81,7 +79,27 @@
     return table_ref[2], table_ref[3]
 
 
-def prep_kernel(pos_ref, probe_ref, meas_ref, table_ref, cols_ref, rows_ref, probe_out, meas_out, table_out, cols_out, rows_out):
+def unpack_kernel(obj_ref, left_out, right_out, q00_out):
+    for part in range(2):
+        left_out[part] = obj_ref[part, :, :H]
+        right_out[part] = obj_ref[part, :, H:]
+        q00_out[part] = obj_ref[part, :H, :H]
+
+
+def prep_kernel(
+    pos_ref, probe_hbm, meas_hbm, table_hbm, cols_hbm, rows_hbm,
+    probe_out, meas_out, table_out, cols_out, rows_out, probe_ref, meas_ref, sems,
+):
+    copies = [
+        pltpu.make_async_copy(source, target, sems.at[number])
+        for number, (source, target) in enumerate(
+            ((probe_hbm, probe_ref), (meas_hbm, meas_ref), (table_hbm, table_out), (cols_hbm, cols_out), (rows_hbm, rows_out))
+        )
+    ]
+    for copy in copies:
+        copy.start()
+    for copy in copies:
+        copy.wait()
     p0 = pos_ref[0]
     p1 = pos_ref[1]
     for part in range(2):
@@ -103,9 +121,6 @@
     cols_move = jnp.where(first == evens_first(second), 1.0, 0.0).astype(jnp.bfloat16)
     x = moved(meas_ref[...], lambda part: dot(rows_move, part))
     meas_out[...] = moved(x, lambda part: dot(part, cols_move))
-    table_out[...] = table_ref[...]
-    cols_out[...] = cols_ref[...]
-    rows_out[...] = rows_ref[...]
 
 
 def row_stage(patch, pr, pi, table, w_ref):
@@ -260,67 +275,71 @@
     return jax.ShapeDtypeStruct(dims, dtype)
 
 
-def kernel(body, name, flops, scalars, arrays, outs):
+def kernel(body, flops, scalars, arrays, outs, space=VMEM, scratch=()):
     return pl.pallas_call(
         body,
         out_shape=outs,
-        in_specs=[SMEM] * scalars + [VMEM] * arrays,
+        in_specs=[SMEM] * scalars + [space] * arrays,
         out_specs=(VMEM,) * len(outs),
+        scratch_shapes=scratch,
         compiler_params=pltpu.CompilerParams(vmem_limit_bytes=16 * 1024 * 1024),
         cost_estimate=pl.CostEstimate(flops=flops, bytes_accessed=10**6, transcendentals=0),
-        name=name,
-    )
-
-
-def on_device(object_field, velocity, positions, measured, probe):
+    )
+
+
+def steps(object_field, velocity, positions, measured, probe):
     tables, along_cols, along_rows = (jnp.asarray(x) for x in constants())
     offsets = positions[0, 0, 0]
     intensity = measured[0, 0, 0]
     has_below = (lax.axis_index("row") < lax.axis_size("row") - 1).astype(jnp.int32).reshape(1)
     half, strip, quad, rows = shape(2, N, H), shape(2, H, N), shape(2, H, H), shape(N, N)
 
-    left, right = object_field[:, :, :H], object_field[:, :, H:]
     lower = shifted(object_field[:, :H, :], -1, 0)
-    corner = shifted(object_field[:, :H, :H], -1, -1)
+    left, right, q00 = kernel(unpack_kernel, 10**6, 0, 1, (half, half, quad))(object_field)
+    corner = shifted(q00, -1, -1)
     beside = shifted(left, 0, -1)
     turned, intensity, tables, along_cols, along_rows = kernel(
-        prep_kernel, "prep", 10**8, 1, 5,
+        prep_kernel, 10**8, 1, 5,
         (shape(2, N, N), rows, shape(4, N, N, dtype=jnp.bfloat16), shape(2, 8, H), shape(2, H, H)),
+        pl.BlockSpec(memory_space=pl.ANY),
+        (pltpu.VMEM((2, N, N), jnp.float32), pltpu.VMEM((N, N), jnp.float32), pltpu.SemaphoreType.DMA((5,))),
     )(offsets, probe, intensity, tables, along_cols, along_rows)
-    pre = kernel(pre_kernel, "pre", 10**8, 1, 6, (rows,))
-    post = kernel(post_kernel, "post", 10**8, 1, 5, (strip, half))
-
-    (yb,) = pre(offsets, left, right, beside, turned, tables, along_cols)
+
+    def pre(left, right, beside):
+        return kernel(pre_kernel, 10**8, 1, 6, (rows,))(offsets, left, right, beside, turned, tables, along_cols)[0]
+
+    def post(xb, r00):
+        return kernel(post_kernel, 10**8, 1, 5, (strip, half))(offsets, xb, r00, turned, tables, along_cols)
+
+    yb = pre(left, right, beside)
     top, d00, d01, diag, r00, xb = kernel(
-        lambda *refs: main_kernel(True, *refs), "main_first", 10**9, 1, 11, (strip, quad, quad, quad, quad, rows)
+        lambda *refs: main_kernel(True, *refs), 10**9, 1, 11, (strip, quad, quad, quad, quad, rows)
     )(offsets, left, right, lower, beside, corner, turned, intensity, yb, tables, along_cols, along_rows)
     from_above = shifted(d00, 1, 0)
     from_corner = shifted(diag, 1, 1)
-    bottom, right_part = post(offsets, xb, r00, turned, tables, along_cols)
+    bottom, right_part = post(xb, r00)
     before = shifted(right_part, 0, 1)
     above01 = shifted(d01, 1, 0)
-    (ahead,) = kernel(ahead_kernel, "ahead", 10**6, 0, 3, (quad,))(right, velocity, top)
+    (ahead,) = kernel(ahead_kernel, 10**6, 0, 3, (quad,))(right, velocity, top)
     up01 = shifted(ahead, -1, 0)
 
-    left, q00, vel_left = kernel(left_update_kernel, "left_update", 10**6, 0, 7, (half, quad, half))(
+    left, q00, vel_left = kernel(left_update_kernel, 10**6, 0, 7, (half, quad, half))(
         left, velocity, top, bottom, from_above, before, from_corner
     )
     up00 = shifted(q00, -1, 0)
     corner = shifted(q00, -1, -1)
     beside = shifted(left, 0, -1)
-    right, vel_right = kernel(right_update_kernel, "right_update", 10**6, 0, 5, (half, half))(
-        right, velocity, top, bottom, above01
-    )
-
-    (yb,) = pre(offsets, left, right, beside, turned, tables, along_cols)
+    right, vel_right = kernel(right_update_kernel, 10**6, 0, 5, (half, half))(right, velocity, top, bottom, above01)
+
+    yb = pre(left, right, beside)
     top, down, diag, r00, xb = kernel(
-        lambda *refs: main_kernel(False, *refs), "main_last", 10**9, 2, 13, (strip, strip, quad, quad, rows)
+        lambda *refs: main_kernel(False, *refs), 10**9, 2, 13, (strip, strip, quad, quad, rows)
     )(offsets, has_below, left, right, up00, up01, d01, beside, corner, turned, intensity, yb, tables, along_cols, along_rows)
     above = shifted(down, 1, 0)
     from_corner = shifted(diag, 1, 1)
-    bottom, right_part = post(offsets, xb, r00, turned, tables, along_cols)
+    bottom, right_part = post(xb, r00)
     before = shifted(right_part, 0, 1)
-    return kernel(final_kernel, "final", 10**6, 0, 9, (shape(2, N, N), shape(2, N, N)))(
+    return kernel(final_kernel, 10**6, 0, 9, (shape(2, N, N), shape(2, N, N)))(
         left, right, vel_left, vel_right, top, bottom, above, before, from_corner
     )
 
@@ -334,7 +353,7 @@
         P(),
     )
     return jax.shard_map(
-        on_device,
+        steps,
         mesh=mesh,
         in_specs=placed,
         out_specs=(P(None, "row", "col"), P(None, "row", "col")),

time: 77.6 us -> 76.7 us (0.988)
  waiting for transfers between devices: 23.5 us -> 21.5 us
    unnamed x18 -> x20, local copies, waits for them, and re-layouts: 0.65 us -> 4.24 us
    slice x3 -> x1, local copies, waits for them, and re-layouts: 3.02 us -> 0.02 us  [steps(): lower = shifted(object_field[:, :H, :], -1, 0)]
    ppermute x14, waiting for transfers between devices: 23.5 us -> 21.5 us  [shifted(): return lax.ppermute(value, ('row', 'col'), pairs)]
    pallas_call x11 -> x12, Pallas kernels: 12.2 us -> 12.6 us  [the longest x1 2.84 us: steps(): kernel(lambda *refs: main_kernel(True, *refs), 10 ** 9, 1, 11, (strip, qu...]
  transfers between devices with their start and end apart: 14 -> 14, of which waited for: 8 -> 8; matrix products, arithmetic and copies ran while one was open for 2% -> 0% of each run, Pallas kernels for 4% -> 5%
where the time goes in v1:
time: 76.7 us; the launch traced here: 75.2 us
  starting transfers between devices  36 us (47%)
  waiting for transfers between devices  21.5 us (28%)
  Pallas kernels  12.6 us (16%)
  local copies, waits for them, and re-layouts  4.26 us (6%)
  between operations  0.9 us (1%)
    ppermute x14, starting transfers between devices, shifted(): return lax.ppermute(value, ('row', 'col'), pairs)  36 us
    ppermute x14, waiting for transfers between devices, shifted(): return lax.ppermute(value, ('row', 'col'), pairs)  21.5 us
    unnamed x20, local copies, waits for them, and re-layouts  4.24 us
    pallas_call x1, Pallas kernels, steps(): kernel(lambda *refs: main_kernel(True, *refs), 10 ** 9, 1, 11, (strip, qu...  2.84 us
    pallas_call x1, Pallas kernels, steps(): kernel(lambda *refs: main_kernel(False, *refs), 10 ** 9, 2, 13, (strip, s...  2.73 us
    pallas_call x2, Pallas kernels, post(): kernel(post_kernel, 10 ** 8, 1, 5, (strip, half))  1.69 us
    pallas_call x1, Pallas kernels, steps(): kernel(prep_kernel, 10 ** 8, 1, 5, (shape(2, N, N), rows, shape(4, N, N,...  1.65 us
    pallas_call x2, Pallas kernels, pre(): kernel(pre_kernel, 10 ** 8, 1, 6, (rows,))  1.65 us
  transfers between devices with their start and end apart: 14, of which 8 were waited for; matrix products, arithmetic and copies ran while one was open for 0% of the time, Pallas kernels for 5%

profile of v1, /device:TPU:11, one launch (start us, length us, event | category | flops | bytes accessed | tf_op | source)
XLA Modules:
  0.0 75.2 jit_solution(11735755707581979327)
XLA Ops:
  0.6 1.0 %copy-done.1 = f32[2,256,256]{2,1,0:T(8,128)S(1)} copy-done((f32[2,256,256]{2,1,0:T(8,128)S(1)}, f32[2,256,256]{2,1,0:T(8,128)}, u32[]{:S(2)}) %copy-start.1) | copy-done | bytes 524312
  1.7 2.7 %collective-permute-start.1 = (f32[2,256,128]{2,1,0:T(8,128)S(1)}, f32[2,256,128]{2,1,0:T(8,128)S(1)}, u32[]{:S(2)}, u32[]{:S(2)}) collective-permute-start(f32[2,256,128]{2,1,0:T(8,128)S(1)} %get-tuple-element.30.left_ref.refs_1_), channel_id=1, source_target_pairs={{1,0},{2,1},{3,2},{4,3},{5,4},{6,5},{7,6},{9,8},{10,9},{11,10},{12... | collective-permute-start | bytes 786440 | tf_op jit(solution)/shard_map/ppermute | solution.py:31
  4.5 2.2 %collective-permute-start = (f32[2,128,256]{2,1,0:T(8,128)S(1)}, f32[2,128,256]{2,1,0:T(8,128)S(1)}, u32[]{:S(2)}, u32[]{:S(2)}) collective-permute-start(f32[2,128,256]{2,1,0:T(8,128)S(1)} %slice.3), channel_id=1, source_target_pairs={{8,0},{9,1},{10,2},{11,3},{12,4},{13,5},{14,6},{15,7},{16,8},{17,9... | collective-permute-start | bytes 786440 | tf_op jit(solution)/shard_map/ppermute | solution.py:31
  6.6 1.9 %collective-permute-start.2 = (f32[2,128,128]{2,1,0:T(8,128)S(1)}, f32[2,128,128]{2,1,0:T(8,128)S(1)}, u32[]{:S(2)}, u32[]{:S(2)}) collective-permute-start(f32[2,128,128]{2,1,0:T(8,128)S(1)} %get-tuple-element.32), channel_id=1, source_target_pairs={{9,0},{10,1},{11,2},{12,3},{13,4},{14,5},{15,6},{17,8},{18,9},{19,... | collective-permute-start | bytes 393224 | tf_op jit(solution)/shard_map/ppermute | solution.py:31
  9.2 0.9 %copy-done.4 = f32[1,1,1,256,256]{4,3,2,1,0:T(8,128)S(1)} copy-done((f32[1,1,1,256,256]{4,3,2,1,0:T(8,128)S(1)}, f32[1,1,1,256,256]{4,3,2,1,0:T(8,128)}, u32[]{:S(2)}) %copy-start.4) | copy-done | bytes 262168
  10.2 0.9 %copy-done.5 = f32[2,128,128]{2,1,0:T(8,128)S(1)} copy-done((f32[2,128,128]{2,1,0:T(8,128)S(1)}, f32[2,128,128]{2,1,0:T(8,128)}, u32[]{:S(2)}) %copy-start.5) | copy-done | bytes 131096
  11.8 1.6 %shard_map.96 = (f32[2,256,256]{2,1,0:T(8,128)S(1)}, f32[256,256]{1,0:T(8,128)S(1)}, bf16[4,256,256]{2,1,0:T(8,128)(2,1)S(1)}, f32[2,8,128]{2,1,0:T(8,128)S(1)}, f32[2,128,128]{2,1,0:T(8,128)S(1)}) custom-call(s32[2]{0:T(128)S(1)} %bitcast.4, f32[2,256,256]{2,1,0:T(8,128)S(1)} %copy-done.2, f32[256,256]{1,0:T(8,128)S(1)} %bitcast.3, ...), custom_call_target="tpu_custom_call" | custom-call | flops 100000000 | bytes 1000000 | tf_op jit(solution)/shard_map/pallas_call | solution.py:301
  13.5 0.8 %shard_map.97.refs_8_ = f32[256,256]{1,0:T(8,128)S(1)} custom-call(s32[2]{0:T(128)S(1)} %bitcast.5, f32[2,256,128]{2,1,0:T(8,128)S(1)} %get-tuple-element.30.left_ref.refs_1_, f32[2,256,128]{2,1,0:T(8,128)S(1)} %get-tuple-element.31.right_ref.refs_2_, f32[2,256,128]{2,1,0:T(8,128)S(1)} %collective-permute-done.1.beside_ref.refs_4_, ...), custom_call_target="tpu_custom_call" | custom-call | flops 100000000 | bytes 1000000 | tf_op jit(solution)/shard_map/pallas_call | solution.py:309
  14.3 1.3 %collective-permute-done.2.refs_5_ = f32[2,128,128]{2,1,0:T(8,128)S(1)} collective-permute-done((f32[2,128,128]{2,1,0:T(8,128)S(1)}, f32[2,128,128]{2,1,0:T(8,128)S(1)}, u32[]{:S(2)}, u32[]{:S(2)}) %collective-permute-start.2) | collective-permute-done | bytes 131104 | tf_op jit(solution)/shard_map/ppermute | solution.py:31
  15.6 1.0 %collective-permute-done.refs_3_ = f32[2,128,256]{2,1,0:T(8,128)S(1)} collective-permute-done((f32[2,128,256]{2,1,0:T(8,128)S(1)}, f32[2,128,256]{2,1,0:T(8,128)S(1)}, u32[]{:S(2)}, u32[]{:S(2)}) %collective-permute-start) | collective-permute-done | bytes 262176 | tf_op jit(solution)/shard_map/ppermute | solution.py:31
  16.5 2.8 %shard_map.98 = (f32[2,128,256]{2,1,0:T(8,128)S(1)}, f32[2,128,128]{2,1,0:T(8,128)S(1)}, f32[2,128,128]{2,1,0:T(8,128)}, f32[2,128,128]{2,1,0:T(8,128)S(1)}, f32...) custom-call(s32[2]{0:T(128)S(1)} %bitcast.6, f32[2,256,128]{2,1,0:T(8,128)S(1)} %get-tuple-element.30.left_ref.refs_1_, ...), custom_call_target="tpu_custom_call" | custom-call | flops 1000000000 | bytes 1000000 | tf_op jit(solution)/shard_map/pallas_call | solution.py:315
  19.4 0.8 %shard_map.99 = (f32[2,128,256]{2,1,0:T(8,128)S(1)}, f32[2,256,128]{2,1,0:T(8,128)S(1)}) custom-call(s32[2]{0:T(128)S(1)} %bitcast.7, f32[256,256]{1,0:T(8,128)S(1)} %get-tuple-element.39.xb_ref, f32[2,128,128]{2,1,0:T(8,128)S(1)} %get-tuple-element.40.r00_ref, f32[2,256,256]{2,1,0:T(8,128)S(1)} %get-tuple-element.33.probe_ref.refs_6_.refs_9_, ...), custom_call_target="tpu_custom_call" | custom-call | flops 100000000 | bytes 1000000 | tf_op jit(solution)/shard_map/pallas_call | solution.py:312
  20.2 5.4 %collective-permute-start.4 = (f32[2,256,128]{2,1,0:T(8,128)S(1)}, f32[2,256,128]{2,1,0:T(8,128)S(1)}, u32[]{:S(2)}, u32[]{:S(2)}) collective-permute-start(f32[2,256,128]{2,1,0:T(8,128)S(1)} %get-tuple-element.43), channel_id=1, source_target_pairs={{0,1},{1,2},{2,3},{3,4},{4,5},{5,6},{6,7},{8,9},{9,10},{10,11},{11... | collective-permute-start | bytes 786440 | tf_op jit(solution)/shard_map/ppermute | solution.py:31
  25.6 2.2 %collective-permute-start.3 = (f32[2,128,128]{2,1,0:T(8,128)S(1)}, f32[2,128,128]{2,1,0:T(8,128)S(1)}, u32[]{:S(2)}, u32[]{:S(2)}) collective-permute-start(f32[2,128,128]{2,1,0:T(8,128)S(1)} %get-tuple-element.42), channel_id=1, source_target_pairs={{0,8},{1,9},{2,10},{3,11},{4,12},{5,13},{6,14},{7,15},{8,16},{9,17... | collective-permute-start | bytes 393224 | tf_op jit(solution)/shard_map/ppermute | solution.py:31
  27.8 1.9 %collective-permute-start.5 = (f32[2,128,128]{2,1,0:T(8,128)S(1)}, f32[2,128,128]{2,1,0:T(8,128)S(1)}, u32[]{:S(2)}, u32[]{:S(2)}) collective-permute-start(f32[2,128,128]{2,1,0:T(8,128)S(1)} %get-tuple-element.44), channel_id=1, source_target_pairs={{0,9},{1,10},{2,11},{3,12},{4,13},{5,14},{6,15},{8,17},{9,18},{10,... | collective-permute-start | bytes 393224 | tf_op jit(solution)/shard_map/ppermute | solution.py:31
  29.8 2.2 %collective-permute-done.3.d00_ref = f32[2,128,128]{2,1,0:T(8,128)S(1)} collective-permute-done((f32[2,128,128]{2,1,0:T(8,128)S(1)}, f32[2,128,128]{2,1,0:T(8,128)S(1)}, u32[]{:S(2)}, u32[]{:S(2)}) %collective-permute-start.3) | collective-permute-done | bytes 131104 | tf_op jit(solution)/shard_map/ppermute | solution.py:31
  32.0 2.8 %collective-permute-done.5.diag_ref = f32[2,128,128]{2,1,0:T(8,128)S(1)} collective-permute-done((f32[2,128,128]{2,1,0:T(8,128)S(1)}, f32[2,128,128]{2,1,0:T(8,128)S(1)}, u32[]{:S(2)}, u32[]{:S(2)}) %collective-permute-start.5) | collective-permute-done | bytes 131104 | tf_op jit(solution)/shard_map/ppermute | solution.py:31
  35.6 1.9 %collective-permute-start.9 = (f32[2,256,128]{2,1,0:T(8,128)S(1)}, f32[2,256,128]{2,1,0:T(8,128)S(1)}, u32[]{:S(2)}, u32[]{:S(2)}) collective-permute-start(f32[2,256,128]{2,1,0:T(8,128)S(1)} %get-tuple-element.45.left_ref.refs_2_), channel_id=1, source_target_pairs={{1,0},{2,1},{3,2},{4,3},{5,4},{6,5},{7,6},{9,8},{10,9},{11,10},{12... | collective-permute-start | bytes 786440 | tf_op jit(solution)/shard_map/ppermute | solution.py:31
  37.5 3.1 %collective-permute-start.6 = (f32[2,128,128]{2,1,0:T(8,128)}, f32[2,128,128]{2,1,0:T(8,128)S(1)}, u32[]{:S(2)}, u32[]{:S(2)}) collective-permute-start(f32[2,128,128]{2,1,0:T(8,128)} %get-tuple-element.46.refs_6_), channel_id=1, source_target_pairs={{0,8},{1,9},{2,10},{3,11},{4,12},{5,13},{6,14},{7,15},{8,16},{9,17... | collective-permute-start | bytes 393224 | tf_op jit(solution)/shard_map/ppermute | solution.py:31
  40.6 2.2 %collective-permute-start.8 = (f32[2,128,128]{2,1,0:T(8,128)S(1)}, f32[2,128,128]{2,1,0:T(8,128)}, u32[]{:S(2)}, u32[]{:S(2)}) collective-permute-start(f32[2,128,128]{2,1,0:T(8,128)S(1)} %shard_map.102), channel_id=1, source_target_pairs={{8,0},{9,1},{10,2},{11,3},{12,4},{13,5},{14,6},{15,7},{16,8},{17,9... | collective-permute-start | bytes 393224 | tf_op jit(solution)/shard_map/ppermute | solution.py:31
  42.8 1.9 %collective-permute-start.10 = (f32[2,128,128]{2,1,0:T(8,128)}, f32[2,128,128]{2,1,0:T(8,128)}, u32[]{:S(2)}, u32[]{:S(2)}) collective-permute-start(f32[2,128,128]{2,1,0:T(8,128)} %get-tuple-element.50), channel_id=1, source_target_pairs={{9,0},{10,1},{11,2},{12,3},{13,4},{14,5},{15,6},{17,8},{18,9},{19,... | collective-permute-start | bytes 393224 | tf_op jit(solution)/shard_map/ppermute | solution.py:31
  44.8 1.9 %collective-permute-start.7 = (f32[2,128,128]{2,1,0:T(8,128)}, f32[2,128,128]{2,1,0:T(8,128)}, u32[]{:S(2)}, u32[]{:S(2)}) collective-permute-start(f32[2,128,128]{2,1,0:T(8,128)} %get-tuple-element.50), channel_id=1, source_target_pairs={{8,0},{9,1},{10,2},{11,3},{12,4},{13,5},{14,6},{15,7},{16,8},{17,9... | collective-permute-start | bytes 393224 | tf_op jit(solution)/shard_map/ppermute | solution.py:31
  47.6 1.1 %collective-permute-done.8.refs_5_ = f32[2,128,128]{2,1,0:T(8,128)} collective-permute-done((f32[2,128,128]{2,1,0:T(8,128)S(1)}, f32[2,128,128]{2,1,0:T(8,128)}, u32[]{:S(2)}, u32[]{:S(2)}) %collective-permute-start.8) | collective-permute-done | bytes 131104 | tf_op jit(solution)/shard_map/ppermute | solution.py:31
  48.8 3.1 %collective-permute-done.10.refs_8_ = f32[2,128,128]{2,1,0:T(8,128)} collective-permute-done((f32[2,128,128]{2,1,0:T(8,128)}, f32[2,128,128]{2,1,0:T(8,128)}, u32[]{:S(2)}, u32[]{:S(2)}) %collective-permute-start.10) | collective-permute-done | bytes 131104 | tf_op jit(solution)/shard_map/ppermute | solution.py:31
  51.9 2.9 %collective-permute-done.7.refs_4_ = f32[2,128,128]{2,1,0:T(8,128)} collective-permute-done((f32[2,128,128]{2,1,0:T(8,128)}, f32[2,128,128]{2,1,0:T(8,128)}, u32[]{:S(2)}, u32[]{:S(2)}) %collective-permute-start.7) | collective-permute-done | bytes 131104 | tf_op jit(solution)/shard_map/ppermute | solution.py:31
  54.9 2.7 %shard_map.104 = (f32[2,128,256]{2,1,0:T(8,128)S(1)}, f32[2,128,256]{2,1,0:T(8,128)S(1)}, f32[2,128,128]{2,1,0:T(8,128)S(1)}, f32[2,128,128]{2,1,0:T(8,128)S(1)}, f32[256,256]{1,0:T(8,128)S(1)}) custom-call(s32[2]{0:T(128)S(1)} %bitcast.9, s32[1]{0:T(128)} %bitcast.2.refs_1_, f32[2,256,128]{2,1,0:T(8,128)S(1)} %get-tuple-element.45.left_ref.refs_2_, ...), custom_call_target="tpu_custom_call" | custom-call | flops 1000000000 | bytes 1000000 | tf_op jit(solution)/shard_map/pallas_call | solution.py:335
  57.6 0.8 %shard_map.105 = (f32[2,128,256]{2,1,0:T(8,128)S(1)}, f32[2,256,128]{2,1,0:T(8,128)S(1)}) custom-call(s32[2]{0:T(128)S(1)} %bitcast.10, f32[256,256]{1,0:T(8,128)S(1)} %get-tuple-element.52.xb_ref, f32[2,128,128]{2,1,0:T(8,128)S(1)} %get-tuple-element.53.r00_ref, f32[2,256,256]{2,1,0:T(8,128)S(1)} %get-tuple-element.33.probe_ref.refs_6_.refs_9_, ...), custom_call_target="tpu_custom_call" | custom-call | flops 100000000 | bytes 1000000 | tf_op jit(solution)/shard_map/pallas_call | solution.py:312
  58.5 3.6 %collective-permute-start.12 = (f32[2,256,128]{2,1,0:T(8,128)S(1)}, f32[2,256,128]{2,1,0:T(8,128)S(1)}, u32[]{:S(2)}, u32[]{:S(2)}) collective-permute-start(f32[2,256,128]{2,1,0:T(8,128)S(1)} %get-tuple-element.56), channel_id=1, source_target_pairs={{0,1},{1,2},{2,3},{3,4},{4,5},{5,6},{6,7},{8,9},{9,10},{10,11},{11... | collective-permute-start | bytes 786440 | tf_op jit(solution)/shard_map/ppermute | solution.py:31
  62.1 3.1 %collective-permute-start.11 = (f32[2,128,256]{2,1,0:T(8,128)S(1)}, f32[2,128,256]{2,1,0:T(8,128)S(1)}, u32[]{:S(2)}, u32[]{:S(2)}) collective-permute-start(f32[2,128,256]{2,1,0:T(8,128)S(1)} %get-tuple-element.55), channel_id=1, source_target_pairs={{0,8},{1,9},{2,10},{3,11},{4,12},{5,13},{6,14},{7,15},{8,16},{9,17... | collective-permute-start | bytes 786440 | tf_op jit(solution)/shard_map/ppermute | solution.py:31
  65.2 1.9 %collective-permute-start.13 = (f32[2,128,128]{2,1,0:T(8,128)S(1)}, f32[2,128,128]{2,1,0:T(8,128)S(1)}, u32[]{:S(2)}, u32[]{:S(2)}) collective-permute-start(f32[2,128,128]{2,1,0:T(8,128)S(1)} %get-tuple-element.57), channel_id=1, source_target_pairs={{0,9},{1,10},{2,11},{3,12},{4,13},{5,14},{6,15},{8,17},{9,18},{10,... | collective-permute-start | bytes 393224 | tf_op jit(solution)/shard_map/ppermute | solution.py:31
  67.1 7.0 %collective-permute-done.13.diag_ref = f32[2,128,128]{2,1,0:T(8,128)S(1)} collective-permute-done((f32[2,128,128]{2,1,0:T(8,128)S(1)}, f32[2,128,128]{2,1,0:T(8,128)S(1)}, u32[]{:S(2)}, u32[]{:S(2)}) %collective-permute-start.13) | collective-permute-done | bytes 131104 | tf_op jit(solution)/shard_map/ppermute | solution.py:31
  74.1 1.1 %shard_map.106 = (f32[2,256,256]{2,1,0:T(8,128)}, f32[2,256,256]{2,1,0:T(8,128)}) custom-call(f32[2,256,128]{2,1,0:T(8,128)S(1)} %get-tuple-element.45.left_ref.refs_2_, f32[2,256,128]{2,1,0:T(8,128)S(1)} %get-tuple-element.47.right_ref.refs_3_, f32[2,256,128]{2,1,0:T(8,128)S(1)} %get-tuple-element.48.vl_ref, f32[2,256,128]{2,1,0:T(8,128)S(1)} %get-tuple-element.49.vr_ref, ...), custom_call_target="tpu_custom_call" | custom-call | flops 1000000 | bytes 1000000 | tf_op jit(solution)/shard_map/pallas_call | solution.py:342
  (29 shorter events, 3.1 us)
Async XLA Ops:
  0.6 1.0 %copy-start.1 = (f32[2,256,256]{2,1,0:T(8,128)S(1)}, f32[2,256,256]{2,1,0:T(8,128)}, u32[]{:S(2)}) copy-start(f32[2,256,256]{2,1,0:T(8,128)} %obj_ref.1) | copy-start | bytes 1572868
  1.7 6.9 %copy-start.2 = (f32[2,256,256]{2,1,0:T(8,128)S(1)}, f32[2,256,256]{2,1,0:T(8,128)}, u32[]{:S(2)}) copy-start(f32[2,256,256]{2,1,0:T(8,128)} %probe_hbm.1) | copy-start | bytes 1572868
  1.7 6.9 %copy-start.3 = (bf16[4,256,256]{2,1,0:T(8,128)(2,1)S(1)}, bf16[4,256,256]{2,1,0:T(8,128)(2,1)}, u32[]{:S(2)}) copy-start(bf16[4,256,256]{2,1,0:T(8,128)(2,1)} %constant.13.clone.table_hbm) | copy-start | bytes 1572868
  1.7 11.7 %collective-permute-start.1 = (f32[2,256,128]{2,1,0:T(8,128)S(1)}, f32[2,256,128]{2,1,0:T(8,128)S(1)}, u32[]{:S(2)}, u32[]{:S(2)}) collective-permute-start(f32[2,256,128]{2,1,0:T(8,128)S(1)} %get-tuple-element.30.left_ref.refs_1_), channel_id=1, source_target_pairs={{1,0},{2,1},{3,2},{4,3},{5,4},{6,5},{7,6},{9,8},{10,9},{11,10},{12... | collective-permute-start | bytes 786440 | tf_op jit(solution)/shard_map/ppermute | solution.py:31
  4.5 12.0 %collective-permute-start = (f32[2,128,256]{2,1,0:T(8,128)S(1)}, f32[2,128,256]{2,1,0:T(8,128)S(1)}, u32[]{:S(2)}, u32[]{:S(2)}) collective-permute-start(f32[2,128,256]{2,1,0:T(8,128)S(1)} %slice.3), channel_id=1, source_target_pairs={{8,0},{9,1},{10,2},{11,3},{12,4},{13,5},{14,6},{15,7},{16,8},{17,9... | collective-permute-start | bytes 786440 | tf_op jit(solution)/shard_map/ppermute | solution.py:31
  6.6 8.9 %collective-permute-start.2 = (f32[2,128,128]{2,1,0:T(8,128)S(1)}, f32[2,128,128]{2,1,0:T(8,128)S(1)}, u32[]{:S(2)}, u32[]{:S(2)}) collective-permute-start(f32[2,128,128]{2,1,0:T(8,128)S(1)} %get-tuple-element.32), channel_id=1, source_target_pairs={{9,0},{10,1},{11,2},{12,3},{13,4},{14,5},{15,6},{17,8},{18,9},{19,... | collective-permute-start | bytes 393224 | tf_op jit(solution)/shard_map/ppermute | solution.py:31
  8.6 0.7 copy-start.6
  9.2 0.9 %copy-start.4 = (f32[1,1,1,256,256]{4,3,2,1,0:T(8,128)S(1)}, f32[1,1,1,256,256]{4,3,2,1,0:T(8,128)}, u32[]{:S(2)}) copy-start(f32[1,1,1,256,256]{4,3,2,1,0:T(8,128)} %param.11) | copy-start | bytes 786436
  10.2 0.9 %copy-start.5 = (f32[2,128,128]{2,1,0:T(8,128)S(1)}, f32[2,128,128]{2,1,0:T(8,128)}, u32[]{:S(2)}) copy-start(f32[2,128,128]{2,1,0:T(8,128)} %constant.15.clone.rows_hbm) | copy-start | bytes 393220
  11.1 0.7 copy-start.7
  13.4 3.1 %copy-start.8 = (f32[256,256]{1,0:T(8,128)}, f32[256,256]{1,0:T(8,128)S(1)}, u32[]{:S(2)}) copy-start(f32[256,256]{1,0:T(8,128)S(1)} %get-tuple-element.34.refs_7_.refs_10_) | copy-start | bytes 786436
  19.4 15.5 %copy-start = (f32[2,256,256]{2,1,0:T(8,128)S(1)}, f32[2,256,256]{2,1,0:T(8,128)}, u32[]{:S(2)}) copy-start(f32[2,256,256]{2,1,0:T(8,128)} %vel_ref.5) | copy-start | bytes 1572868
  20.2 14.6 %collective-permute-start.4 = (f32[2,256,128]{2,1,0:T(8,128)S(1)}, f32[2,256,128]{2,1,0:T(8,128)S(1)}, u32[]{:S(2)}, u32[]{:S(2)}) collective-permute-start(f32[2,256,128]{2,1,0:T(8,128)S(1)} %get-tuple-element.43), channel_id=1, source_target_pairs={{0,1},{1,2},{2,3},{3,4},{4,5},{5,6},{6,7},{8,9},{9,10},{10,11},{11... | collective-permute-start | bytes 786440 | tf_op jit(solution)/shard_map/ppermute | solution.py:31
  25.6 6.4 %collective-permute-start.3 = (f32[2,128,128]{2,1,0:T(8,128)S(1)}, f32[2,128,128]{2,1,0:T(8,128)S(1)}, u32[]{:S(2)}, u32[]{:S(2)}) collective-permute-start(f32[2,128,128]{2,1,0:T(8,128)S(1)} %get-tuple-element.42), channel_id=1, source_target_pairs={{0,8},{1,9},{2,10},{3,11},{4,12},{5,13},{6,14},{7,15},{8,16},{9,17... | collective-permute-start | bytes 393224 | tf_op jit(solution)/shard_map/ppermute | solution.py:31
  27.8 7.0 %collective-permute-start.5 = (f32[2,128,128]{2,1,0:T(8,128)S(1)}, f32[2,128,128]{2,1,0:T(8,128)S(1)}, u32[]{:S(2)}, u32[]{:S(2)}) collective-permute-start(f32[2,128,128]{2,1,0:T(8,128)S(1)} %get-tuple-element.44), channel_id=1, source_target_pairs={{0,9},{1,10},{2,11},{3,12},{4,13},{5,14},{6,15},{8,17},{9,18},{10,... | collective-permute-start | bytes 393224 | tf_op jit(solution)/shard_map/ppermute | solution.py:31
  35.6 11.2 %collective-permute-start.9 = (f32[2,256,128]{2,1,0:T(8,128)S(1)}, f32[2,256,128]{2,1,0:T(8,128)S(1)}, u32[]{:S(2)}, u32[]{:S(2)}) collective-permute-start(f32[2,256,128]{2,1,0:T(8,128)S(1)} %get-tuple-element.45.left_ref.refs_2_), channel_id=1, source_target_pairs={{1,0},{2,1},{3,2},{4,3},{5,4},{6,5},{7,6},{9,8},{10,9},{11,10},{12... | collective-permute-start | bytes 786440 | tf_op jit(solution)/shard_map/ppermute | solution.py:31
  37.5 9.2 %collective-permute-start.6 = (f32[2,128,128]{2,1,0:T(8,128)}, f32[2,128,128]{2,1,0:T(8,128)S(1)}, u32[]{:S(2)}, u32[]{:S(2)}) collective-permute-start(f32[2,128,128]{2,1,0:T(8,128)} %get-tuple-element.46.refs_6_), channel_id=1, source_target_pairs={{0,8},{1,9},{2,10},{3,11},{4,12},{5,13},{6,14},{7,15},{8,16},{9,17... | collective-permute-start | bytes 393224 | tf_op jit(solution)/shard_map/ppermute | solution.py:31
  40.6 8.1 %collective-permute-start.8 = (f32[2,128,128]{2,1,0:T(8,128)S(1)}, f32[2,128,128]{2,1,0:T(8,128)}, u32[]{:S(2)}, u32[]{:S(2)}) collective-permute-start(f32[2,128,128]{2,1,0:T(8,128)S(1)} %shard_map.102), channel_id=1, source_target_pairs={{8,0},{9,1},{10,2},{11,3},{12,4},{13,5},{14,6},{15,7},{16,8},{17,9... | collective-permute-start | bytes 393224 | tf_op jit(solution)/shard_map/ppermute | solution.py:31
  42.8 9.1 %collective-permute-start.10 = (f32[2,128,128]{2,1,0:T(8,128)}, f32[2,128,128]{2,1,0:T(8,128)}, u32[]{:S(2)}, u32[]{:S(2)}) collective-permute-start(f32[2,128,128]{2,1,0:T(8,128)} %get-tuple-element.50), channel_id=1, source_target_pairs={{9,0},{10,1},{11,2},{12,3},{13,4},{14,5},{15,6},{17,8},{18,9},{19,... | collective-permute-start | bytes 393224 | tf_op jit(solution)/shard_map/ppermute | solution.py:31
  44.8 10.1 %collective-permute-start.7 = (f32[2,128,128]{2,1,0:T(8,128)}, f32[2,128,128]{2,1,0:T(8,128)}, u32[]{:S(2)}, u32[]{:S(2)}) collective-permute-start(f32[2,128,128]{2,1,0:T(8,128)} %get-tuple-element.50), channel_id=1, source_target_pairs={{8,0},{9,1},{10,2},{11,3},{12,4},{13,5},{14,6},{15,7},{16,8},{17,9... | collective-permute-start | bytes 393224 | tf_op jit(solution)/shard_map/ppermute | solution.py:31
  46.8 8.1 %copy-start.9 = (f32[256,256]{1,0:T(8,128)S(1)}, f32[256,256]{1,0:T(8,128)}, u32[]{:S(2)}) copy-start(f32[256,256]{1,0:T(8,128)} %copy-done.8) | copy-start | bytes 786436
  58.5 15.6 %collective-permute-start.12 = (f32[2,256,128]{2,1,0:T(8,128)S(1)}, f32[2,256,128]{2,1,0:T(8,128)S(1)}, u32[]{:S(2)}, u32[]{:S(2)}) collective-permute-start(f32[2,256,128]{2,1,0:T(8,128)S(1)} %get-tuple-element.56), channel_id=1, source_target_pairs={{0,1},{1,2},{2,3},{3,4},{4,5},{5,6},{6,7},{8,9},{9,10},{10,11},{11... | collective-permute-start | bytes 786440 | tf_op jit(solution)/shard_map/ppermute | solution.py:31
  62.1 12.0 %collective-permute-start.11 = (f32[2,128,256]{2,1,0:T(8,128)S(1)}, f32[2,128,256]{2,1,0:T(8,128)S(1)}, u32[]{:S(2)}, u32[]{:S(2)}) collective-permute-start(f32[2,128,256]{2,1,0:T(8,128)S(1)} %get-tuple-element.55), channel_id=1, source_target_pairs={{0,8},{1,9},{2,10},{3,11},{4,12},{5,13},{6,14},{7,15},{8,16},{9,17... | collective-permute-start | bytes 786440 | tf_op jit(solution)/shard_map/ppermute | solution.py:31
  65.2 8.9 %collective-permute-start.13 = (f32[2,128,128]{2,1,0:T(8,128)S(1)}, f32[2,128,128]{2,1,0:T(8,128)S(1)}, u32[]{:S(2)}, u32[]{:S(2)}) collective-permute-start(f32[2,128,128]{2,1,0:T(8,128)S(1)} %get-tuple-element.57), channel_id=1, source_target_pairs={{0,9},{1,10},{2,11},{3,12},{4,13},{5,14},{6,15},{8,17},{9,18},{10,... | collective-permute-start | bytes 393224 | tf_op jit(solution)/shard_map/ppermute | solution.py:31

commit v2 on v1

--- a/solution.py
+++ b/solution.py
@@ -2,7 +2,6 @@
 
 import jax
 import jax.numpy as jnp
-import numpy as np
 from jax import lax
 from jax.experimental import pallas as pl
 from jax.experimental.pallas import tpu as pltpu
@@ -31,21 +30,10 @@
     return lax.ppermute(value, ("row", "col"), pairs)
 
 
-def constants():
-    index = np.arange(H)
-    angle = -2.0 * math.pi * (index[:, None] * index[None, :] % H) / H
-    scale = 1.0 / math.sqrt(P_SIZE)
-    c, s = np.cos(angle) * scale, np.sin(angle) * scale
-    pairs = []
-    for block in (np.block([[c, s], [-s, c]]), np.block([[c, -s], [s, c]])):
-        block = block.astype(np.float32)
-        high = block.astype(jnp.bfloat16)
-        pairs += [high, (block - high.astype(np.float32)).astype(jnp.bfloat16)]
-    turn = -2.0 * math.pi * index / P_SIZE
-    twiddle = np.stack([np.cos(turn), np.sin(turn)]).astype(np.float32)
-    along_cols = np.broadcast_to(twiddle[:, None, :], (2, 8, H))
-    along_rows = np.broadcast_to(twiddle[:, :, None], (2, H, H))
-    return np.stack(pairs), np.ascontiguousarray(along_cols), np.ascontiguousarray(along_rows)
+def turns(step, length, scale):
+    step = jnp.where(step > length // 2, step - length, step)
+    angle = step.astype(jnp.float32) * (-2.0 * math.pi / length)
+    return jnp.cos(angle) * scale, jnp.sin(angle) * scale
 
 
 def halves(x):
@@ -79,29 +67,29 @@
     return table_ref[2], table_ref[3]
 
 
-def unpack_kernel(obj_ref, left_out, right_out, q00_out):
+def unpack_kernel(obj_ref, left_out, right_out, q00_out, send_out):
     for part in range(2):
         left_out[part] = obj_ref[part, :, :H]
+        send_out[part] = obj_ref[part, :, :H]
         right_out[part] = obj_ref[part, :, H:]
         q00_out[part] = obj_ref[part, :H, :H]
 
 
 def prep_kernel(
-    pos_ref, probe_hbm, meas_hbm, table_hbm, cols_hbm, rows_hbm,
-    probe_out, meas_out, table_out, cols_out, rows_out, probe_ref, meas_ref, sems,
+    pos_ref, below_ref, probe_ref, meas_ref, probe_out, meas_out, mask_out, table_out, cols_out, rows_out
 ):
-    copies = [
-        pltpu.make_async_copy(source, target, sems.at[number])
-        for number, (source, target) in enumerate(
-            ((probe_hbm, probe_ref), (meas_hbm, meas_ref), (table_hbm, table_out), (cols_hbm, cols_out), (rows_hbm, rows_out))
-        )
-    ]
-    for copy in copies:
-        copy.start()
-    for copy in copies:
-        copy.wait()
     p0 = pos_ref[0]
     p1 = pos_ref[1]
+    row_id = lax.broadcasted_iota(jnp.int32, (H, H), 0)
+    col_id = lax.broadcasted_iota(jnp.int32, (H, H), 1)
+    mask_out[0] = jnp.where(row_id < p0, 1, 0)
+    mask_out[1] = jnp.where(col_id < p1, 1, 0)
+    mask_out[2] = jnp.full((H, H), below_ref[0], jnp.int32)
+    c, s = turns(row_id * col_id & (H - 1), H, 1.0 / math.sqrt(P_SIZE))
+    for number, block in enumerate((quads(c, s, -s, c), quads(c, -s, s, c))):
+        table_out[2 * number], table_out[2 * number + 1] = halves(block)
+    rows_out[0], rows_out[1] = turns(row_id, P_SIZE, 1.0)
+    cols_out[0], cols_out[1] = turns(col_id[:8], P_SIZE, 1.0)
     for part in range(2):
         x = pltpu.roll(probe_ref[part], p0, 0)
         probe_out[part] = pltpu.roll(x, p1, 1)
@@ -144,14 +132,12 @@
     return pr * br + pi * bi, pr * bi - pi * br
 
 
-def masks(pos_ref):
-    row_id = lax.broadcasted_iota(jnp.int32, (H, H), 0)
-    col_id = lax.broadcasted_iota(jnp.int32, (H, H), 1)
-    return row_id < pos_ref[0], col_id < pos_ref[1]
-
-
-def pre_kernel(pos_ref, left_ref, right_ref, beside_ref, probe_ref, table_ref, cols_ref, y_ref):
-    _, beyond = masks(pos_ref)
+def masks(mask_ref):
+    return mask_ref[0] > 0, mask_ref[1] > 0
+
+
+def pre_kernel(mask_ref, left_ref, right_ref, beside_ref, probe_ref, table_ref, cols_ref, y_ref):
+    _, beyond = masks(mask_ref)
     patch = [
         jnp.concatenate(
             [jnp.where(beyond, beside_ref[part, H:], left_ref[part, H:]), right_ref[part, H:]], axis=1
@@ -161,18 +147,23 @@
     y_ref[...] = row_stage(patch, probe_ref[0, H:], probe_ref[1, H:], plus(table_ref), cols_ref)
 
 
-def main_kernel(split, *refs):
-    if split:
-        (pos_ref, left_ref, right_ref, lower_ref, beside_ref, corner_ref, probe_ref, meas_ref, yb_ref,
-         table_ref, cols_ref, rows_ref, own_out, d00_out, d01_out, diag_out, r00_out, xb_out) = refs
-        lower = [[lower_ref[part, :, :H], lower_ref[part, :, H:]] for part in range(2)]
+def main_kernel(form, *refs):
+    split = form == "first"
+    if form == "first":
+        (mask_ref, left_ref, right_ref, lower_ref, beside_ref, corner_ref, probe_ref, meas_ref, yb_ref,
+         table_ref, cols_ref, rows_ref, own_out, d00_out, d01_out, kept_out, diag_out, r00_out, xb_out) = refs
+    elif form == "whole":
+        (mask_ref, left_ref, right_ref, lower_ref, beside_ref, corner_ref, probe_ref, meas_ref, yb_ref,
+         table_ref, cols_ref, rows_ref, own_out, down_out, diag_out, r00_out, xb_out) = refs
     else:
-        (pos_ref, below_ref, left_ref, right_ref, up00_ref, up01_ref, mine01_ref, beside_ref, corner_ref,
+        (mask_ref, left_ref, right_ref, up00_ref, up01_ref, mine01_ref, beside_ref, corner_ref,
          probe_ref, meas_ref, yb_ref, table_ref, cols_ref, rows_ref,
          own_out, down_out, diag_out, r00_out, xb_out) = refs
-        scale = jnp.where(below_ref[0] > 0, step_size, 0.0)
+        scale = mask_ref[2].astype(jnp.float32) * step_size
         lower = [[up00_ref[part], up01_ref[part] - scale * mine01_ref[part]] for part in range(2)]
-    below, beyond = masks(pos_ref)
+    if form != "second":
+        lower = [[lower_ref[part, :, :H], lower_ref[part, :, H:]] for part in range(2)]
+    below, beyond = masks(mask_ref)
     pr, pi = probe_ref[0, :H], probe_ref[1, :H]
     patch = []
     for part in range(2):
@@ -212,6 +203,7 @@
         if split:
             d00_out[part] = d00
             d01_out[part] = d01
+            kept_out[part] = d01
         else:
             down_out[part, :, :H] = d00
             down_out[part, :, H:] = d01
@@ -219,8 +211,8 @@
         r00_out[part] = jnp.where(jnp.logical_and(~below, beyond), g00, 0.0)
 
 
-def post_kernel(pos_ref, xb_ref, r00_ref, probe_ref, table_ref, cols_ref, own_out, right_out):
-    _, beyond = masks(pos_ref)
+def post_kernel(mask_ref, xb_ref, r00_ref, probe_ref, table_ref, cols_ref, own_out, right_out):
+    _, beyond = masks(mask_ref)
     out = back_stage(xb_ref[...], probe_ref[0, H:], probe_ref[1, H:], minus(table_ref), cols_ref)
     for part in range(2):
         g10, g11 = out[part][:, :H], out[part][:, H:]
@@ -240,15 +232,20 @@
         up_out[part], _ = stepped(right_ref[part, :H], vel_ref[part, :H, H:], own_ref[part, :, H:])
 
 
-def left_update_kernel(left_ref, vel_ref, top_ref, bottom_ref, d00_ref, before_ref, diag_ref, obj_out, q00_out, vel_out):
+def left_update_kernel(left_ref, vel_ref, top_ref, bottom_ref, d00_ref, before_ref, diag_ref, obj_out, up_out, corner_out, send_out, vel_out):
     for part in range(2):
         g00 = (top_ref[part, :, :H] + d00_ref[part]) + (before_ref[part, :H] + diag_ref[part])
         g10 = bottom_ref[part, :, :H] + before_ref[part, H:]
         obj, vel = stepped(left_ref[part, :H], vel_ref[part, :H, :H], g00)
         obj_out[part, :H] = obj
-        q00_out[part] = obj
+        send_out[part, :H] = obj
+        up_out[part] = obj
+        corner_out[part] = obj
         vel_out[part, :H] = vel
-        obj_out[part, H:], vel_out[part, H:] = stepped(left_ref[part, H:], vel_ref[part, H:, :H], g10)
+        obj, vel = stepped(left_ref[part, H:], vel_ref[part, H:, :H], g10)
+        obj_out[part, H:] = obj
+        send_out[part, H:] = obj
+        vel_out[part, H:] = vel
 
 
 def right_update_kernel(right_ref, vel_ref, top_ref, bottom_ref, d01_ref, obj_out, vel_out):
@@ -258,6 +255,25 @@
         obj_out[part, H:], vel_out[part, H:] = stepped(
             right_ref[part, H:], vel_ref[part, H:, H:], bottom_ref[part, :, H:]
         )
+
+
+def update_kernel(
+    left_ref, right_ref, vel_ref, top_ref, bottom_ref, above_ref, before_ref, diag_ref,
+    left_out, right_out, vl_out, vr_out, strip_out, corner_out, send_out,
+):
+    for part in range(2):
+        g00 = (top_ref[part, :, :H] + above_ref[part, :, :H]) + (before_ref[part, :H] + diag_ref[part])
+        g01 = top_ref[part, :, H:] + above_ref[part, :, H:]
+        g10 = bottom_ref[part, :, :H] + before_ref[part, H:]
+        g11 = bottom_ref[part, :, H:]
+        obj, vel = stepped(left_ref[part, :H], vel_ref[part, :H, :H], g00)
+        left_out[part, :H], vl_out[part, :H] = obj, vel
+        strip_out[part, :, :H], corner_out[part], send_out[part, :H] = obj, obj, obj
+        obj, vel = stepped(right_ref[part, :H], vel_ref[part, :H, H:], g01)
+        right_out[part, :H], vr_out[part, :H], strip_out[part, :, H:] = obj, vel, obj
+        obj, vel = stepped(left_ref[part, H:], vel_ref[part, H:, :H], g10)
+        left_out[part, H:], vl_out[part, H:], send_out[part, H:] = obj, vel, obj
+        right_out[part, H:], vr_out[part, H:] = stepped(right_ref[part, H:], vel_ref[part, H:, H:], g11)
 
 
 def final_kernel(left_ref, right_ref, vl_ref, vr_ref, top_ref, bottom_ref, above_ref, before_ref, diag_ref, obj_out, vel_out):
@@ -275,70 +291,93 @@
     return jax.ShapeDtypeStruct(dims, dtype)
 
 
-def kernel(body, flops, scalars, arrays, outs, space=VMEM, scratch=()):
+def kernel(body, flops, scalars, arrays, outs):
     return pl.pallas_call(
         body,
         out_shape=outs,
-        in_specs=[SMEM] * scalars + [space] * arrays,
+        in_specs=[SMEM] * scalars + [VMEM] * arrays,
         out_specs=(VMEM,) * len(outs),
-        scratch_shapes=scratch,
         compiler_params=pltpu.CompilerParams(vmem_limit_bytes=16 * 1024 * 1024),
         cost_estimate=pl.CostEstimate(flops=flops, bytes_accessed=10**6, transcendentals=0),
     )
 
 
+AHEAD = False
+
+
 def steps(object_field, velocity, positions, measured, probe):
-    tables, along_cols, along_rows = (jnp.asarray(x) for x in constants())
     offsets = positions[0, 0, 0]
     intensity = measured[0, 0, 0]
     has_below = (lax.axis_index("row") < lax.axis_size("row") - 1).astype(jnp.int32).reshape(1)
     half, strip, quad, rows = shape(2, N, H), shape(2, H, N), shape(2, H, H), shape(N, N)
 
     lower = shifted(object_field[:, :H, :], -1, 0)
-    left, right, q00 = kernel(unpack_kernel, 10**6, 0, 1, (half, half, quad))(object_field)
+    left, right, q00, left_send = kernel(unpack_kernel, 10**6, 0, 1, (half, half, quad, half))(object_field)
+    beside = shifted(left_send, 0, -1)
     corner = shifted(q00, -1, -1)
-    beside = shifted(left, 0, -1)
-    turned, intensity, tables, along_cols, along_rows = kernel(
-        prep_kernel, 10**8, 1, 5,
-        (shape(2, N, N), rows, shape(4, N, N, dtype=jnp.bfloat16), shape(2, 8, H), shape(2, H, H)),
-        pl.BlockSpec(memory_space=pl.ANY),
-        (pltpu.VMEM((2, N, N), jnp.float32), pltpu.VMEM((N, N), jnp.float32), pltpu.SemaphoreType.DMA((5,))),
-    )(offsets, probe, intensity, tables, along_cols, along_rows)
+    turned, intensity, mask, tables, along_cols, along_rows = kernel(
+        prep_kernel, 10**8, 2, 2,
+        (
+            shape(2, N, N), rows, shape(3, H, H, dtype=jnp.int32),
+            shape(4, N, N, dtype=jnp.bfloat16), shape(2, 8, H), shape(2, H, H),
+        ),
+    )(offsets, has_below, probe, intensity)
 
     def pre(left, right, beside):
-        return kernel(pre_kernel, 10**8, 1, 6, (rows,))(offsets, left, right, beside, turned, tables, along_cols)[0]
+        return kernel(pre_kernel, 10**8, 0, 7, (rows,))(
+            mask, left, right, beside, turned, tables, along_cols
+        )[0]
+
+    def main(body, outs, *arrays):
+        rest = (turned, intensity, pre(arrays[0], arrays[1], arrays[-2]), tables, along_cols, along_rows)
+        return kernel(body, 10**9, 0, 1 + len(arrays) + len(rest), outs)(mask, *arrays, *rest)
 
     def post(xb, r00):
-        return kernel(post_kernel, 10**8, 1, 5, (strip, half))(offsets, xb, r00, turned, tables, along_cols)
-
-    yb = pre(left, right, beside)
-    top, d00, d01, diag, r00, xb = kernel(
-        lambda *refs: main_kernel(True, *refs), 10**9, 1, 11, (strip, quad, quad, quad, quad, rows)
-    )(offsets, left, right, lower, beside, corner, turned, intensity, yb, tables, along_cols, along_rows)
-    from_above = shifted(d00, 1, 0)
-    from_corner = shifted(diag, 1, 1)
+        return kernel(post_kernel, 10**8, 0, 6, (strip, half))(mask, xb, r00, turned, tables, along_cols)
+
+    def whole(*refs):
+        main_kernel("whole", *refs)
+
+    if AHEAD:
+        top, d00, d01, kept, diag, r00, xb = main(
+            lambda *refs: main_kernel("first", *refs), (strip, quad, quad, quad, quad, quad, rows),
+            left, right, lower, beside, corner,
+        )
+        from_above = shifted(d00, 1, 0)
+        from_corner = shifted(diag, 1, 1)
+        bottom, right_part = post(xb, r00)
+        before = shifted(right_part, 0, 1)
+        above01 = shifted(d01, 1, 0)
+        (ahead,) = kernel(ahead_kernel, 10**6, 0, 3, (quad,))(right, velocity, top)
+        up01 = shifted(ahead, -1, 0)
+        left, q00, q00_corner, left_send, vel_left = kernel(
+            left_update_kernel, 10**6, 0, 7, (half, quad, quad, half, half)
+        )(left, velocity, top, bottom, from_above, before, from_corner)
+        up00 = shifted(q00, -1, 0)
+        beside = shifted(left_send, 0, -1)
+        corner = shifted(q00_corner, -1, -1)
+        right, vel_right = kernel(right_update_kernel, 10**6, 0, 5, (half, half))(right, velocity, top, bottom, above01)
+        top, down, diag, r00, xb = main(
+            lambda *refs: main_kernel("second", *refs), (strip, strip, quad, quad, rows),
+            left, right, up00, up01, kept, beside, corner,
+        )
+    else:
+        top, down, diag, r00, xb = main(whole, (strip, strip, quad, quad, rows), left, right, lower, beside, corner)
+        above = shifted(down, 1, 0)
+        bottom, right_part = post(xb, r00)
+        before = shifted(right_part, 0, 1)
+        from_corner = shifted(diag, 1, 1)
+        left, right, vel_left, vel_right, strip_send, q00, left_send = kernel(
+            update_kernel, 10**6, 0, 8, (half, half, half, half, strip, quad, half)
+        )(left, right, velocity, top, bottom, above, before, from_corner)
+        lower = shifted(strip_send, -1, 0)
+        beside = shifted(left_send, 0, -1)
+        corner = shifted(q00, -1, -1)
+        top, down, diag, r00, xb = main(whole, (strip, strip, quad, quad, rows), left, right, lower, beside, corner)
+    above = shifted(down, 1, 0)
     bottom, right_part = post(xb, r00)
     before = shifted(right_part, 0, 1)
-    above01 = shifted(d01, 1, 0)
-    (ahead,) = kernel(ahead_kernel, 10**6, 0, 3, (quad,))(right, velocity, top)
-    up01 = shifted(ahead, -1, 0)
-
-    left, q00, vel_left = kernel(left_update_kernel, 10**6, 0, 7, (half, quad, half))(
-        left, velocity, top, bottom, from_above, before, from_corner
-    )
-    up00 = shifted(q00, -1, 0)
-    corner = shifted(q00, -1, -1)
-    beside = shifted(left, 0, -1)
-    right, vel_right = kernel(right_update_kernel, 10**6, 0, 5, (half, half))(right, velocity, top, bottom, above01)
-
-    yb = pre(left, right, beside)
-    top, down, diag, r00, xb = kernel(
-        lambda *refs: main_kernel(False, *refs), 10**9, 2, 13, (strip, strip, quad, quad, rows)
-    )(offsets, has_below, left, right, up00, up01, d01, beside, corner, turned, intensity, yb, tables, along_cols, along_rows)
-    above = shifted(down, 1, 0)
     from_corner = shifted(diag, 1, 1)
-    bottom, right_part = post(xb, r00)
-    before = shifted(right_part, 0, 1)
     return kernel(final_kernel, 10**6, 0, 9, (shape(2, N, N), shape(2, N, N)))(
         left, right, vel_left, vel_right, top, bottom, above, before, from_corner
     )

time: 76.7 us -> 69.1 us (0.901); the launches traced: 75.2 us -> 68.7 us
  waiting for transfers between devices: 21.5 us -> 27.3 us
  starting transfers between devices: 36 us -> 31 us
  Pallas kernels: 12.6 us -> 7.82 us
  local copies, waits for them, and re-layouts: 4.26 us -> 1.7 us
    ppermute x14 -> x12, waiting for transfers between devices: 21.5 us -> 27.3 us  [shifted(): return lax.ppermute(value, ('row', 'col'), pairs)]
    ppermute x14 -> x12, starting transfers between devices: 36 us -> 31 us  [shifted(): return lax.ppermute(value, ('row', 'col'), pairs)]
    pallas_call x11 -> x9, Pallas kernels: 11.5 us -> 6.68 us  [the longest x2 3.44 us: main(): kernel(body, 10 ** 9, 0, 1 + len(arrays) + len(rest), outs)]
    unnamed x20 -> x10, local copies, waits for them, and re-layouts: 4.24 us -> 1.68 us
  transfers between devices with their start and end apart: 14 -> 12, of which waited for: 8 -> 7; matrix products, arithmetic and copies ran while one was open for 0% -> 0% of each run, Pallas kernels for 5% -> 4%
where the time goes in v2:
time: 69.1 us; the launch traced here: 68.7 us
  starting transfers between devices  31 us (45%)
  waiting for transfers between devices  27.3 us (40%)
  Pallas kernels  7.82 us (11%)
  local copies, waits for them, and re-layouts  1.7 us (2%)
  between operations  0.86 us (1%)
    ppermute x12, starting transfers between devices, shifted(): return lax.ppermute(value, ('row', 'col'), pairs)  31 us
    ppermute x12, waiting for transfers between devices, shifted(): return lax.ppermute(value, ('row', 'col'), pairs)  27.3 us
    pallas_call x2, Pallas kernels, main(): kernel(body, 10 ** 9, 0, 1 + len(arrays) + len(rest), outs)  3.44 us
    pallas_call x1, Pallas kernels, steps(): kernel(prep_kernel, 10 ** 8, 2, 2, (shape(2, N, N), rows, shape(3, H, H,...  1.85 us
    unnamed x10, local copies, waits for them, and re-layouts  1.68 us
  transfers between devices with their start and end apart: 12, of which 7 were waited for; matrix products, arithmetic and copies ran while one was open for 0% of the time, Pallas kernels for 4%

profile of v2, /device:TPU:11, one launch (start us, length us, event | category | flops | bytes accessed | tf_op | source)
XLA Modules:
  0.0 68.7 jit_solution(8937359295240282152)
XLA Ops:
  0.6 1.0 %copy-done = f32[2,256,256]{2,1,0:T(8,128)S(1)} copy-done((f32[2,256,256]{2,1,0:T(8,128)S(1)}, f32[2,256,256]{2,1,0:T(8,128)}, u32[]{:S(2)}) %copy-start) | copy-done | bytes 524312
  1.7 0.1 shard_map.68
  1.7 0.0 copy-start.3
  1.7 2.7 %collective-permute-start.1 = (f32[2,256,128]{2,1,0:T(8,128)S(1)}, f32[2,256,128]{2,1,0:T(8,128)S(1)}, u32[]{:S(2)}, u32[]{:S(2)}) collective-permute-start(f32[2,256,128]{2,1,0:T(8,128)S(1)} %get-tuple-element.36), channel_id=1, source_target_pairs={{1,0},{2,1},{3,2},{4,3},{5,4},{6,5},{7,6},{9,8},{10,9},{11,10},{12... | collective-permute-start | bytes 786440 | tf_op jit(solution)/shard_map/ppermute | solution.py:30
  4.5 2.2 %collective-permute-start = (f32[2,128,256]{2,1,0:T(8,128)S(1)}, f32[2,128,256]{2,1,0:T(8,128)S(1)}, u32[]{:S(2)}, u32[]{:S(2)}) collective-permute-start(f32[2,128,256]{2,1,0:T(8,128)S(1)} %slice.3), channel_id=1, source_target_pairs={{8,0},{9,1},{10,2},{11,3},{12,4},{13,5},{14,6},{15,7},{16,8},{17,9... | collective-permute-start | bytes 786440 | tf_op jit(solution)/shard_map/ppermute | solution.py:30
  6.7 1.9 %collective-permute-start.2 = (f32[2,128,128]{2,1,0:T(8,128)S(1)}, f32[2,128,128]{2,1,0:T(8,128)S(1)}, u32[]{:S(2)}, u32[]{:S(2)}) collective-permute-start(f32[2,128,128]{2,1,0:T(8,128)S(1)} %get-tuple-element.37), channel_id=1, source_target_pairs={{9,0},{10,1},{11,2},{12,3},{13,4},{14,5},{15,6},{17,8},{18,9},{19,... | collective-permute-start | bytes 393224 | tf_op jit(solution)/shard_map/ppermute | solution.py:30
  8.6 0.6 copy-done.4
  9.3 1.8 %shard_map.69 = (f32[2,256,256]{2,1,0:T(8,128)S(1)}, f32[256,256]{1,0:T(8,128)S(1)}, s32[3,128,128]{2,1,0:T(8,128)S(1)}, bf16[4,256,256]{2,1,0:T(8,128)(2,1)S(1)...) custom-call(s32[2]{0:T(128)S(1)} %bitcast.4, s32[1]{0:T(128)} %bitcast.1.below_ref, f32[2,256,256]{2,1,0:T(8,128)S(1)} %copy-done.2, ...), custom_call_target="tpu_custom_call" | custom-call | flops 100000000 | bytes 1000000 | tf_op jit(solution)/shard_map/pallas_call | solution.py:318
  11.1 0.3 shard_map.70.refs_8_
  11.4 4.2 %collective-permute-done.2.refs_5_ = f32[2,128,128]{2,1,0:T(8,128)S(1)} collective-permute-done((f32[2,128,128]{2,1,0:T(8,128)S(1)}, f32[2,128,128]{2,1,0:T(8,128)S(1)}, u32[]{:S(2)}, u32[]{:S(2)}) %collective-permute-start.2) | collective-permute-done | bytes 131104 | tf_op jit(solution)/shard_map/ppermute | solution.py:30
  15.6 1.0 %collective-permute-done.refs_3_ = f32[2,128,256]{2,1,0:T(8,128)S(1)} collective-permute-done((f32[2,128,256]{2,1,0:T(8,128)S(1)}, f32[2,128,256]{2,1,0:T(8,128)S(1)}, u32[]{:S(2)}, u32[]{:S(2)}) %collective-permute-start) | collective-permute-done | bytes 262176 | tf_op jit(solution)/shard_map/ppermute | solution.py:30
  16.5 1.7 %shard_map.71 = (f32[2,128,256]{2,1,0:T(8,128)S(1)}, f32[2,128,256]{2,1,0:T(8,128)S(1)}, f32[2,128,128]{2,1,0:T(8,128)S(1)}, f32[2,128,128]{2,1,0:T(8,128)S(1)}, f32[256,256]{1,0:T(8,128)S(1)}) custom-call(s32[3,128,128]{2,1,0:T(8,128)S(1)} %get-tuple-element.35.mask_ref.refs_0_, f32[2,256,128]{2,1,0:T(8,128)S(1)} %get-tuple-element.33.left_ref.refs_1_, ...), custom_call_target="tpu_custom_call" | custom-call | flops 1000000000 | bytes 1000000 | tf_op jit(solution)/shard_map/pallas_call | solution.py:333
  18.3 3.1 %collective-permute-start.3 = (f32[2,128,256]{2,1,0:T(8,128)S(1)}, f32[2,128,256]{2,1,0:T(8,128)S(1)}, u32[]{:S(2)}, u32[]{:S(2)}) collective-permute-start(f32[2,128,256]{2,1,0:T(8,128)S(1)} %get-tuple-element.47), channel_id=1, source_target_pairs={{0,8},{1,9},{2,10},{3,11},{4,12},{5,13},{6,14},{7,15},{8,16},{9,17... | collective-permute-start | bytes 786440 | tf_op jit(solution)/shard_map/ppermute | solution.py:30
  21.4 0.3 shard_map.72
  21.7 4.8 %collective-permute-start.4 = (f32[2,256,128]{2,1,0:T(8,128)S(1)}, f32[2,256,128]{2,1,0:T(8,128)S(1)}, u32[]{:S(2)}, u32[]{:S(2)}) collective-permute-start(f32[2,256,128]{2,1,0:T(8,128)S(1)} %get-tuple-element.48), channel_id=1, source_target_pairs={{0,1},{1,2},{2,3},{3,4},{4,5},{5,6},{6,7},{8,9},{9,10},{10,11},{11... | collective-permute-start | bytes 786440 | tf_op jit(solution)/shard_map/ppermute | solution.py:30
  26.5 1.9 %collective-permute-start.5 = (f32[2,128,128]{2,1,0:T(8,128)S(1)}, f32[2,128,128]{2,1,0:T(8,128)S(1)}, u32[]{:S(2)}, u32[]{:S(2)}) collective-permute-start(f32[2,128,128]{2,1,0:T(8,128)S(1)} %get-tuple-element.49), channel_id=1, source_target_pairs={{0,9},{1,10},{2,11},{3,12},{4,13},{5,14},{6,15},{8,17},{9,18},{10,... | collective-permute-start | bytes 393224 | tf_op jit(solution)/shard_map/ppermute | solution.py:30
  28.4 5.7 %collective-permute-done.5.diag_ref = f32[2,128,128]{2,1,0:T(8,128)S(1)} collective-permute-done((f32[2,128,128]{2,1,0:T(8,128)S(1)}, f32[2,128,128]{2,1,0:T(8,128)S(1)}, u32[]{:S(2)}, u32[]{:S(2)}) %collective-permute-start.5) | collective-permute-done | bytes 131104 | tf_op jit(solution)/shard_map/ppermute | solution.py:30
  34.1 0.1 shard_map.73
  34.3 1.9 %collective-permute-start.7 = (f32[2,256,128]{2,1,0:T(8,128)S(1)}, f32[2,256,128]{2,1,0:T(8,128)S(1)}, u32[]{:S(2)}, u32[]{:S(2)}) collective-permute-start(f32[2,256,128]{2,1,0:T(8,128)S(1)} %get-tuple-element.55), channel_id=1, source_target_pairs={{1,0},{2,1},{3,2},{4,3},{5,4},{6,5},{7,6},{9,8},{10,9},{11,10},{12... | collective-permute-start | bytes 786440 | tf_op jit(solution)/shard_map/ppermute | solution.py:30
  36.2 1.9 %collective-permute-start.6 = (f32[2,128,256]{2,1,0:T(8,128)S(1)}, f32[2,128,256]{2,1,0:T(8,128)S(1)}, u32[]{:S(2)}, u32[]{:S(2)}) collective-permute-start(f32[2,128,256]{2,1,0:T(8,128)S(1)} %get-tuple-element.54), channel_id=1, source_target_pairs={{8,0},{9,1},{10,2},{11,3},{12,4},{13,5},{14,6},{15,7},{16,8},{17,9... | collective-permute-start | bytes 786440 | tf_op jit(solution)/shard_map/ppermute | solution.py:30
  38.1 1.9 %collective-permute-start.8 = (f32[2,128,128]{2,1,0:T(8,128)S(1)}, f32[2,128,128]{2,1,0:T(8,128)S(1)}, u32[]{:S(2)}, u32[]{:S(2)}) collective-permute-start(f32[2,128,128]{2,1,0:T(8,128)S(1)} %get-tuple-element.56), channel_id=1, source_target_pairs={{9,0},{10,1},{11,2},{12,3},{13,4},{14,5},{15,6},{17,8},{18,9},{19,... | collective-permute-start | bytes 393224 | tf_op jit(solution)/shard_map/ppermute | solution.py:30
  40.0 2.2 %collective-permute-done.7.beside_ref.refs_4_ = f32[2,256,128]{2,1,0:T(8,128)S(1)} collective-permute-done((f32[2,256,128]{2,1,0:T(8,128)S(1)}, f32[2,256,128]{2,1,0:T(8,128)S(1)}, u32[]{:S(2)}, u32[]{:S(2)}) %collective-permute-start.7) | collective-permute-done | bytes 262176 | tf_op jit(solution)/shard_map/ppermute | solution.py:30
  42.2 0.3 shard_map.74.refs_8_
  42.5 4.5 %collective-permute-done.8.refs_5_ = f32[2,128,128]{2,1,0:T(8,128)S(1)} collective-permute-done((f32[2,128,128]{2,1,0:T(8,128)S(1)}, f32[2,128,128]{2,1,0:T(8,128)S(1)}, u32[]{:S(2)}, u32[]{:S(2)}) %collective-permute-start.8) | collective-permute-done | bytes 131104 | tf_op jit(solution)/shard_map/ppermute | solution.py:30
  47.0 1.4 %collective-permute-done.6.refs_3_ = f32[2,128,256]{2,1,0:T(8,128)S(1)} collective-permute-done((f32[2,128,256]{2,1,0:T(8,128)S(1)}, f32[2,128,256]{2,1,0:T(8,128)S(1)}, u32[]{:S(2)}, u32[]{:S(2)}) %collective-permute-start.6) | collective-permute-done | bytes 262176 | tf_op jit(solution)/shard_map/ppermute | solution.py:30
  48.4 1.7 %shard_map.75 = (f32[2,128,256]{2,1,0:T(8,128)S(1)}, f32[2,128,256]{2,1,0:T(8,128)S(1)}, f32[2,128,128]{2,1,0:T(8,128)S(1)}, f32[2,128,128]{2,1,0:T(8,128)S(1)}, f32[256,256]{1,0:T(8,128)S(1)}) custom-call(s32[3,128,128]{2,1,0:T(8,128)S(1)} %get-tuple-element.35.mask_ref.refs_0_, f32[2,256,128]{2,1,0:T(8,128)S(1)} %get-tuple-element.50.left_ref.refs_1_, ...), custom_call_target="tpu_custom_call" | custom-call | flops 1000000000 | bytes 1000000 | tf_op jit(solution)/shard_map/pallas_call | solution.py:333
  50.1 0.3 shard_map.76
  50.4 4.6 %collective-permute-start.10 = (f32[2,256,128]{2,1,0:T(8,128)S(1)}, f32[2,256,128]{2,1,0:T(8,128)S(1)}, u32[]{:S(2)}, u32[]{:S(2)}) collective-permute-start(f32[2,256,128]{2,1,0:T(8,128)S(1)} %get-tuple-element.62), channel_id=1, source_target_pairs={{0,1},{1,2},{2,3},{3,4},{4,5},{5,6},{6,7},{8,9},{9,10},{10,11},{11... | collective-permute-start | bytes 786440 | tf_op jit(solution)/shard_map/ppermute | solution.py:30
  55.0 2.1 %collective-permute-start.9 = (f32[2,128,256]{2,1,0:T(8,128)S(1)}, f32[2,128,256]{2,1,0:T(8,128)S(1)}, u32[]{:S(2)}, u32[]{:S(2)}) collective-permute-start(f32[2,128,256]{2,1,0:T(8,128)S(1)} %get-tuple-element.61), channel_id=1, source_target_pairs={{0,8},{1,9},{2,10},{3,11},{4,12},{5,13},{6,14},{7,15},{8,16},{9,17... | collective-permute-start | bytes 786440 | tf_op jit(solution)/shard_map/ppermute | solution.py:30
  57.1 1.9 %collective-permute-start.11 = (f32[2,128,128]{2,1,0:T(8,128)S(1)}, f32[2,128,128]{2,1,0:T(8,128)S(1)}, u32[]{:S(2)}, u32[]{:S(2)}) collective-permute-start(f32[2,128,128]{2,1,0:T(8,128)S(1)} %get-tuple-element.63), channel_id=1, source_target_pairs={{0,9},{1,10},{2,11},{3,12},{4,13},{5,14},{6,15},{8,17},{9,18},{10,... | collective-permute-start | bytes 393224 | tf_op jit(solution)/shard_map/ppermute | solution.py:30
  59.1 8.4 %collective-permute-done.11.diag_ref = f32[2,128,128]{2,1,0:T(8,128)S(1)} collective-permute-done((f32[2,128,128]{2,1,0:T(8,128)S(1)}, f32[2,128,128]{2,1,0:T(8,128)S(1)}, u32[]{:S(2)}, u32[]{:S(2)}) %collective-permute-start.11) | collective-permute-done | bytes 131104 | tf_op jit(solution)/shard_map/ppermute | solution.py:30
  67.5 1.1 %shard_map.77 = (f32[2,256,256]{2,1,0:T(8,128)}, f32[2,256,256]{2,1,0:T(8,128)}) custom-call(f32[2,256,128]{2,1,0:T(8,128)S(1)} %get-tuple-element.50.left_ref.refs_1_, f32[2,256,128]{2,1,0:T(8,128)S(1)} %get-tuple-element.51.right_ref.refs_2_, f32[2,256,128]{2,1,0:T(8,128)S(1)} %get-tuple-element.52.vl_ref, f32[2,256,128]{2,1,0:T(8,128)S(1)} %get-tuple-element.53.vr_ref, ...), custom_call_target="tpu_custom_call" | custom-call | flops 1000000 | bytes 1000000 | tf_op jit(solution)/shard_map/pallas_call | solution.py:381
  (13 shorter events, 0.1 us)
Async XLA Ops:
  0.6 1.0 %copy-start = (f32[2,256,256]{2,1,0:T(8,128)S(1)}, f32[2,256,256]{2,1,0:T(8,128)}, u32[]{:S(2)}) copy-start(f32[2,256,256]{2,1,0:T(8,128)} %obj_ref.1) | copy-start | bytes 1572868
  1.7 6.9 %copy-start.2 = (f32[2,256,256]{2,1,0:T(8,128)S(1)}, f32[2,256,256]{2,1,0:T(8,128)}, u32[]{:S(2)}) copy-start(f32[2,256,256]{2,1,0:T(8,128)} %probe_ref.1) | copy-start | bytes 1572868
  1.7 6.9 %copy-start.3 = (f32[1,1,1,256,256]{4,3,2,1,0:T(8,128)S(1)}, f32[1,1,1,256,256]{4,3,2,1,0:T(8,128)}, u32[]{:S(2)}) copy-start(f32[1,1,1,256,256]{4,3,2,1,0:T(8,128)} %param.8) | copy-start | bytes 786436
  1.7 9.4 %collective-permute-start.1 = (f32[2,256,128]{2,1,0:T(8,128)S(1)}, f32[2,256,128]{2,1,0:T(8,128)S(1)}, u32[]{:S(2)}, u32[]{:S(2)}) collective-permute-start(f32[2,256,128]{2,1,0:T(8,128)S(1)} %get-tuple-element.36), channel_id=1, source_target_pairs={{1,0},{2,1},{3,2},{4,3},{5,4},{6,5},{7,6},{9,8},{10,9},{11,10},{12... | collective-permute-start | bytes 786440 | tf_op jit(solution)/shard_map/ppermute | solution.py:30
  4.5 12.0 %collective-permute-start = (f32[2,128,256]{2,1,0:T(8,128)S(1)}, f32[2,128,256]{2,1,0:T(8,128)S(1)}, u32[]{:S(2)}, u32[]{:S(2)}) collective-permute-start(f32[2,128,256]{2,1,0:T(8,128)S(1)} %slice.3), channel_id=1, source_target_pairs={{8,0},{9,1},{10,2},{11,3},{12,4},{13,5},{14,6},{15,7},{16,8},{17,9... | collective-permute-start | bytes 786440 | tf_op jit(solution)/shard_map/ppermute | solution.py:30
  6.7 8.9 %collective-permute-start.2 = (f32[2,128,128]{2,1,0:T(8,128)S(1)}, f32[2,128,128]{2,1,0:T(8,128)S(1)}, u32[]{:S(2)}, u32[]{:S(2)}) collective-permute-start(f32[2,128,128]{2,1,0:T(8,128)S(1)} %get-tuple-element.37), channel_id=1, source_target_pairs={{9,0},{10,1},{11,2},{12,3},{13,4},{14,5},{15,6},{17,8},{18,9},{19,... | collective-permute-start | bytes 393224 | tf_op jit(solution)/shard_map/ppermute | solution.py:30
  8.6 0.7 copy-start.4
  18.3 15.8 %collective-permute-start.3 = (f32[2,128,256]{2,1,0:T(8,128)S(1)}, f32[2,128,256]{2,1,0:T(8,128)S(1)}, u32[]{:S(2)}, u32[]{:S(2)}) collective-permute-start(f32[2,128,256]{2,1,0:T(8,128)S(1)} %get-tuple-element.47), channel_id=1, source_target_pairs={{0,8},{1,9},{2,10},{3,11},{4,12},{5,13},{6,14},{7,15},{8,16},{9,17... | collective-permute-start | bytes 786440 | tf_op jit(solution)/shard_map/ppermute | solution.py:30
  21.3 12.8 %copy-start.1 = (f32[2,256,256]{2,1,0:T(8,128)S(1)}, f32[2,256,256]{2,1,0:T(8,128)}, u32[]{:S(2)}) copy-start(f32[2,256,256]{2,1,0:T(8,128)} %vel_ref.1) | copy-start | bytes 1572868
  21.7 12.4 %collective-permute-start.4 = (f32[2,256,128]{2,1,0:T(8,128)S(1)}, f32[2,256,128]{2,1,0:T(8,128)S(1)}, u32[]{:S(2)}, u32[]{:S(2)}) collective-permute-start(f32[2,256,128]{2,1,0:T(8,128)S(1)} %get-tuple-element.48), channel_id=1, source_target_pairs={{0,1},{1,2},{2,3},{3,4},{4,5},{5,6},{6,7},{8,9},{9,10},{10,11},{11... | collective-permute-start | bytes 786440 | tf_op jit(solution)/shard_map/ppermute | solution.py:30
  26.5 7.6 %collective-permute-start.5 = (f32[2,128,128]{2,1,0:T(8,128)S(1)}, f32[2,128,128]{2,1,0:T(8,128)S(1)}, u32[]{:S(2)}, u32[]{:S(2)}) collective-permute-start(f32[2,128,128]{2,1,0:T(8,128)S(1)} %get-tuple-element.49), channel_id=1, source_target_pairs={{0,9},{1,10},{2,11},{3,12},{4,13},{5,14},{6,15},{8,17},{9,18},{10,... | collective-permute-start | bytes 393224 | tf_op jit(solution)/shard_map/ppermute | solution.py:30
  34.3 8.0 %collective-permute-start.7 = (f32[2,256,128]{2,1,0:T(8,128)S(1)}, f32[2,256,128]{2,1,0:T(8,128)S(1)}, u32[]{:S(2)}, u32[]{:S(2)}) collective-permute-start(f32[2,256,128]{2,1,0:T(8,128)S(1)} %get-tuple-element.55), channel_id=1, source_target_pairs={{1,0},{2,1},{3,2},{4,3},{5,4},{6,5},{7,6},{9,8},{10,9},{11,10},{12... | collective-permute-start | bytes 786440 | tf_op jit(solution)/shard_map/ppermute | solution.py:30
  36.2 12.2 %collective-permute-start.6 = (f32[2,128,256]{2,1,0:T(8,128)S(1)}, f32[2,128,256]{2,1,0:T(8,128)S(1)}, u32[]{:S(2)}, u32[]{:S(2)}) collective-permute-start(f32[2,128,256]{2,1,0:T(8,128)S(1)} %get-tuple-element.54), channel_id=1, source_target_pairs={{8,0},{9,1},{10,2},{11,3},{12,4},{13,5},{14,6},{15,7},{16,8},{17,9... | collective-permute-start | bytes 786440 | tf_op jit(solution)/shard_map/ppermute | solution.py:30
  38.1 8.9 %collective-permute-start.8 = (f32[2,128,128]{2,1,0:T(8,128)S(1)}, f32[2,128,128]{2,1,0:T(8,128)S(1)}, u32[]{:S(2)}, u32[]{:S(2)}) collective-permute-start(f32[2,128,128]{2,1,0:T(8,128)S(1)} %get-tuple-element.56), channel_id=1, source_target_pairs={{9,0},{10,1},{11,2},{12,3},{13,4},{14,5},{15,6},{17,8},{18,9},{19,... | collective-permute-start | bytes 393224 | tf_op jit(solution)/shard_map/ppermute | solution.py:30
  50.4 17.1 %collective-permute-start.10 = (f32[2,256,128]{2,1,0:T(8,128)S(1)}, f32[2,256,128]{2,1,0:T(8,128)S(1)}, u32[]{:S(2)}, u32[]{:S(2)}) collective-permute-start(f32[2,256,128]{2,1,0:T(8,128)S(1)} %get-tuple-element.62), channel_id=1, source_target_pairs={{0,1},{1,2},{2,3},{3,4},{4,5},{5,6},{6,7},{8,9},{9,10},{10,11},{11... | collective-permute-start | bytes 786440 | tf_op jit(solution)/shard_map/ppermute | solution.py:30
  55.0 12.5 %collective-permute-start.9 = (f32[2,128,256]{2,1,0:T(8,128)S(1)}, f32[2,128,256]{2,1,0:T(8,128)S(1)}, u32[]{:S(2)}, u32[]{:S(2)}) collective-permute-start(f32[2,128,256]{2,1,0:T(8,128)S(1)} %get-tuple-element.61), channel_id=1, source_target_pairs={{0,8},{1,9},{2,10},{3,11},{4,12},{5,13},{6,14},{7,15},{8,16},{9,17... | collective-permute-start | bytes 786440 | tf_op jit(solution)/shard_map/ppermute | solution.py:30
  57.1 10.4 %collective-permute-start.11 = (f32[2,128,128]{2,1,0:T(8,128)S(1)}, f32[2,128,128]{2,1,0:T(8,128)S(1)}, u32[]{:S(2)}, u32[]{:S(2)}) collective-permute-start(f32[2,128,128]{2,1,0:T(8,128)S(1)} %get-tuple-element.63), channel_id=1, source_target_pairs={{0,9},{1,10},{2,11},{3,12},{4,13},{5,14},{6,15},{8,17},{9,18},{10,... | collective-permute-start | bytes 393224 | tf_op jit(solution)/shard_map/ppermute | solution.py:30

commit v3 on v2

v3 whole, which is shorter than its diff:
```python
import math

import jax
import jax.numpy as jnp
from jax import lax
from jax.experimental import pallas as pl
from jax.experimental.pallas import tpu as pltpu
from jax.sharding import PartitionSpec as P


P_SIZE = 256

step_size = 0.1
momentum_rate = 0.8

VMEM = pl.BlockSpec(memory_space=pltpu.VMEM)
SMEM = pl.BlockSpec(memory_space=pltpu.SMEM)
N = P_SIZE
H = P_SIZE // 2


def shifted(value, row_steps, col_steps):
    rows, cols = lax.axis_size("row"), lax.axis_size("col")
    pairs = []
    for r in range(rows):
        for c in range(cols):
            to_r, to_c = r + row_steps, c + col_steps
            if 0 <= to_r < rows and 0 <= to_c < cols:
                pairs.append((r * cols + c, to_r * cols + to_c))
    return lax.ppermute(value, ("row", "col"), pairs)


def turns(step, length, scale):
    step = jnp.where(step > length // 2, step - length, step)
    angle = step.astype(jnp.float32) * (-2.0 * math.pi / length)
    return jnp.cos(angle) * scale, jnp.sin(angle) * scale


def halves(x):
    high = x.astype(jnp.bfloat16)
    return high, (x - high.astype(jnp.float32)).astype(jnp.bfloat16)


def dot(a, b):
    return jnp.dot(a, b, preferred_element_type=jnp.float32)


def times(a, b):
    return dot(a[0], b[0]) + dot(a[0], b[1]) + dot(a[1], b[0])


def quads(q00, q01, q10, q11):
    return jnp.concatenate(
        [jnp.concatenate([q00, q01], axis=1), jnp.concatenate([q10, q11], axis=1)], axis=0
    )


def block_transpose(x):
    return quads(x[:H, :H], x[H:, :H], x[:H, H:], x[H:, H:])


def plus(table_ref):
    return table_ref[0], table_ref[1]


def minus(table_ref):
    return table_ref[2], table_ref[3]


def unpack_kernel(obj_ref, left_out, right_out, q00_out, send_out):
    for part in range(2):
        left_out[part] = obj_ref[part, :, :H]
        send_out[part] = obj_ref[part, :, :H]
        right_out[part] = obj_ref[part, :, H:]
        q00_out[part] = obj_ref[part, :H, :H]


def prep_kernel(
    pos_ref, below_ref, beside_ref, probe_ref, meas_ref, probe_out, meas_out, mask_out, table_out, cols_out, rows_out
):
    p0 = pos_ref[0]
    p1 = pos_ref[1]
    row_id = lax.broadcasted_iota(jnp.int32, (H, H), 0)
    col_id = lax.broadcasted_iota(jnp.int32, (H, H), 1)
    mask_out[0] = jnp.where(row_id < p0, 1, 0)
    mask_out[1] = jnp.where(col_id < p1, 1, 0)
    mask_out[2] = jnp.full((H, H), below_ref[0], jnp.int32)
    mask_out[3] = jnp.full((H, H), beside_ref[0], jnp.int32)
    c, s = turns(row_id * col_id & (H - 1), H, 1.0 / math.sqrt(P_SIZE))
    for number, block in enumerate((quads(c, s, -s, c), quads(c, -s, s, c))):
        table_out[2 * number], table_out[2 * number + 1] = halves(block)
    rows_out[0], rows_out[1] = turns(row_id, P_SIZE, 1.0)
    cols_out[0], cols_out[1] = turns(col_id[:8], P_SIZE, 1.0)
    for part in range(2):
        x = pltpu.roll(probe_ref[part], p0, 0)
        probe_out[part] = pltpu.roll(x, p1, 1)
    first = lax.broadcasted_iota(jnp.int32, (N, N), 0)
    second = lax.broadcasted_iota(jnp.int32, (N, N), 1)

    def evens_first(place):
        return jnp.where(place < H, 2 * place, 2 * (place - H) + 1)

    def moved(x, move):
        high, rest = halves(x)
        mid = x - high.astype(jnp.float32)
        low = (mid - rest.astype(jnp.float32)).astype(jnp.bfloat16)
        return move(high) + (move(rest) + move(low))

    rows_move = jnp.where(second == evens_first(first), 1.0, 0.0).astype(jnp.bfloat16)
    cols_move = jnp.where(first == evens_first(second), 1.0, 0.0).astype(jnp.bfloat16)
    x = moved(meas_ref[...], lambda part: dot(rows_move, part))
    meas_out[...] = moved(x, lambda part: dot(part, cols_move))


def row_stage(patch, pr, pi, table, w_ref):
    er = pr * patch[0] - pi * patch[1]
    ei = pr * patch[1] + pi * patch[0]
    wr, wi = w_ref[0, 0:1], w_ref[1, 0:1]
    dr, di = er[:, :H] - er[:, H:], ei[:, :H] - ei[:, H:]
    x = quads(
        er[:, :H] + er[:, H:], ei[:, :H] + ei[:, H:], dr * wr - di * wi, dr * wi + di * wr
    )
    return times(halves(x), table)


def back_stage(x, pr, pi, table, w_ref):
    y = times(halves(block_transpose(x)), table)
    wr, wi = w_ref[0, 0:1], w_ref[1, 0:1]
    qr, qi = y[H:, :H], y[H:, H:]
    tr, ti = qr * wr + qi * wi, qi * wr - qr * wi
    br = jnp.concatenate([y[:H, :H] + tr, y[:H, :H] - tr], axis=1)
    bi = jnp.concatenate([y[:H, H:] + ti, y[:H, H:] - ti], axis=1)
    return pr * br + pi * bi, pr * bi - pi * br


def masks(mask_ref):
    return mask_ref[0] > 0, mask_ref[1] > 0


def pre_kernel(mask_ref, left_ref, right_ref, beside_ref, probe_ref, table_ref, cols_ref, y_ref):
    _, beyond = masks(mask_ref)
    patch = [
        jnp.concatenate(
            [jnp.where(beyond, beside_ref[part, H:], left_ref[part, H:]), right_ref[part, H:]], axis=1
        )
        for part in range(2)
    ]
    y_ref[...] = row_stage(patch, probe_ref[0, H:], probe_ref[1, H:], plus(table_ref), cols_ref)


def main_kernel(first, *refs):
    if first:
        (mask_ref, left_ref, right_ref, lower_ref, beside_ref, corner_ref, probe_ref, meas_ref, yb_ref,
         table_ref, cols_ref, rows_ref, own_out, down_out, diag_out, r00_out, xb_out, kept_out) = refs
    else:
        (mask_ref, left_ref, right_ref, up00_ref, up01_ref, kept_ref, fix_ref, diag_ref, beside_ref, corner_ref,
         probe_ref, meas_ref, yb_ref, table_ref, cols_ref, rows_ref,
         own_out, down_out, diag_out, r00_out, xb_out) = refs
        kept_scale = mask_ref[2].astype(jnp.float32) * step_size
        corner_scale = kept_scale * mask_ref[3].astype(jnp.float32)
    below, beyond = masks(mask_ref)
    pr, pi = probe_ref[0, :H], probe_ref[1, :H]
    patch = []
    for part in range(2):
        own00, beside = left_ref[part, :H], beside_ref[part, :H]
        if first:
            lower00, lower01, corner = lower_ref[part, :, :H], lower_ref[part, :, H:], corner_ref[part]
        else:
            own00 = own00 - step_size * diag_ref[part]
            beside = beside - fix_ref[part, :, H:]
            lower00 = up00_ref[part] - fix_ref[part, :, :H]
            lower01 = up01_ref[part] - kept_scale * kept_ref[part, :, H:]
            corner = corner_ref[part] - corner_scale * kept_ref[part, :, :H]
        q00 = jnp.where(below, jnp.where(beyond, corner, lower00), jnp.where(beyond, beside, own00))
        q01 = jnp.where(below, lower01, right_ref[part, :H])
        patch.append(jnp.concatenate([q00, q01], axis=1))
    yt = row_stage(patch, pr, pi, plus(table_ref), cols_ref)
    yb = yb_ref[...]
    wr = jnp.concatenate([rows_ref[0], rows_ref[0]], axis=0)
    wi = jnp.concatenate([rows_ref[1], rows_ref[1]], axis=0)
    diff = yt - yb
    dr, di = diff[:, :H], diff[:, H:]
    odd = jnp.concatenate([dr * wr - di * wi, dr * wi + di * wr], axis=1)
    back = []
    for parity, x in enumerate((yt + yb, odd)):
        z = times(minus(table_ref), halves(block_transpose(x)))
        zr, zi = z[:H], z[H:]
        misfit = zr * zr + zi * zi - meas_ref[parity * H : (parity + 1) * H]
        g = jnp.concatenate([misfit * zr, misfit * zi], axis=0)
        back.append(times(plus(table_ref), halves(g)))
    qr, qi = back[1][:H], back[1][H:]
    wr = jnp.concatenate([rows_ref[0], rows_ref[0]], axis=1)
    wi = jnp.concatenate([rows_ref[1], rows_ref[1]], axis=1)
    turned = jnp.concatenate([qr * wr + qi * wi, qi * wr - qr * wi], axis=0)
    xb_out[...] = back[0] - turned
    out = back_stage(back[0] + turned, pr, pi, minus(table_ref), cols_ref)
    for part in range(2):
        g00, g01 = out[part][:, :H], out[part][:, H:]
        own_out[part, :, :H] = jnp.where(jnp.logical_or(below, beyond), 0.0, g00)
        own_out[part, :, H:] = jnp.where(below, 0.0, g01)
        d01 = jnp.where(below, g01, 0.0)
        diag = jnp.where(jnp.logical_and(below, beyond), g00, 0.0)
        diag_out[part] = diag
        if first:
            down_out[part * H : (part + 1) * H, :H] = jnp.where(below, g00, 0.0)
            down_out[part * H : (part + 1) * H, H:] = d01
            r00_out[part] = jnp.where(beyond, g00, 0.0)
            kept_out[part, :, :H] = diag
            kept_out[part, :, H:] = d01
        else:
            down_out[part, :, :H] = jnp.where(jnp.logical_and(below, ~beyond), g00, 0.0)
            down_out[part, :, H:] = d01
            r00_out[part] = jnp.where(jnp.logical_and(~below, beyond), g00, 0.0)
    if first:
        down_out[2 * H :, :H] = mask_ref[1, :8].astype(jnp.float32)
        down_out[2 * H :, H:] = jnp.zeros((8, H), jnp.float32)


def post_kernel(first, mask_ref, xb_ref, r00_ref, probe_ref, table_ref, cols_ref, own_out, right_out):
    below, beyond = masks(mask_ref)
    out = back_stage(xb_ref[...], probe_ref[0, H:], probe_ref[1, H:], minus(table_ref), cols_ref)
    for part in range(2):
        g10, g11 = out[part][:, :H], out[part][:, H:]
        own_out[part, :, :H] = jnp.where(beyond, 0.0, g10)
        own_out[part, :, H:] = g11
        r10 = jnp.where(beyond, g10, 0.0)
        if first:
            right_out[part * N : part * N + H] = r00_ref[part]
            right_out[part * N + H : (part + 1) * N] = r10
        else:
            right_out[part, :H] = r00_ref[part]
            right_out[part, H:] = r10
    if first:
        rows = jnp.sum(below.astype(jnp.float32), axis=0, keepdims=True)
        right_out[2 * N :] = jnp.broadcast_to(rows, (8, H))


def stepped(obj, vel, g):
    vel = momentum_rate * vel + g
    return obj - step_size * vel, vel


def ahead_kernel(right_ref, vel_ref, own_ref, up_out):
    for part in range(2):
        up_out[part], _ = stepped(right_ref[part, :H], vel_ref[part, :H, H:], own_ref[part, :, H:])


def update_kernel(
    mask_ref, left_ref, right_ref, vel_ref, top_ref, bottom_ref, above_ref, before_ref,
    left_out, right_out, vl_out, vr_out, up_out, corner_out, send_out, fix_out,
):
    row_id = lax.broadcasted_iota(jnp.int32, (H, H), 0).astype(jnp.float32)
    ours_above = above_ref[2 * H : 2 * H + 1, :H] < 0.5
    ours_before = row_id >= before_ref[2 * N : 2 * N + 1]
    for part in range(2):
        above, before = above_ref[part * H : (part + 1) * H], before_ref[part * N : (part + 1) * N]
        g00 = (top_ref[part, :, :H] + jnp.where(ours_above, above[:, :H], 0.0)) + jnp.where(ours_before, before[:H], 0.0)
        g01 = top_ref[part, :, H:] + above[:, H:]
        g10 = bottom_ref[part, :, :H] + before[H:]
        g11 = bottom_ref[part, :, H:]
        obj, vel = stepped(left_ref[part, :H], vel_ref[part, :H, :H], g00)
        left_out[part, :H], vl_out[part, :H] = obj, vel
        up_out[part], corner_out[part], send_out[part, :H] = obj, obj, obj
        right_out[part, :H], vr_out[part, :H] = stepped(right_ref[part, :H], vel_ref[part, :H, H:], g01)
        obj, vel = stepped(left_ref[part, H:], vel_ref[part, H:, :H], g10)
        left_out[part, H:], vl_out[part, H:], send_out[part, H:] = obj, vel, obj
        right_out[part, H:], vr_out[part, H:] = stepped(right_ref[part, H:], vel_ref[part, H:, H:], g11)
        scale = mask_ref[2].astype(jnp.float32) * step_size
        fix_out[part, :, :H] = scale * jnp.where(ours_before, 0.0, before[:H])
        scale = mask_ref[3].astype(jnp.float32) * step_size
        fix_out[part, :, H:] = scale * jnp.where(ours_above, 0.0, above[:, :H])


def final_kernel(
    left_ref, right_ref, vl_ref, vr_ref, late_ref, top_ref, bottom_ref, above_ref, before_ref, diag_ref, obj_out, vel_out
):
    for part in range(2):
        g00 = (top_ref[part, :, :H] + above_ref[part, :, :H]) + (before_ref[part, :H] + diag_ref[part])
        g01 = top_ref[part, :, H:] + above_ref[part, :, H:]
        g10 = bottom_ref[part, :, :H] + before_ref[part, H:]
        g11 = bottom_ref[part, :, H:]
        obj = left_ref[part, :H] - step_size * late_ref[part]
        obj_out[part, :H, :H], vel_out[part, :H, :H] = stepped(obj, vl_ref[part, :H] + late_ref[part], g00)
        obj_out[part, H:, :H], vel_out[part, H:, :H] = stepped(left_ref[part, H:], vl_ref[part, H:], g10)
        for rows, g in ((slice(0, H), g01), (slice(H, N), g11)):
            obj_out[part, rows, H:], vel_out[part, rows, H:] = stepped(right_ref[part, rows], vr_ref[part, rows], g)


def shape(*dims, dtype=jnp.float32):
    return jax.ShapeDtypeStruct(dims, dtype)


def kernel(body, flops, scalars, arrays, outs):
    return pl.pallas_call(
        body,
        out_shape=outs,
        in_specs=[SMEM] * scalars + [VMEM] * arrays,
        out_specs=(VMEM,) * len(outs),
        compiler_params=pltpu.CompilerParams(vmem_limit_bytes=16 * 1024 * 1024),
        cost_estimate=pl.CostEstimate(flops=flops, bytes_accessed=10**6, transcendentals=0),
    )


def steps(object_field, velocity, positions, measured, probe):
    offsets = positions[0, 0, 0]
    intensity = measured[0, 0, 0]
    edges = [
        (lax.axis_index(axis) < lax.axis_size(axis) - 1).astype(jnp.int32).reshape(1) for axis in ("row", "col")
    ]
    half, strip, quad, rows = shape(2, N, H), shape(2, H, N), shape(2, H, H), shape(N, N)

    lower = shifted(object_field[:, :H, :], -1, 0)
    left, right, q00, left_send = kernel(unpack_kernel, 10**6, 0, 1, (half, half, quad, half))(object_field)
    beside = shifted(left_send, 0, -1)
    corner = shifted(q00, -1, -1)
    turned, intensity, mask, tables, along_cols, along_rows = kernel(
        prep_kernel, 10**8, 3, 2,
        (
            shape(2, N, N), rows, shape(4, H, H, dtype=jnp.int32),
            shape(4, N, N, dtype=jnp.bfloat16), shape(2, 8, H), shape(2, H, H),
        ),
    )(offsets, *edges, probe, intensity)

    def pre(left, right, beside):
        return kernel(pre_kernel, 10**8, 0, 7, (rows,))(
            mask, left, right, beside, turned, tables, along_cols
        )[0]

    def main(body, outs, *arrays):
        rest = (turned, intensity, pre(arrays[0], arrays[1], arrays[-2]), tables, along_cols, along_rows)
        return kernel(body, 10**9, 0, 1 + len(arrays) + len(rest), outs)(mask, *arrays, *rest)

    def post(first, sent, xb, r00):
        return kernel(lambda *refs: post_kernel(first, *refs), 10**8, 0, 6, (strip, sent))(
            mask, xb, r00, turned, tables, along_cols
        )

    top, down, diag, r00, xb, kept = main(
        lambda *refs: main_kernel(True, *refs), (strip, shape(N + 8, N), quad, quad, rows, strip),
        left, right, lower, beside, corner,
    )
    above = shifted(down, 1, 0)
    bottom, right_part = post(True, shape(2 * N + 8, H), xb, r00)
    before = shifted(right_part, 0, 1)
    late = shifted(diag, 1, 1)
    (ahead,) = kernel(ahead_kernel, 10**6, 0, 3, (quad,))(right, velocity, top)
    up01 = shifted(ahead, -1, 0)
    left, right, vel_left, vel_right, q00, q00_corner, left_send, fix = kernel(
        update_kernel, 10**6, 0, 8, (half, half, half, half, quad, quad, half, strip)
    )(mask, left, right, velocity, top, bottom, above, before)
    up00 = shifted(q00, -1, 0)
    corner = shifted(q00_corner, -1, -1)
    beside = shifted(left_send, 0, -1)
    top, down, diag, r00, xb = main(
        lambda *refs: main_kernel(False, *refs), (strip, strip, quad, quad, rows),
        left, right, up00, up01, kept, fix, late, beside, corner,
    )
    above = shifted(down, 1, 0)
    bottom, right_part = post(False, half, xb, r00)
    before = shifted(right_part, 0, 1)
    from_corner = shifted(diag, 1, 1)
    return kernel(final_kernel, 10**6, 0, 10, (shape(2, N, N), shape(2, N, N)))(
        left, right, vel_left, vel_right, late, top, bottom, above, before, from_corner
    )


def solution(mesh):
    placed = (
        P(None, "row", "col"),
        P(None, "row", "col"),
        P("row", "col", None, None),
        P("row", "col", None, None, None),
        P(),
    )
    return jax.shard_map(
        steps,
        mesh=mesh,
        in_specs=placed,
        out_specs=(P(None, "row", "col"), P(None, "row", "col")),
        check_vma=False,
    )
```

time: 69.1 us -> 71.2 us (1.030); the launches traced: 68.7 us -> 70 us
  starting transfers between devices: 31 us -> 37.3 us
  waiting for transfers between devices: 27.3 us -> 22.1 us
    ppermute x12 -> x13, starting transfers between devices: 31 us -> 37.3 us  [shifted(): return lax.ppermute(value, ('row', 'col'), pairs)]
    ppermute x12 -> x13, waiting for transfers between devices: 27.3 us -> 22.1 us  [shifted(): return lax.ppermute(value, ('row', 'col'), pairs)]
    pallas_call x5 -> x6, Pallas kernels: 3.75 us -> 3.84 us  [the longest x1 1.85 us: steps(): kernel(prep_kernel, 10 ** 8, 3, 2, (shape(2, N, N), rows, shape(4, H, H,...]
  transfers between devices with their start and end apart: 12 -> 13, of which waited for: 7 -> 6; matrix products, arithmetic and copies ran while one was open for 0% -> 0% of each run, Pallas kernels for 4% -> 4%
where the time goes in v3:
time: 71.2 us; the launch traced here: 70 us
  starting transfers between devices  37.3 us (52%)
  waiting for transfers between devices  22.1 us (31%)
  Pallas kernels  7.93 us (11%)
  local copies, waits for them, and re-layouts  1.7 us (2%)
  between operations  0.89 us (1%)
    ppermute x13, starting transfers between devices, shifted(): return lax.ppermute(value, ('row', 'col'), pairs)  37.3 us
    ppermute x13, waiting for transfers between devices, shifted(): return lax.ppermute(value, ('row', 'col'), pairs)  22.1 us
    pallas_call x2, Pallas kernels, main(): kernel(body, 10 ** 9, 0, 1 + len(arrays) + len(rest), outs)  3.46 us
    pallas_call x1, Pallas kernels, steps(): kernel(prep_kernel, 10 ** 8, 3, 2, (shape(2, N, N), rows, shape(4, H, H,...  1.85 us
    unnamed x10, local copies, waits for them, and re-layouts  1.68 us
  transfers between devices with their start and end apart: 13, of which 6 were waited for; matrix products, arithmetic and copies ran while one was open for 0% of the time, Pallas kernels for 4%

profile of v3, /device:TPU:11, one launch (start us, length us, event | category | flops | bytes accessed | tf_op | source)
XLA Modules:
  0.0 70.0 jit_solution(14751696879671031966)
XLA Ops:
  0.6 1.0 %copy-done.1 = f32[2,256,256]{2,1,0:T(8,128)S(1)} copy-done((f32[2,256,256]{2,1,0:T(8,128)S(1)}, f32[2,256,256]{2,1,0:T(8,128)}, u32[]{:S(2)}) %copy-start.1) | copy-done | bytes 524312
  1.7 0.1 shard_map.69
  1.7 0.0 copy-start.3
  1.7 2.7 %collective-permute-start.1 = (f32[2,256,128]{2,1,0:T(8,128)S(1)}, f32[2,256,128]{2,1,0:T(8,128)S(1)}, u32[]{:S(2)}, u32[]{:S(2)}) collective-permute-start(f32[2,256,128]{2,1,0:T(8,128)S(1)} %get-tuple-element.38), channel_id=1, source_target_pairs={{1,0},{2,1},{3,2},{4,3},{5,4},{6,5},{7,6},{9,8},{10,9},{11,10},{12... | collective-permute-start | bytes 786440 | tf_op jit(solution)/shard_map/ppermute | solution.py:30
  4.5 2.2 %collective-permute-start = (f32[2,128,256]{2,1,0:T(8,128)S(1)}, f32[2,128,256]{2,1,0:T(8,128)S(1)}, u32[]{:S(2)}, u32[]{:S(2)}) collective-permute-start(f32[2,128,256]{2,1,0:T(8,128)S(1)} %slice.3), channel_id=1, source_target_pairs={{8,0},{9,1},{10,2},{11,3},{12,4},{13,5},{14,6},{15,7},{16,8},{17,9... | collective-permute-start | bytes 786440 | tf_op jit(solution)/shard_map/ppermute | solution.py:30
  6.7 1.9 %collective-permute-start.2 = (f32[2,128,128]{2,1,0:T(8,128)S(1)}, f32[2,128,128]{2,1,0:T(8,128)S(1)}, u32[]{:S(2)}, u32[]{:S(2)}) collective-permute-start(f32[2,128,128]{2,1,0:T(8,128)S(1)} %get-tuple-element.39), channel_id=1, source_target_pairs={{9,0},{10,1},{11,2},{12,3},{13,4},{14,5},{15,6},{17,8},{18,9},{19,... | collective-permute-start | bytes 393224 | tf_op jit(solution)/shard_map/ppermute | solution.py:30
  8.6 0.6 copy-done.4
  9.3 1.9 %shard_map.68 = (f32[2,256,256]{2,1,0:T(8,128)S(1)}, f32[256,256]{1,0:T(8,128)S(1)}, s32[4,128,128]{2,1,0:T(8,128)S(1)}, bf16[4,256,256]{2,1,0:T(8,128)(2,1)S(1)...) custom-call(s32[2]{0:T(128)S(1)} %bitcast.5, s32[1]{0:T(128)} %bitcast.1.below_ref, s32[1]{0:T(128)} %bitcast.2.beside_ref, ...), custom_call_target="tpu_custom_call" | custom-call | flops 100000000 | bytes 1000000 | tf_op jit(solution)/shard_map/pallas_call | solution.py:316
  11.1 0.3 shard_map.70.refs_8_
  11.4 4.2 %collective-permute-done.2.refs_5_ = f32[2,128,128]{2,1,0:T(8,128)S(1)} collective-permute-done((f32[2,128,128]{2,1,0:T(8,128)S(1)}, f32[2,128,128]{2,1,0:T(8,128)S(1)}, u32[]{:S(2)}, u32[]{:S(2)}) %collective-permute-start.2) | collective-permute-done | bytes 131104 | tf_op jit(solution)/shard_map/ppermute | solution.py:30
  15.6 1.0 %collective-permute-done.refs_3_ = f32[2,128,256]{2,1,0:T(8,128)S(1)} collective-permute-done((f32[2,128,256]{2,1,0:T(8,128)S(1)}, f32[2,128,256]{2,1,0:T(8,128)S(1)}, u32[]{:S(2)}, u32[]{:S(2)}) %collective-permute-start) | collective-permute-done | bytes 262176 | tf_op jit(solution)/shard_map/ppermute | solution.py:30
  16.5 1.7 %shard_map.71 = (f32[2,128,256]{2,1,0:T(8,128)S(1)}, f32[264,256]{1,0:T(8,128)S(1)}, f32[2,128,128]{2,1,0:T(8,128)S(1)}, f32[2,128,128]{2,1,0:T(8,128)S(1)}, f32...) custom-call(s32[4,128,128]{2,1,0:T(8,128)S(1)} %get-tuple-element.35.mask_ref.refs_0_, ...), custom_call_target="tpu_custom_call" | custom-call | flops 1000000000 | bytes 1000000 | tf_op jit(solution)/shard_map/pallas_call | solution.py:331
  18.3 3.1 %collective-permute-start.3 = (f32[264,256]{1,0:T(8,128)S(1)}, f32[264,256]{1,0:T(8,128)S(1)}, u32[]{:S(2)}, u32[]{:S(2)}) collective-permute-start(f32[264,256]{1,0:T(8,128)S(1)} %get-tuple-element.49), channel_id=1, source_target_pairs={{0,8},{1,9},{2,10},{3,11},{4,12},{5,13},{6,14},{7,15},{8,16},{9,17... | collective-permute-start | bytes 811016 | tf_op jit(solution)/shard_map/ppermute | solution.py:30
  21.3 0.3 shard_map.72
  21.7 4.8 %collective-permute-start.4 = (f32[520,128]{1,0:T(8,128)S(1)}, f32[520,128]{1,0:T(8,128)S(1)}, u32[]{:S(2)}, u32[]{:S(2)}) collective-permute-start(f32[520,128]{1,0:T(8,128)S(1)} %get-tuple-element.50), channel_id=1, source_target_pairs={{0,1},{1,2},{2,3},{3,4},{4,5},{5,6},{6,7},{8,9},{9,10},{10,11},{11... | collective-permute-start | bytes 798728 | tf_op jit(solution)/shard_map/ppermute | solution.py:30
  26.5 3.3 %collective-permute-done.4.before_ref = f32[520,128]{1,0:T(8,128)S(1)} collective-permute-done((f32[520,128]{1,0:T(8,128)S(1)}, f32[520,128]{1,0:T(8,128)S(1)}, u32[]{:S(2)}, u32[]{:S(2)}) %collective-permute-start.4) | collective-permute-done | bytes 266272 | tf_op jit(solution)/shard_map/ppermute | solution.py:30
  29.8 0.2 shard_map.73
  30.0 3.2 %collective-permute-start.8 = (f32[2,256,128]{2,1,0:T(8,128)S(1)}, f32[2,256,128]{2,1,0:T(8,128)S(1)}, u32[]{:S(2)}, u32[]{:S(2)}) collective-permute-start(f32[2,256,128]{2,1,0:T(8,128)S(1)} %get-tuple-element.59), channel_id=1, source_target_pairs={{1,0},{2,1},{3,2},{4,3},{5,4},{6,5},{7,6},{9,8},{10,9},{11,10},{12... | collective-permute-start | bytes 786440 | tf_op jit(solution)/shard_map/ppermute | solution.py:30
  33.3 3.1 %collective-permute-start.7 = (f32[2,128,128]{2,1,0:T(8,128)S(1)}, f32[2,128,128]{2,1,0:T(8,128)S(1)}, u32[]{:S(2)}, u32[]{:S(2)}) collective-permute-start(f32[2,128,128]{2,1,0:T(8,128)S(1)} %shard_map.74), channel_id=1, source_target_pairs={{8,0},{9,1},{10,2},{11,3},{12,4},{13,5},{14,6},{15,7},{16,8},{17,9... | collective-permute-start | bytes 393224 | tf_op jit(solution)/shard_map/ppermute | solution.py:30
  36.4 4.3 %collective-permute-start.5 = (f32[2,128,128]{2,1,0:T(8,128)S(1)}, f32[2,128,128]{2,1,0:T(8,128)S(1)}, u32[]{:S(2)}, u32[]{:S(2)}) collective-permute-start(f32[2,128,128]{2,1,0:T(8,128)S(1)} %get-tuple-element.55), channel_id=1, source_target_pairs={{0,9},{1,10},{2,11},{3,12},{4,13},{5,14},{6,15},{8,17},{9,18},{10,... | collective-permute-start | bytes 393224 | tf_op jit(solution)/shard_map/ppermute | solution.py:30
  40.7 2.2 %collective-permute-start.6 = (f32[2,128,128]{2,1,0:T(8,128)S(1)}, f32[2,128,128]{2,1,0:T(8,128)S(1)}, u32[]{:S(2)}, u32[]{:S(2)}) collective-permute-start(f32[2,128,128]{2,1,0:T(8,128)S(1)} %get-tuple-element.56), channel_id=1, source_target_pairs={{8,0},{9,1},{10,2},{11,3},{12,4},{13,5},{14,6},{15,7},{16,8},{17,9... | collective-permute-start | bytes 393224 | tf_op jit(solution)/shard_map/ppermute | solution.py:30
  42.8 1.9 %collective-permute-start.9 = (f32[2,128,128]{2,1,0:T(8,128)S(1)}, f32[2,128,128]{2,1,0:T(8,128)S(1)}, u32[]{:S(2)}, u32[]{:S(2)}) collective-permute-start(f32[2,128,128]{2,1,0:T(8,128)S(1)} %get-tuple-element.60), channel_id=1, source_target_pairs={{9,0},{10,1},{11,2},{12,3},{13,4},{14,5},{15,6},{17,8},{18,9},{19,... | collective-permute-start | bytes 393224 | tf_op jit(solution)/shard_map/ppermute | solution.py:30
  44.8 0.3 shard_map.75.refs_12_
  45.1 3.2 %collective-permute-done.6.refs_3_ = f32[2,128,128]{2,1,0:T(8,128)S(1)} collective-permute-done((f32[2,128,128]{2,1,0:T(8,128)S(1)}, f32[2,128,128]{2,1,0:T(8,128)S(1)}, u32[]{:S(2)}, u32[]{:S(2)}) %collective-permute-start.6) | collective-permute-done | bytes 131104 | tf_op jit(solution)/shard_map/ppermute | solution.py:30
  48.3 2.7 %collective-permute-done.9.refs_9_ = f32[2,128,128]{2,1,0:T(8,128)S(1)} collective-permute-done((f32[2,128,128]{2,1,0:T(8,128)S(1)}, f32[2,128,128]{2,1,0:T(8,128)S(1)}, u32[]{:S(2)}, u32[]{:S(2)}) %collective-permute-start.9) | collective-permute-done | bytes 131104 | tf_op jit(solution)/shard_map/ppermute | solution.py:30
  51.0 1.8 %shard_map.76 = (f32[2,128,256]{2,1,0:T(8,128)S(1)}, f32[2,128,256]{2,1,0:T(8,128)S(1)}, f32[2,128,128]{2,1,0:T(8,128)S(1)}, f32[2,128,128]{2,1,0:T(8,128)S(1)}, f32[256,256]{1,0:T(8,128)S(1)}) custom-call(s32[4,128,128]{2,1,0:T(8,128)S(1)} %get-tuple-element.35.mask_ref.refs_0_, f32[2,256,128]{2,1,0:T(8,128)S(1)} %get-tuple-element.51.left_ref.refs_1_, ...), custom_call_target="tpu_custom_call" | custom-call | flops 1000000000 | bytes 1000000 | tf_op jit(solution)/shard_map/pallas_call | solution.py:331
  52.8 0.3 shard_map.77
  53.1 3.0 %collective-permute-start.11 = (f32[2,256,128]{2,1,0:T(8,128)S(1)}, f32[2,256,128]{2,1,0:T(8,128)S(1)}, u32[]{:S(2)}, u32[]{:S(2)}) collective-permute-start(f32[2,256,128]{2,1,0:T(8,128)S(1)} %get-tuple-element.66), channel_id=1, source_target_pairs={{0,1},{1,2},{2,3},{3,4},{4,5},{5,6},{6,7},{8,9},{9,10},{10,11},{11... | collective-permute-start | bytes 786440 | tf_op jit(solution)/shard_map/ppermute | solution.py:30
  56.1 3.1 %collective-permute-start.10 = (f32[2,128,256]{2,1,0:T(8,128)S(1)}, f32[2,128,256]{2,1,0:T(8,128)S(1)}, u32[]{:S(2)}, u32[]{:S(2)}) collective-permute-start(f32[2,128,256]{2,1,0:T(8,128)S(1)} %get-tuple-element.65), channel_id=1, source_target_pairs={{0,8},{1,9},{2,10},{3,11},{4,12},{5,13},{6,14},{7,15},{8,16},{9,17... | collective-permute-start | bytes 786440 | tf_op jit(solution)/shard_map/ppermute | solution.py:30
  59.2 1.9 %collective-permute-start.12 = (f32[2,128,128]{2,1,0:T(8,128)S(1)}, f32[2,128,128]{2,1,0:T(8,128)S(1)}, u32[]{:S(2)}, u32[]{:S(2)}) collective-permute-start(f32[2,128,128]{2,1,0:T(8,128)S(1)} %get-tuple-element.67), channel_id=1, source_target_pairs={{0,9},{1,10},{2,11},{3,12},{4,13},{5,14},{6,15},{8,17},{9,18},{10,... | collective-permute-start | bytes 393224 | tf_op jit(solution)/shard_map/ppermute | solution.py:30
  61.1 7.7 %collective-permute-done.12.diag_ref = f32[2,128,128]{2,1,0:T(8,128)S(1)} collective-permute-done((f32[2,128,128]{2,1,0:T(8,128)S(1)}, f32[2,128,128]{2,1,0:T(8,128)S(1)}, u32[]{:S(2)}, u32[]{:S(2)}) %collective-permute-start.12) | collective-permute-done | bytes 131104 | tf_op jit(solution)/shard_map/ppermute | solution.py:30
  68.8 1.1 %shard_map.78 = (f32[2,256,256]{2,1,0:T(8,128)}, f32[2,256,256]{2,1,0:T(8,128)}) custom-call(f32[2,256,128]{2,1,0:T(8,128)S(1)} %get-tuple-element.51.left_ref.refs_1_, f32[2,256,128]{2,1,0:T(8,128)S(1)} %get-tuple-element.52.right_ref.refs_2_, f32[2,256,128]{2,1,0:T(8,128)S(1)} %get-tuple-element.53.vl_ref, f32[2,256,128]{2,1,0:T(8,128)S(1)} %get-tuple-element.54.vr_ref, ...), custom_call_target="tpu_custom_call" | custom-call | flops 1000000 | bytes 1000000 | tf_op jit(solution)/shard_map/pallas_call | solution.py:362
  (16 shorter events, 0.1 us)
Async XLA Ops:
  0.6 1.0 %copy-start.1 = (f32[2,256,256]{2,1,0:T(8,128)S(1)}, f32[2,256,256]{2,1,0:T(8,128)}, u32[]{:S(2)}) copy-start(f32[2,256,256]{2,1,0:T(8,128)} %obj_ref.1) | copy-start | bytes 1572868
  1.7 7.0 %copy-start.2 = (f32[2,256,256]{2,1,0:T(8,128)S(1)}, f32[2,256,256]{2,1,0:T(8,128)}, u32[]{:S(2)}) copy-start(f32[2,256,256]{2,1,0:T(8,128)} %probe_ref.1) | copy-start | bytes 1572868
  1.7 6.9 %copy-start.3 = (f32[1,1,1,256,256]{4,3,2,1,0:T(8,128)S(1)}, f32[1,1,1,256,256]{4,3,2,1,0:T(8,128)}, u32[]{:S(2)}) copy-start(f32[1,1,1,256,256]{4,3,2,1,0:T(8,128)} %param.8) | copy-start | bytes 786436
  1.7 9.4 %collective-permute-start.1 = (f32[2,256,128]{2,1,0:T(8,128)S(1)}, f32[2,256,128]{2,1,0:T(8,128)S(1)}, u32[]{:S(2)}, u32[]{:S(2)}) collective-permute-start(f32[2,256,128]{2,1,0:T(8,128)S(1)} %get-tuple-element.38), channel_id=1, source_target_pairs={{1,0},{2,1},{3,2},{4,3},{5,4},{6,5},{7,6},{9,8},{10,9},{11,10},{12... | collective-permute-start | bytes 786440 | tf_op jit(solution)/shard_map/ppermute | solution.py:30
  4.5 12.0 %collective-permute-start = (f32[2,128,256]{2,1,0:T(8,128)S(1)}, f32[2,128,256]{2,1,0:T(8,128)S(1)}, u32[]{:S(2)}, u32[]{:S(2)}) collective-permute-start(f32[2,128,256]{2,1,0:T(8,128)S(1)} %slice.3), channel_id=1, source_target_pairs={{8,0},{9,1},{10,2},{11,3},{12,4},{13,5},{14,6},{15,7},{16,8},{17,9... | collective-permute-start | bytes 786440 | tf_op jit(solution)/shard_map/ppermute | solution.py:30
  6.7 8.9 %collective-permute-start.2 = (f32[2,128,128]{2,1,0:T(8,128)S(1)}, f32[2,128,128]{2,1,0:T(8,128)S(1)}, u32[]{:S(2)}, u32[]{:S(2)}) collective-permute-start(f32[2,128,128]{2,1,0:T(8,128)S(1)} %get-tuple-element.39), channel_id=1, source_target_pairs={{9,0},{10,1},{11,2},{12,3},{13,4},{14,5},{15,6},{17,8},{18,9},{19,... | collective-permute-start | bytes 393224 | tf_op jit(solution)/shard_map/ppermute | solution.py:30
  8.6 0.7 copy-start.4
  18.3 11.6 %collective-permute-start.3 = (f32[264,256]{1,0:T(8,128)S(1)}, f32[264,256]{1,0:T(8,128)S(1)}, u32[]{:S(2)}, u32[]{:S(2)}) collective-permute-start(f32[264,256]{1,0:T(8,128)S(1)} %get-tuple-element.49), channel_id=1, source_target_pairs={{0,8},{1,9},{2,10},{3,11},{4,12},{5,13},{6,14},{7,15},{8,16},{9,17... | collective-permute-start | bytes 811016 | tf_op jit(solution)/shard_map/ppermute | solution.py:30
  21.3 8.5 %copy-start = (f32[2,256,256]{2,1,0:T(8,128)S(1)}, f32[2,256,256]{2,1,0:T(8,128)}, u32[]{:S(2)}) copy-start(f32[2,256,256]{2,1,0:T(8,128)} %vel_ref.3) | copy-start | bytes 1572868
  21.7 8.2 %collective-permute-start.4 = (f32[520,128]{1,0:T(8,128)S(1)}, f32[520,128]{1,0:T(8,128)S(1)}, u32[]{:S(2)}, u32[]{:S(2)}) collective-permute-start(f32[520,128]{1,0:T(8,128)S(1)} %get-tuple-element.50), channel_id=1, source_target_pairs={{0,1},{1,2},{2,3},{3,4},{4,5},{5,6},{6,7},{8,9},{9,10},{10,11},{11... | collective-permute-start | bytes 798728 | tf_op jit(solution)/shard_map/ppermute | solution.py:30
  30.0 14.8 %collective-permute-start.8 = (f32[2,256,128]{2,1,0:T(8,128)S(1)}, f32[2,256,128]{2,1,0:T(8,128)S(1)}, u32[]{:S(2)}, u32[]{:S(2)}) collective-permute-start(f32[2,256,128]{2,1,0:T(8,128)S(1)} %get-tuple-element.59), channel_id=1, source_target_pairs={{1,0},{2,1},{3,2},{4,3},{5,4},{6,5},{7,6},{9,8},{10,9},{11,10},{12... | collective-permute-start | bytes 786440 | tf_op jit(solution)/shard_map/ppermute | solution.py:30
  33.3 11.8 %collective-permute-start.7 = (f32[2,128,128]{2,1,0:T(8,128)S(1)}, f32[2,128,128]{2,1,0:T(8,128)S(1)}, u32[]{:S(2)}, u32[]{:S(2)}) collective-permute-start(f32[2,128,128]{2,1,0:T(8,128)S(1)} %shard_map.74), channel_id=1, source_target_pairs={{8,0},{9,1},{10,2},{11,3},{12,4},{13,5},{14,6},{15,7},{16,8},{17,9... | collective-permute-start | bytes 393224 | tf_op jit(solution)/shard_map/ppermute | solution.py:30
  36.4 8.7 %collective-permute-start.5 = (f32[2,128,128]{2,1,0:T(8,128)S(1)}, f32[2,128,128]{2,1,0:T(8,128)S(1)}, u32[]{:S(2)}, u32[]{:S(2)}) collective-permute-start(f32[2,128,128]{2,1,0:T(8,128)S(1)} %get-tuple-element.55), channel_id=1, source_target_pairs={{0,9},{1,10},{2,11},{3,12},{4,13},{5,14},{6,15},{8,17},{9,18},{10,... | collective-permute-start | bytes 393224 | tf_op jit(solution)/shard_map/ppermute | solution.py:30
  40.7 7.7 %collective-permute-start.6 = (f32[2,128,128]{2,1,0:T(8,128)S(1)}, f32[2,128,128]{2,1,0:T(8,128)S(1)}, u32[]{:S(2)}, u32[]{:S(2)}) collective-permute-start(f32[2,128,128]{2,1,0:T(8,128)S(1)} %get-tuple-element.56), channel_id=1, source_target_pairs={{8,0},{9,1},{10,2},{11,3},{12,4},{13,5},{14,6},{15,7},{16,8},{17,9... | collective-permute-start | bytes 393224 | tf_op jit(solution)/shard_map/ppermute | solution.py:30
  42.8 8.2 %collective-permute-start.9 = (f32[2,128,128]{2,1,0:T(8,128)S(1)}, f32[2,128,128]{2,1,0:T(8,128)S(1)}, u32[]{:S(2)}, u32[]{:S(2)}) collective-permute-start(f32[2,128,128]{2,1,0:T(8,128)S(1)} %get-tuple-element.60), channel_id=1, source_target_pairs={{9,0},{10,1},{11,2},{12,3},{13,4},{14,5},{15,6},{17,8},{18,9},{19,... | collective-permute-start | bytes 393224 | tf_op jit(solution)/shard_map/ppermute | solution.py:30
  53.1 15.7 %collective-permute-start.11 = (f32[2,256,128]{2,1,0:T(8,128)S(1)}, f32[2,256,128]{2,1,0:T(8,128)S(1)}, u32[]{:S(2)}, u32[]{:S(2)}) collective-permute-start(f32[2,256,128]{2,1,0:T(8,128)S(1)} %get-tuple-element.66), channel_id=1, source_target_pairs={{0,1},{1,2},{2,3},{3,4},{4,5},{5,6},{6,7},{8,9},{9,10},{10,11},{11... | collective-permute-start | bytes 786440 | tf_op jit(solution)/shard_map/ppermute | solution.py:30
  56.1 12.7 %collective-permute-start.10 = (f32[2,128,256]{2,1,0:T(8,128)S(1)}, f32[2,128,256]{2,1,0:T(8,128)S(1)}, u32[]{:S(2)}, u32[]{:S(2)}) collective-permute-start(f32[2,128,256]{2,1,0:T(8,128)S(1)} %get-tuple-element.65), channel_id=1, source_target_pairs={{0,8},{1,9},{2,10},{3,11},{4,12},{5,13},{6,14},{7,15},{8,16},{9,17... | collective-permute-start | bytes 786440 | tf_op jit(solution)/shard_map/ppermute | solution.py:30
  59.2 9.6 %collective-permute-start.12 = (f32[2,128,128]{2,1,0:T(8,128)S(1)}, f32[2,128,128]{2,1,0:T(8,128)S(1)}, u32[]{:S(2)}, u32[]{:S(2)}) collective-permute-start(f32[2,128,128]{2,1,0:T(8,128)S(1)} %get-tuple-element.67), channel_id=1, source_target_pairs={{0,9},{1,10},{2,11},{3,12},{4,13},{5,14},{6,15},{8,17},{9,18},{10,... | collective-permute-start | bytes 393224 | tf_op jit(solution)/shard_map/ppermute | solution.py:30

commit v4 on v3

--- a/solution.py
+++ b/solution.py
@@ -153,11 +153,10 @@
         (mask_ref, left_ref, right_ref, lower_ref, beside_ref, corner_ref, probe_ref, meas_ref, yb_ref,
          table_ref, cols_ref, rows_ref, own_out, down_out, diag_out, r00_out, xb_out, kept_out) = refs
     else:
-        (mask_ref, left_ref, right_ref, up00_ref, up01_ref, kept_ref, fix_ref, diag_ref, beside_ref, corner_ref,
+        (mask_ref, left_ref, right_ref, up_ref, kept_ref, fix_ref, diag_ref, beside_ref, corner_ref,
          probe_ref, meas_ref, yb_ref, table_ref, cols_ref, rows_ref,
          own_out, down_out, diag_out, r00_out, xb_out) = refs
-        kept_scale = mask_ref[2].astype(jnp.float32) * step_size
-        corner_scale = kept_scale * mask_ref[3].astype(jnp.float32)
+        corner_scale = (mask_ref[2] * mask_ref[3]).astype(jnp.float32) * step_size
     below, beyond = masks(mask_ref)
     pr, pi = probe_ref[0, :H], probe_ref[1, :H]
     patch = []
@@ -168,9 +167,9 @@
         else:
             own00 = own00 - step_size * diag_ref[part]
             beside = beside - fix_ref[part, :, H:]
-            lower00 = up00_ref[part] - fix_ref[part, :, :H]
-            lower01 = up01_ref[part] - kept_scale * kept_ref[part, :, H:]
-            corner = corner_ref[part] - corner_scale * kept_ref[part, :, :H]
+            lower00 = up_ref[part, :, :H] - fix_ref[part, :, :H]
+            lower01 = up_ref[part, :, H:]
+            corner = corner_ref[part] - corner_scale * kept_ref[part]
         q00 = jnp.where(below, jnp.where(beyond, corner, lower00), jnp.where(beyond, beside, own00))
         q01 = jnp.where(below, lower01, right_ref[part, :H])
         patch.append(jnp.concatenate([q00, q01], axis=1))
@@ -205,8 +204,7 @@
             down_out[part * H : (part + 1) * H, :H] = jnp.where(below, g00, 0.0)
             down_out[part * H : (part + 1) * H, H:] = d01
             r00_out[part] = jnp.where(beyond, g00, 0.0)
-            kept_out[part, :, :H] = diag
-            kept_out[part, :, H:] = d01
+            kept_out[part] = diag
         else:
             down_out[part, :, :H] = jnp.where(jnp.logical_and(below, ~beyond), g00, 0.0)
             down_out[part, :, H:] = d01
@@ -240,11 +238,6 @@
     return obj - step_size * vel, vel
 
 
-def ahead_kernel(right_ref, vel_ref, own_ref, up_out):
-    for part in range(2):
-        up_out[part], _ = stepped(right_ref[part, :H], vel_ref[part, :H, H:], own_ref[part, :, H:])
-
-
 def update_kernel(
     mask_ref, left_ref, right_ref, vel_ref, top_ref, bottom_ref, above_ref, before_ref,
     left_out, right_out, vl_out, vr_out, up_out, corner_out, send_out, fix_out,
@@ -260,8 +253,9 @@
         g11 = bottom_ref[part, :, H:]
         obj, vel = stepped(left_ref[part, :H], vel_ref[part, :H, :H], g00)
         left_out[part, :H], vl_out[part, :H] = obj, vel
-        up_out[part], corner_out[part], send_out[part, :H] = obj, obj, obj
-        right_out[part, :H], vr_out[part, :H] = stepped(right_ref[part, :H], vel_ref[part, :H, H:], g01)
+        up_out[part, :, :H], corner_out[part], send_out[part, :H] = obj, obj, obj
+        obj, vel = stepped(right_ref[part, :H], vel_ref[part, :H, H:], g01)
+        right_out[part, :H], vr_out[part, :H], up_out[part, :, H:] = obj, vel, obj
         obj, vel = stepped(left_ref[part, H:], vel_ref[part, H:, :H], g10)
         left_out[part, H:], vl_out[part, H:], send_out[part, H:] = obj, vel, obj
         right_out[part, H:], vr_out[part, H:] = stepped(right_ref[part, H:], vel_ref[part, H:, H:], g11)
@@ -336,24 +330,22 @@
         )
 
     top, down, diag, r00, xb, kept = main(
-        lambda *refs: main_kernel(True, *refs), (strip, shape(N + 8, N), quad, quad, rows, strip),
+        lambda *refs: main_kernel(True, *refs), (strip, shape(N + 8, N), quad, quad, rows, quad),
         left, right, lower, beside, corner,
     )
     above = shifted(down, 1, 0)
     bottom, right_part = post(True, shape(2 * N + 8, H), xb, r00)
     before = shifted(right_part, 0, 1)
     late = shifted(diag, 1, 1)
-    (ahead,) = kernel(ahead_kernel, 10**6, 0, 3, (quad,))(right, velocity, top)
-    up01 = shifted(ahead, -1, 0)
     left, right, vel_left, vel_right, q00, q00_corner, left_send, fix = kernel(
-        update_kernel, 10**6, 0, 8, (half, half, half, half, quad, quad, half, strip)
+        update_kernel, 10**6, 0, 8, (half, half, half, half, strip, quad, half, strip)
     )(mask, left, right, velocity, top, bottom, above, before)
     up00 = shifted(q00, -1, 0)
     corner = shifted(q00_corner, -1, -1)
     beside = shifted(left_send, 0, -1)
     top, down, diag, r00, xb = main(
         lambda *refs: main_kernel(False, *refs), (strip, strip, quad, quad, rows),
-        left, right, up00, up01, kept, fix, late, beside, corner,
+        left, right, up00, kept, fix, late, beside, corner,
     )
     above = shifted(down, 1, 0)
     bottom, right_part = post(False, half, xb, r00)

time: 71.2 us -> 69.1 us (0.971)
  waiting for transfers between devices: 22.1 us -> 20.9 us
    ppermute x13 -> x12, waiting for transfers between devices: 22.1 us -> 20.9 us  [shifted(): return lax.ppermute(value, ('row', 'col'), pairs)]
    ppermute x13 -> x12, starting transfers between devices: 37.3 us -> 36.9 us  [shifted(): return lax.ppermute(value, ('row', 'col'), pairs)]
  transfers between devices with their start and end apart: 13 -> 12, of which waited for: 6 -> 6; matrix products, arithmetic and copies ran while one was open for 0% -> 0% of each run, Pallas kernels for 4% -> 4%
where the time goes in v4:
time: 69.1 us; the launch traced here: 68.2 us
  starting transfers between devices  36.9 us (53%)
  waiting for transfers between devices  20.9 us (30%)
  Pallas kernels  7.89 us (11%)
  local copies, waits for them, and re-layouts  1.7 us (2%)
  between operations  0.87 us (1%)
    ppermute x12, starting transfers between devices, shifted(): return lax.ppermute(value, ('row', 'col'), pairs)  36.9 us
    ppermute x12, waiting for transfers between devices, shifted(): return lax.ppermute(value, ('row', 'col'), pairs)  20.9 us
    pallas_call x2, Pallas kernels, main(): kernel(body, 10 ** 9, 0, 1 + len(arrays) + len(rest), outs)  3.46 us
    pallas_call x1, Pallas kernels, steps(): kernel(prep_kernel, 10 ** 8, 3, 2, (shape(2, N, N), rows, shape(4, H, H,...  1.85 us
    unnamed x10, local copies, waits for them, and re-layouts  1.68 us
  transfers between devices with their start and end apart: 12, of which 6 were waited for; matrix products, arithmetic and copies ran while one was open for 0% of the time, Pallas kernels for 4%

profile of v4, /device:TPU:11, one launch (start us, length us, event | category | flops | bytes accessed | tf_op | source)
XLA Modules:
  0.0 68.2 jit_solution(6659818659342654202)
XLA Ops:
  0.6 1.0 %copy-done = f32[2,256,256]{2,1,0:T(8,128)S(1)} copy-done((f32[2,256,256]{2,1,0:T(8,128)S(1)}, f32[2,256,256]{2,1,0:T(8,128)}, u32[]{:S(2)}) %copy-start) | copy-done | bytes 524312
  1.7 0.1 shard_map.69
  1.7 0.0 copy-start.3
  1.7 2.7 %collective-permute-start.1 = (f32[2,256,128]{2,1,0:T(8,128)S(1)}, f32[2,256,128]{2,1,0:T(8,128)S(1)}, u32[]{:S(2)}, u32[]{:S(2)}) collective-permute-start(f32[2,256,128]{2,1,0:T(8,128)S(1)} %get-tuple-element.38), channel_id=1, source_target_pairs={{1,0},{2,1},{3,2},{4,3},{5,4},{6,5},{7,6},{9,8},{10,9},{11,10},{12... | collective-permute-start | bytes 786440 | tf_op jit(solution)/shard_map/ppermute | solution.py:30
  4.5 2.2 %collective-permute-start = (f32[2,128,256]{2,1,0:T(8,128)S(1)}, f32[2,128,256]{2,1,0:T(8,128)S(1)}, u32[]{:S(2)}, u32[]{:S(2)}) collective-permute-start(f32[2,128,256]{2,1,0:T(8,128)S(1)} %slice.3), channel_id=1, source_target_pairs={{8,0},{9,1},{10,2},{11,3},{12,4},{13,5},{14,6},{15,7},{16,8},{17,9... | collective-permute-start | bytes 786440 | tf_op jit(solution)/shard_map/ppermute | solution.py:30
  6.7 1.9 %collective-permute-start.2 = (f32[2,128,128]{2,1,0:T(8,128)S(1)}, f32[2,128,128]{2,1,0:T(8,128)S(1)}, u32[]{:S(2)}, u32[]{:S(2)}) collective-permute-start(f32[2,128,128]{2,1,0:T(8,128)S(1)} %get-tuple-element.39), channel_id=1, source_target_pairs={{9,0},{10,1},{11,2},{12,3},{13,4},{14,5},{15,6},{17,8},{18,9},{19,... | collective-permute-start | bytes 393224 | tf_op jit(solution)/shard_map/ppermute | solution.py:30
  8.6 0.0 copy-start.4
  8.6 0.6 copy-done.4
  9.3 1.9 %shard_map.68 = (f32[2,256,256]{2,1,0:T(8,128)S(1)}, f32[256,256]{1,0:T(8,128)S(1)}, s32[4,128,128]{2,1,0:T(8,128)S(1)}, bf16[4,256,256]{2,1,0:T(8,128)(2,1)S(1)...) custom-call(s32[2]{0:T(128)S(1)} %bitcast.5, s32[1]{0:T(128)} %bitcast.1.below_ref, s32[1]{0:T(128)} %bitcast.2.beside_ref, ...), custom_call_target="tpu_custom_call" | custom-call | flops 100000000 | bytes 1000000 | tf_op jit(solution)/shard_map/pallas_call | solution.py:310
  11.1 0.3 shard_map.70.refs_8_
  11.4 4.2 %collective-permute-done.2.refs_5_ = f32[2,128,128]{2,1,0:T(8,128)S(1)} collective-permute-done((f32[2,128,128]{2,1,0:T(8,128)S(1)}, f32[2,128,128]{2,1,0:T(8,128)S(1)}, u32[]{:S(2)}, u32[]{:S(2)}) %collective-permute-start.2) | collective-permute-done | bytes 131104 | tf_op jit(solution)/shard_map/ppermute | solution.py:30
  15.6 1.0 %collective-permute-done.refs_3_ = f32[2,128,256]{2,1,0:T(8,128)S(1)} collective-permute-done((f32[2,128,256]{2,1,0:T(8,128)S(1)}, f32[2,128,256]{2,1,0:T(8,128)S(1)}, u32[]{:S(2)}, u32[]{:S(2)}) %collective-permute-start) | collective-permute-done | bytes 262176 | tf_op jit(solution)/shard_map/ppermute | solution.py:30
  16.5 1.7 %shard_map.71 = (f32[2,128,256]{2,1,0:T(8,128)S(1)}, f32[264,256]{1,0:T(8,128)S(1)}, f32[2,128,128]{2,1,0:T(8,128)S(1)}, f32[2,128,128]{2,1,0:T(8,128)S(1)}, f32...) custom-call(s32[4,128,128]{2,1,0:T(8,128)S(1)} %get-tuple-element.35.mask_ref.refs_0_, ...), custom_call_target="tpu_custom_call" | custom-call | flops 1000000000 | bytes 1000000 | tf_op jit(solution)/shard_map/pallas_call | solution.py:325
  18.3 3.1 %collective-permute-start.3 = (f32[264,256]{1,0:T(8,128)S(1)}, f32[264,256]{1,0:T(8,128)S(1)}, u32[]{:S(2)}, u32[]{:S(2)}) collective-permute-start(f32[264,256]{1,0:T(8,128)S(1)} %get-tuple-element.49), channel_id=1, source_target_pairs={{0,8},{1,9},{2,10},{3,11},{4,12},{5,13},{6,14},{7,15},{8,16},{9,17... | collective-permute-start | bytes 811016 | tf_op jit(solution)/shard_map/ppermute | solution.py:30
  21.3 0.3 shard_map.72
  21.6 4.8 %collective-permute-start.4 = (f32[520,128]{1,0:T(8,128)S(1)}, f32[520,128]{1,0:T(8,128)S(1)}, u32[]{:S(2)}, u32[]{:S(2)}) collective-permute-start(f32[520,128]{1,0:T(8,128)S(1)} %get-tuple-element.50), channel_id=1, source_target_pairs={{0,1},{1,2},{2,3},{3,4},{4,5},{5,6},{6,7},{8,9},{9,10},{10,11},{11... | collective-permute-start | bytes 798728 | tf_op jit(solution)/shard_map/ppermute | solution.py:30
  26.5 3.3 %collective-permute-done.4.before_ref = f32[520,128]{1,0:T(8,128)S(1)} collective-permute-done((f32[520,128]{1,0:T(8,128)S(1)}, f32[520,128]{1,0:T(8,128)S(1)}, u32[]{:S(2)}, u32[]{:S(2)}) %collective-permute-start.4) | collective-permute-done | bytes 266272 | tf_op jit(solution)/shard_map/ppermute | solution.py:30
  29.8 0.2 shard_map.73
  30.0 3.2 %collective-permute-start.7 = (f32[2,256,128]{2,1,0:T(8,128)S(1)}, f32[2,256,128]{2,1,0:T(8,128)S(1)}, u32[]{:S(2)}, u32[]{:S(2)}) collective-permute-start(f32[2,256,128]{2,1,0:T(8,128)S(1)} %get-tuple-element.59), channel_id=1, source_target_pairs={{1,0},{2,1},{3,2},{4,3},{5,4},{6,5},{7,6},{9,8},{10,9},{11,10},{12... | collective-permute-start | bytes 786440 | tf_op jit(solution)/shard_map/ppermute | solution.py:30
  33.2 3.1 %collective-permute-start.6 = (f32[2,128,256]{2,1,0:T(8,128)S(1)}, f32[2,128,256]{2,1,0:T(8,128)S(1)}, u32[]{:S(2)}, u32[]{:S(2)}) collective-permute-start(f32[2,128,256]{2,1,0:T(8,128)S(1)} %get-tuple-element.56), channel_id=1, source_target_pairs={{8,0},{9,1},{10,2},{11,3},{12,4},{13,5},{14,6},{15,7},{16,8},{17,9... | collective-permute-start | bytes 786440 | tf_op jit(solution)/shard_map/ppermute | solution.py:30
  36.3 4.3 %collective-permute-start.5 = (f32[2,128,128]{2,1,0:T(8,128)S(1)}, f32[2,128,128]{2,1,0:T(8,128)S(1)}, u32[]{:S(2)}, u32[]{:S(2)}) collective-permute-start(f32[2,128,128]{2,1,0:T(8,128)S(1)} %get-tuple-element.55), channel_id=1, source_target_pairs={{0,9},{1,10},{2,11},{3,12},{4,13},{5,14},{6,15},{8,17},{9,18},{10,... | collective-permute-start | bytes 393224 | tf_op jit(solution)/shard_map/ppermute | solution.py:30
  40.6 1.9 %collective-permute-start.8 = (f32[2,128,128]{2,1,0:T(8,128)S(1)}, f32[2,128,128]{2,1,0:T(8,128)S(1)}, u32[]{:S(2)}, u32[]{:S(2)}) collective-permute-start(f32[2,128,128]{2,1,0:T(8,128)S(1)} %get-tuple-element.60), channel_id=1, source_target_pairs={{9,0},{10,1},{11,2},{12,3},{13,4},{14,5},{15,6},{17,8},{18,9},{19,... | collective-permute-start | bytes 393224 | tf_op jit(solution)/shard_map/ppermute | solution.py:30
  42.6 0.3 shard_map.74.refs_11_
  42.8 1.5 %collective-permute-done.5.refs_6_.late_ref = f32[2,128,128]{2,1,0:T(8,128)S(1)} collective-permute-done((f32[2,128,128]{2,1,0:T(8,128)S(1)}, f32[2,128,128]{2,1,0:T(8,128)S(1)}, u32[]{:S(2)}, u32[]{:S(2)}) %collective-permute-start.5) | collective-permute-done | bytes 131104 | tf_op jit(solution)/shard_map/ppermute | solution.py:30
  44.3 4.5 %collective-permute-done.8.refs_8_ = f32[2,128,128]{2,1,0:T(8,128)S(1)} collective-permute-done((f32[2,128,128]{2,1,0:T(8,128)S(1)}, f32[2,128,128]{2,1,0:T(8,128)S(1)}, u32[]{:S(2)}, u32[]{:S(2)}) %collective-permute-start.8) | collective-permute-done | bytes 131104 | tf_op jit(solution)/shard_map/ppermute | solution.py:30
  48.8 1.8 %shard_map.75 = (f32[2,128,256]{2,1,0:T(8,128)S(1)}, f32[2,128,256]{2,1,0:T(8,128)S(1)}, f32[2,128,128]{2,1,0:T(8,128)S(1)}, f32[2,128,128]{2,1,0:T(8,128)S(1)}, f32[256,256]{1,0:T(8,128)S(1)}) custom-call(s32[4,128,128]{2,1,0:T(8,128)S(1)} %get-tuple-element.35.mask_ref.refs_0_, f32[2,256,128]{2,1,0:T(8,128)S(1)} %get-tuple-element.51.left_ref.refs_1_, ...), custom_call_target="tpu_custom_call" | custom-call | flops 1000000000 | bytes 1000000 | tf_op jit(solution)/shard_map/pallas_call | solution.py:325
  50.6 0.3 shard_map.76
  50.9 4.2 %collective-permute-start.10 = (f32[2,256,128]{2,1,0:T(8,128)S(1)}, f32[2,256,128]{2,1,0:T(8,128)S(1)}, u32[]{:S(2)}, u32[]{:S(2)}) collective-permute-start(f32[2,256,128]{2,1,0:T(8,128)S(1)} %get-tuple-element.66), channel_id=1, source_target_pairs={{0,1},{1,2},{2,3},{3,4},{4,5},{5,6},{6,7},{8,9},{9,10},{10,11},{11... | collective-permute-start | bytes 786440 | tf_op jit(solution)/shard_map/ppermute | solution.py:30
  55.1 1.9 %collective-permute-start.9 = (f32[2,128,256]{2,1,0:T(8,128)S(1)}, f32[2,128,256]{2,1,0:T(8,128)S(1)}, u32[]{:S(2)}, u32[]{:S(2)}) collective-permute-start(f32[2,128,256]{2,1,0:T(8,128)S(1)} %get-tuple-element.65), channel_id=1, source_target_pairs={{0,8},{1,9},{2,10},{3,11},{4,12},{5,13},{6,14},{7,15},{8,16},{9,17... | collective-permute-start | bytes 786440 | tf_op jit(solution)/shard_map/ppermute | solution.py:30
  57.0 3.7 %collective-permute-start.11 = (f32[2,128,128]{2,1,0:T(8,128)S(1)}, f32[2,128,128]{2,1,0:T(8,128)S(1)}, u32[]{:S(2)}, u32[]{:S(2)}) collective-permute-start(f32[2,128,128]{2,1,0:T(8,128)S(1)} %get-tuple-element.67), channel_id=1, source_target_pairs={{0,9},{1,10},{2,11},{3,12},{4,13},{5,14},{6,15},{8,17},{9,18},{10,... | collective-permute-start | bytes 393224 | tf_op jit(solution)/shard_map/ppermute | solution.py:30
  60.7 6.4 %collective-permute-done.11.diag_ref = f32[2,128,128]{2,1,0:T(8,128)S(1)} collective-permute-done((f32[2,128,128]{2,1,0:T(8,128)S(1)}, f32[2,128,128]{2,1,0:T(8,128)S(1)}, u32[]{:S(2)}, u32[]{:S(2)}) %collective-permute-start.11) | collective-permute-done | bytes 131104 | tf_op jit(solution)/shard_map/ppermute | solution.py:30
  67.1 1.1 %shard_map.77 = (f32[2,256,256]{2,1,0:T(8,128)}, f32[2,256,256]{2,1,0:T(8,128)}) custom-call(f32[2,256,128]{2,1,0:T(8,128)S(1)} %get-tuple-element.51.left_ref.refs_1_, f32[2,256,128]{2,1,0:T(8,128)S(1)} %get-tuple-element.52.right_ref.refs_2_, f32[2,256,128]{2,1,0:T(8,128)S(1)} %get-tuple-element.53.vl_ref, f32[2,256,128]{2,1,0:T(8,128)S(1)} %get-tuple-element.54.vr_ref, ...), custom_call_target="tpu_custom_call" | custom-call | flops 1000000 | bytes 1000000 | tf_op jit(solution)/shard_map/pallas_call | solution.py:354
  (13 shorter events, 0.0 us)
Async XLA Ops:
  0.6 1.0 %copy-start = (f32[2,256,256]{2,1,0:T(8,128)S(1)}, f32[2,256,256]{2,1,0:T(8,128)}, u32[]{:S(2)}) copy-start(f32[2,256,256]{2,1,0:T(8,128)} %obj_ref.1) | copy-start | bytes 1572868
  1.7 7.0 %copy-start.1 = (f32[2,256,256]{2,1,0:T(8,128)S(1)}, f32[2,256,256]{2,1,0:T(8,128)}, u32[]{:S(2)}) copy-start(f32[2,256,256]{2,1,0:T(8,128)} %probe_ref.1) | copy-start | bytes 1572868
  1.7 6.9 %copy-start.3 = (f32[1,1,1,256,256]{4,3,2,1,0:T(8,128)S(1)}, f32[1,1,1,256,256]{4,3,2,1,0:T(8,128)}, u32[]{:S(2)}) copy-start(f32[1,1,1,256,256]{4,3,2,1,0:T(8,128)} %param.8) | copy-start | bytes 786436
  1.7 9.4 %collective-permute-start.1 = (f32[2,256,128]{2,1,0:T(8,128)S(1)}, f32[2,256,128]{2,1,0:T(8,128)S(1)}, u32[]{:S(2)}, u32[]{:S(2)}) collective-permute-start(f32[2,256,128]{2,1,0:T(8,128)S(1)} %get-tuple-element.38), channel_id=1, source_target_pairs={{1,0},{2,1},{3,2},{4,3},{5,4},{6,5},{7,6},{9,8},{10,9},{11,10},{12... | collective-permute-start | bytes 786440 | tf_op jit(solution)/shard_map/ppermute | solution.py:30
  4.5 12.0 %collective-permute-start = (f32[2,128,256]{2,1,0:T(8,128)S(1)}, f32[2,128,256]{2,1,0:T(8,128)S(1)}, u32[]{:S(2)}, u32[]{:S(2)}) collective-permute-start(f32[2,128,256]{2,1,0:T(8,128)S(1)} %slice.3), channel_id=1, source_target_pairs={{8,0},{9,1},{10,2},{11,3},{12,4},{13,5},{14,6},{15,7},{16,8},{17,9... | collective-permute-start | bytes 786440 | tf_op jit(solution)/shard_map/ppermute | solution.py:30
  6.7 8.9 %collective-permute-start.2 = (f32[2,128,128]{2,1,0:T(8,128)S(1)}, f32[2,128,128]{2,1,0:T(8,128)S(1)}, u32[]{:S(2)}, u32[]{:S(2)}) collective-permute-start(f32[2,128,128]{2,1,0:T(8,128)S(1)} %get-tuple-element.39), channel_id=1, source_target_pairs={{9,0},{10,1},{11,2},{12,3},{13,4},{14,5},{15,6},{17,8},{18,9},{19,... | collective-permute-start | bytes 393224 | tf_op jit(solution)/shard_map/ppermute | solution.py:30
  8.6 0.7 copy-start.4
  18.3 11.6 %collective-permute-start.3 = (f32[264,256]{1,0:T(8,128)S(1)}, f32[264,256]{1,0:T(8,128)S(1)}, u32[]{:S(2)}, u32[]{:S(2)}) collective-permute-start(f32[264,256]{1,0:T(8,128)S(1)} %get-tuple-element.49), channel_id=1, source_target_pairs={{0,8},{1,9},{2,10},{3,11},{4,12},{5,13},{6,14},{7,15},{8,16},{9,17... | collective-permute-start | bytes 811016 | tf_op jit(solution)/shard_map/ppermute | solution.py:30
  21.3 8.5 %copy-start.2 = (f32[2,256,256]{2,1,0:T(8,128)S(1)}, f32[2,256,256]{2,1,0:T(8,128)}, u32[]{:S(2)}) copy-start(f32[2,256,256]{2,1,0:T(8,128)} %vel_ref.1) | copy-start | bytes 1572868
  21.6 8.2 %collective-permute-start.4 = (f32[520,128]{1,0:T(8,128)S(1)}, f32[520,128]{1,0:T(8,128)S(1)}, u32[]{:S(2)}, u32[]{:S(2)}) collective-permute-start(f32[520,128]{1,0:T(8,128)S(1)} %get-tuple-element.50), channel_id=1, source_target_pairs={{0,1},{1,2},{2,3},{3,4},{4,5},{5,6},{6,7},{8,9},{9,10},{10,11},{11... | collective-permute-start | bytes 798728 | tf_op jit(solution)/shard_map/ppermute | solution.py:30
  30.0 12.5 %collective-permute-start.7 = (f32[2,256,128]{2,1,0:T(8,128)S(1)}, f32[2,256,128]{2,1,0:T(8,128)S(1)}, u32[]{:S(2)}, u32[]{:S(2)}) collective-permute-start(f32[2,256,128]{2,1,0:T(8,128)S(1)} %get-tuple-element.59), channel_id=1, source_target_pairs={{1,0},{2,1},{3,2},{4,3},{5,4},{6,5},{7,6},{9,8},{10,9},{11,10},{12... | collective-permute-start | bytes 786440 | tf_op jit(solution)/shard_map/ppermute | solution.py:30
  33.2 15.6 %collective-permute-start.6 = (f32[2,128,256]{2,1,0:T(8,128)S(1)}, f32[2,128,256]{2,1,0:T(8,128)S(1)}, u32[]{:S(2)}, u32[]{:S(2)}) collective-permute-start(f32[2,128,256]{2,1,0:T(8,128)S(1)} %get-tuple-element.56), channel_id=1, source_target_pairs={{8,0},{9,1},{10,2},{11,3},{12,4},{13,5},{14,6},{15,7},{16,8},{17,9... | collective-permute-start | bytes 786440 | tf_op jit(solution)/shard_map/ppermute | solution.py:30
  36.3 8.0 %collective-permute-start.5 = (f32[2,128,128]{2,1,0:T(8,128)S(1)}, f32[2,128,128]{2,1,0:T(8,128)S(1)}, u32[]{:S(2)}, u32[]{:S(2)}) collective-permute-start(f32[2,128,128]{2,1,0:T(8,128)S(1)} %get-tuple-element.55), channel_id=1, source_target_pairs={{0,9},{1,10},{2,11},{3,12},{4,13},{5,14},{6,15},{8,17},{9,18},{10,... | collective-permute-start | bytes 393224 | tf_op jit(solution)/shard_map/ppermute | solution.py:30
  40.6 8.2 %collective-permute-start.8 = (f32[2,128,128]{2,1,0:T(8,128)S(1)}, f32[2,128,128]{2,1,0:T(8,128)S(1)}, u32[]{:S(2)}, u32[]{:S(2)}) collective-permute-start(f32[2,128,128]{2,1,0:T(8,128)S(1)} %get-tuple-element.60), channel_id=1, source_target_pairs={{9,0},{10,1},{11,2},{12,3},{13,4},{14,5},{15,6},{17,8},{18,9},{19,... | collective-permute-start | bytes 393224 | tf_op jit(solution)/shard_map/ppermute | solution.py:30
  50.9 16.2 %collective-permute-start.10 = (f32[2,256,128]{2,1,0:T(8,128)S(1)}, f32[2,256,128]{2,1,0:T(8,128)S(1)}, u32[]{:S(2)}, u32[]{:S(2)}) collective-permute-start(f32[2,256,128]{2,1,0:T(8,128)S(1)} %get-tuple-element.66), channel_id=1, source_target_pairs={{0,1},{1,2},{2,3},{3,4},{4,5},{5,6},{6,7},{8,9},{9,10},{10,11},{11... | collective-permute-start | bytes 786440 | tf_op jit(solution)/shard_map/ppermute | solution.py:30
  55.1 12.0 %collective-permute-start.9 = (f32[2,128,256]{2,1,0:T(8,128)S(1)}, f32[2,128,256]{2,1,0:T(8,128)S(1)}, u32[]{:S(2)}, u32[]{:S(2)}) collective-permute-start(f32[2,128,256]{2,1,0:T(8,128)S(1)} %get-tuple-element.65), channel_id=1, source_target_pairs={{0,8},{1,9},{2,10},{3,11},{4,12},{5,13},{6,14},{7,15},{8,16},{9,17... | collective-permute-start | bytes 786440 | tf_op jit(solution)/shard_map/ppermute | solution.py:30
  57.0 10.1 %collective-permute-start.11 = (f32[2,128,128]{2,1,0:T(8,128)S(1)}, f32[2,128,128]{2,1,0:T(8,128)S(1)}, u32[]{:S(2)}, u32[]{:S(2)}) collective-permute-start(f32[2,128,128]{2,1,0:T(8,128)S(1)} %get-tuple-element.67), channel_id=1, source_target_pairs={{0,9},{1,10},{2,11},{3,12},{4,13},{5,14},{6,15},{8,17},{9,18},{10,... | collective-permute-start | bytes 393224 | tf_op jit(solution)/shard_map/ppermute | solution.py:30

commit v5 on v4

--- a/solution.py
+++ b/solution.py
@@ -155,7 +155,7 @@
     else:
         (mask_ref, left_ref, right_ref, up_ref, kept_ref, fix_ref, diag_ref, beside_ref, corner_ref,
          probe_ref, meas_ref, yb_ref, table_ref, cols_ref, rows_ref,
-         own_out, down_out, diag_out, r00_out, xb_out) = refs
+         own_out, down_out, diag_out, bottom_out, right_out) = refs
         corner_scale = (mask_ref[2] * mask_ref[3]).astype(jnp.float32) * step_size
     below, beyond = masks(mask_ref)
     pr, pi = probe_ref[0, :H], probe_ref[1, :H]
@@ -191,7 +191,8 @@
     wr = jnp.concatenate([rows_ref[0], rows_ref[0]], axis=1)
     wi = jnp.concatenate([rows_ref[1], rows_ref[1]], axis=1)
     turned = jnp.concatenate([qr * wr + qi * wi, qi * wr - qr * wi], axis=0)
-    xb_out[...] = back[0] - turned
+    if first:
+        xb_out[...] = back[0] - turned
     out = back_stage(back[0] + turned, pr, pi, minus(table_ref), cols_ref)
     for part in range(2):
         g00, g01 = out[part][:, :H], out[part][:, H:]
@@ -208,29 +209,30 @@
         else:
             down_out[part, :, :H] = jnp.where(jnp.logical_and(below, ~beyond), g00, 0.0)
             down_out[part, :, H:] = d01
-            r00_out[part] = jnp.where(jnp.logical_and(~below, beyond), g00, 0.0)
+            right_out[part, :H] = jnp.where(jnp.logical_and(~below, beyond), g00, 0.0)
     if first:
         down_out[2 * H :, :H] = mask_ref[1, :8].astype(jnp.float32)
         down_out[2 * H :, H:] = jnp.zeros((8, H), jnp.float32)
-
-
-def post_kernel(first, mask_ref, xb_ref, r00_ref, probe_ref, table_ref, cols_ref, own_out, right_out):
+    else:
+        out = back_stage(back[0] - turned, probe_ref[0, H:], probe_ref[1, H:], minus(table_ref), cols_ref)
+        for part in range(2):
+            g10, g11 = out[part][:, :H], out[part][:, H:]
+            bottom_out[part, :, :H] = jnp.where(beyond, 0.0, g10)
+            bottom_out[part, :, H:] = g11
+            right_out[part, H:] = jnp.where(beyond, g10, 0.0)
+
+
+def post_kernel(mask_ref, xb_ref, r00_ref, probe_ref, table_ref, cols_ref, own_out, right_out):
     below, beyond = masks(mask_ref)
     out = back_stage(xb_ref[...], probe_ref[0, H:], probe_ref[1, H:], minus(table_ref), cols_ref)
     for part in range(2):
         g10, g11 = out[part][:, :H], out[part][:, H:]
         own_out[part, :, :H] = jnp.where(beyond, 0.0, g10)
         own_out[part, :, H:] = g11
-        r10 = jnp.where(beyond, g10, 0.0)
-        if first:
-            right_out[part * N : part * N + H] = r00_ref[part]
-            right_out[part * N + H : (part + 1) * N] = r10
-        else:
-            right_out[part, :H] = r00_ref[part]
-            right_out[part, H:] = r10
-    if first:
-        rows = jnp.sum(below.astype(jnp.float32), axis=0, keepdims=True)
-        right_out[2 * N :] = jnp.broadcast_to(rows, (8, H))
+        right_out[part * N : part * N + H] = r00_ref[part]
+        right_out[part * N + H : (part + 1) * N] = jnp.where(beyond, g10, 0.0)
+    rows = jnp.sum(below.astype(jnp.float32), axis=0, keepdims=True)
+    right_out[2 * N :] = jnp.broadcast_to(rows, (8, H))
 
 
 def stepped(obj, vel, g):
@@ -324,17 +326,14 @@
         rest = (turned, intensity, pre(arrays[0], arrays[1], arrays[-2]), tables, along_cols, along_rows)
         return kernel(body, 10**9, 0, 1 + len(arrays) + len(rest), outs)(mask, *arrays, *rest)
 
-    def post(first, sent, xb, r00):
-        return kernel(lambda *refs: post_kernel(first, *refs), 10**8, 0, 6, (strip, sent))(
-            mask, xb, r00, turned, tables, along_cols
-        )
-
     top, down, diag, r00, xb, kept = main(
         lambda *refs: main_kernel(True, *refs), (strip, shape(N + 8, N), quad, quad, rows, quad),
         left, right, lower, beside, corner,
     )
     above = shifted(down, 1, 0)
-    bottom, right_part = post(True, shape(2 * N + 8, H), xb, r00)
+    bottom, right_part = kernel(post_kernel, 10**8, 0, 6, (strip, shape(2 * N + 8, H)))(
+        mask, xb, r00, turned, tables, along_cols
+    )
     before = shifted(right_part, 0, 1)
     late = shifted(diag, 1, 1)
     left, right, vel_left, vel_right, q00, q00_corner, left_send, fix = kernel(
@@ -343,12 +342,11 @@
     up00 = shifted(q00, -1, 0)
     corner = shifted(q00_corner, -1, -1)
     beside = shifted(left_send, 0, -1)
-    top, down, diag, r00, xb = main(
-        lambda *refs: main_kernel(False, *refs), (strip, strip, quad, quad, rows),
+    top, down, diag, bottom, right_part = main(
+        lambda *refs: main_kernel(False, *refs), (strip, strip, quad, strip, half),
         left, right, up00, kept, fix, late, beside, corner,
     )
     above = shifted(down, 1, 0)
-    bottom, right_part = post(False, half, xb, r00)
     before = shifted(right_part, 0, 1)
     from_corner = shifted(diag, 1, 1)
     return kernel(final_kernel, 10**6, 0, 10, (shape(2, N, N), shape(2, N, N)))(

time: 69.1 us -> 66.1 us (0.957)
  waiting for transfers between devices: 20.9 us -> 18.8 us
    ppermute x12, waiting for transfers between devices: 20.9 us -> 18.8 us  [shifted(): return lax.ppermute(value, ('row', 'col'), pairs)]
where the time goes in v5:
time: 66.1 us; the launch traced here: 65.6 us
  starting transfers between devices  36.6 us (55%)
  waiting for transfers between devices  18.8 us (28%)
  Pallas kernels  7.64 us (12%)
  local copies, waits for them, and re-layouts  1.7 us (3%)
  between operations  0.86 us (1%)
    ppermute x12, starting transfers between devices, shifted(): return lax.ppermute(value, ('row', 'col'), pairs)  36.6 us
    ppermute x12, waiting for transfers between devices, shifted(): return lax.ppermute(value, ('row', 'col'), pairs)  18.8 us
    pallas_call x2, Pallas kernels, main(): kernel(body, 10 ** 9, 0, 1 + len(arrays) + len(rest), outs)  3.51 us
    pallas_call x1, Pallas kernels, steps(): kernel(prep_kernel, 10 ** 8, 3, 2, (shape(2, N, N), rows, shape(4, H, H,...  1.85 us
    unnamed x10, local copies, waits for them, and re-layouts  1.68 us
  transfers between devices with their start and end apart: 12, of which 6 were waited for; matrix products, arithmetic and copies ran while one was open for 0% of the time, Pallas kernels for 4%

profile of v5, /device:TPU:11, one launch (start us, length us, event | category | flops | bytes accessed | tf_op | source)
XLA Modules:
  0.0 65.6 jit_solution(9236290119655813211)
XLA Ops:
  0.6 1.0 %copy-done = f32[2,256,256]{2,1,0:T(8,128)S(1)} copy-done((f32[2,256,256]{2,1,0:T(8,128)S(1)}, f32[2,256,256]{2,1,0:T(8,128)}, u32[]{:S(2)}) %copy-start) | copy-done | bytes 524312
  1.7 0.1 shard_map.69
  1.7 0.0 copy-start.3
  1.7 2.7 %collective-permute-start.1 = (f32[2,256,128]{2,1,0:T(8,128)S(1)}, f32[2,256,128]{2,1,0:T(8,128)S(1)}, u32[]{:S(2)}, u32[]{:S(2)}) collective-permute-start(f32[2,256,128]{2,1,0:T(8,128)S(1)} %get-tuple-element.36), channel_id=1, source_target_pairs={{1,0},{2,1},{3,2},{4,3},{5,4},{6,5},{7,6},{9,8},{10,9},{11,10},{12... | collective-permute-start | bytes 786440 | tf_op jit(solution)/shard_map/ppermute | solution.py:30
  4.5 2.2 %collective-permute-start = (f32[2,128,256]{2,1,0:T(8,128)S(1)}, f32[2,128,256]{2,1,0:T(8,128)S(1)}, u32[]{:S(2)}, u32[]{:S(2)}) collective-permute-start(f32[2,128,256]{2,1,0:T(8,128)S(1)} %slice.3), channel_id=1, source_target_pairs={{8,0},{9,1},{10,2},{11,3},{12,4},{13,5},{14,6},{15,7},{16,8},{17,9... | collective-permute-start | bytes 786440 | tf_op jit(solution)/shard_map/ppermute | solution.py:30
  6.7 1.9 %collective-permute-start.2 = (f32[2,128,128]{2,1,0:T(8,128)S(1)}, f32[2,128,128]{2,1,0:T(8,128)S(1)}, u32[]{:S(2)}, u32[]{:S(2)}) collective-permute-start(f32[2,128,128]{2,1,0:T(8,128)S(1)} %get-tuple-element.37), channel_id=1, source_target_pairs={{9,0},{10,1},{11,2},{12,3},{13,4},{14,5},{15,6},{17,8},{18,9},{19,... | collective-permute-start | bytes 393224 | tf_op jit(solution)/shard_map/ppermute | solution.py:30
  8.6 0.0 copy-start.4
  8.6 0.6 copy-done.4
  9.3 1.9 %shard_map.68 = (f32[2,256,256]{2,1,0:T(8,128)S(1)}, f32[256,256]{1,0:T(8,128)S(1)}, s32[4,128,128]{2,1,0:T(8,128)S(1)}, bf16[4,256,256]{2,1,0:T(8,128)(2,1)S(1)...) custom-call(s32[2]{0:T(128)S(1)} %bitcast.5, s32[1]{0:T(128)} %bitcast.1.below_ref, s32[1]{0:T(128)} %bitcast.2.beside_ref, ...), custom_call_target="tpu_custom_call" | custom-call | flops 100000000 | bytes 1000000 | tf_op jit(solution)/shard_map/pallas_call | solution.py:312
  11.1 0.3 shard_map.70.refs_8_
  11.4 4.2 %collective-permute-done.2.refs_5_ = f32[2,128,128]{2,1,0:T(8,128)S(1)} collective-permute-done((f32[2,128,128]{2,1,0:T(8,128)S(1)}, f32[2,128,128]{2,1,0:T(8,128)S(1)}, u32[]{:S(2)}, u32[]{:S(2)}) %collective-permute-start.2) | collective-permute-done | bytes 131104 | tf_op jit(solution)/shard_map/ppermute | solution.py:30
  15.6 1.0 %collective-permute-done.refs_3_ = f32[2,128,256]{2,1,0:T(8,128)S(1)} collective-permute-done((f32[2,128,256]{2,1,0:T(8,128)S(1)}, f32[2,128,256]{2,1,0:T(8,128)S(1)}, u32[]{:S(2)}, u32[]{:S(2)}) %collective-permute-start) | collective-permute-done | bytes 262176 | tf_op jit(solution)/shard_map/ppermute | solution.py:30
  16.5 1.7 %shard_map.71 = (f32[2,128,256]{2,1,0:T(8,128)S(1)}, f32[264,256]{1,0:T(8,128)S(1)}, f32[2,128,128]{2,1,0:T(8,128)S(1)}, f32[2,128,128]{2,1,0:T(8,128)S(1)}, f32...) custom-call(s32[4,128,128]{2,1,0:T(8,128)S(1)} %get-tuple-element.33.mask_ref.refs_0_, ...), custom_call_target="tpu_custom_call" | custom-call | flops 1000000000 | bytes 1000000 | tf_op jit(solution)/shard_map/pallas_call | solution.py:327
  18.3 3.1 %collective-permute-start.3 = (f32[264,256]{1,0:T(8,128)S(1)}, f32[264,256]{1,0:T(8,128)S(1)}, u32[]{:S(2)}, u32[]{:S(2)}) collective-permute-start(f32[264,256]{1,0:T(8,128)S(1)} %get-tuple-element.47), channel_id=1, source_target_pairs={{0,8},{1,9},{2,10},{3,11},{4,12},{5,13},{6,14},{7,15},{8,16},{9,17... | collective-permute-start | bytes 811016 | tf_op jit(solution)/shard_map/ppermute | solution.py:30
  21.3 0.0 copy-start.2
  21.3 0.3 shard_map.72
  21.6 4.8 %collective-permute-start.4 = (f32[520,128]{1,0:T(8,128)S(1)}, f32[520,128]{1,0:T(8,128)S(1)}, u32[]{:S(2)}, u32[]{:S(2)}) collective-permute-start(f32[520,128]{1,0:T(8,128)S(1)} %get-tuple-element.48), channel_id=1, source_target_pairs={{0,1},{1,2},{2,3},{3,4},{4,5},{5,6},{6,7},{8,9},{9,10},{10,11},{11... | collective-permute-start | bytes 798728 | tf_op jit(solution)/shard_map/ppermute | solution.py:30
  26.5 3.3 %collective-permute-done.4.before_ref = f32[520,128]{1,0:T(8,128)S(1)} collective-permute-done((f32[520,128]{1,0:T(8,128)S(1)}, f32[520,128]{1,0:T(8,128)S(1)}, u32[]{:S(2)}, u32[]{:S(2)}) %collective-permute-start.4) | collective-permute-done | bytes 266272 | tf_op jit(solution)/shard_map/ppermute | solution.py:30
  29.8 0.2 shard_map.73
  30.0 3.2 %collective-permute-start.7 = (f32[2,256,128]{2,1,0:T(8,128)S(1)}, f32[2,256,128]{2,1,0:T(8,128)S(1)}, u32[]{:S(2)}, u32[]{:S(2)}) collective-permute-start(f32[2,256,128]{2,1,0:T(8,128)S(1)} %get-tuple-element.57), channel_id=1, source_target_pairs={{1,0},{2,1},{3,2},{4,3},{5,4},{6,5},{7,6},{9,8},{10,9},{11,10},{12... | collective-permute-start | bytes 786440 | tf_op jit(solution)/shard_map/ppermute | solution.py:30
  33.2 3.1 %collective-permute-start.6 = (f32[2,128,256]{2,1,0:T(8,128)S(1)}, f32[2,128,256]{2,1,0:T(8,128)S(1)}, u32[]{:S(2)}, u32[]{:S(2)}) collective-permute-start(f32[2,128,256]{2,1,0:T(8,128)S(1)} %get-tuple-element.54), channel_id=1, source_target_pairs={{8,0},{9,1},{10,2},{11,3},{12,4},{13,5},{14,6},{15,7},{16,8},{17,9... | collective-permute-start | bytes 786440 | tf_op jit(solution)/shard_map/ppermute | solution.py:30
  36.3 4.3 %collective-permute-start.5 = (f32[2,128,128]{2,1,0:T(8,128)S(1)}, f32[2,128,128]{2,1,0:T(8,128)S(1)}, u32[]{:S(2)}, u32[]{:S(2)}) collective-permute-start(f32[2,128,128]{2,1,0:T(8,128)S(1)} %get-tuple-element.53), channel_id=1, source_target_pairs={{0,9},{1,10},{2,11},{3,12},{4,13},{5,14},{6,15},{8,17},{9,18},{10,... | collective-permute-start | bytes 393224 | tf_op jit(solution)/shard_map/ppermute | solution.py:30
  40.6 1.9 %collective-permute-start.8 = (f32[2,128,128]{2,1,0:T(8,128)S(1)}, f32[2,128,128]{2,1,0:T(8,128)S(1)}, u32[]{:S(2)}, u32[]{:S(2)}) collective-permute-start(f32[2,128,128]{2,1,0:T(8,128)S(1)} %get-tuple-element.58), channel_id=1, source_target_pairs={{9,0},{10,1},{11,2},{12,3},{13,4},{14,5},{15,6},{17,8},{18,9},{19,... | collective-permute-start | bytes 393224 | tf_op jit(solution)/shard_map/ppermute | solution.py:30
  42.6 0.3 shard_map.74.refs_11_
  42.9 1.5 %collective-permute-done.5.refs_6_.late_ref = f32[2,128,128]{2,1,0:T(8,128)S(1)} collective-permute-done((f32[2,128,128]{2,1,0:T(8,128)S(1)}, f32[2,128,128]{2,1,0:T(8,128)S(1)}, u32[]{:S(2)}, u32[]{:S(2)}) %collective-permute-start.5) | collective-permute-done | bytes 131104 | tf_op jit(solution)/shard_map/ppermute | solution.py:30
  44.3 4.5 %collective-permute-done.8.refs_8_ = f32[2,128,128]{2,1,0:T(8,128)S(1)} collective-permute-done((f32[2,128,128]{2,1,0:T(8,128)S(1)}, f32[2,128,128]{2,1,0:T(8,128)S(1)}, u32[]{:S(2)}, u32[]{:S(2)}) %collective-permute-start.8) | collective-permute-done | bytes 131104 | tf_op jit(solution)/shard_map/ppermute | solution.py:30
  48.8 1.8 %shard_map.75 = (f32[2,128,256]{2,1,0:T(8,128)S(1)}, f32[2,128,256]{2,1,0:T(8,128)S(1)}, f32[2,128,128]{2,1,0:T(8,128)S(1)}, f32[2,128,256]{2,1,0:T(8,128)S(1)}, f32[2,256,128]{2,1,0:T(8,128)S(1)}) custom-call(s32[4,128,128]{2,1,0:T(8,128)S(1)} %get-tuple-element.33.mask_ref.refs_0_, f32[2,256,128]{2,1,0:T(8,128)S(1)} %get-tuple-element.49.left_ref.refs_1_, ...), custom_call_target="tpu_custom_call" | custom-call | flops 1000000000 | bytes 1000000 | tf_op jit(solution)/shard_map/pallas_call | solution.py:327
  50.6 3.9 %collective-permute-start.9 = (f32[2,128,256]{2,1,0:T(8,128)S(1)}, f32[2,128,256]{2,1,0:T(8,128)S(1)}, u32[]{:S(2)}, u32[]{:S(2)}) collective-permute-start(f32[2,128,256]{2,1,0:T(8,128)S(1)} %get-tuple-element.61), channel_id=1, source_target_pairs={{0,8},{1,9},{2,10},{3,11},{4,12},{5,13},{6,14},{7,15},{8,16},{9,17... | collective-permute-start | bytes 786440 | tf_op jit(solution)/shard_map/ppermute | solution.py:30
  54.6 2.2 %collective-permute-start.10 = (f32[2,256,128]{2,1,0:T(8,128)S(1)}, f32[2,256,128]{2,1,0:T(8,128)S(1)}, u32[]{:S(2)}, u32[]{:S(2)}) collective-permute-start(f32[2,256,128]{2,1,0:T(8,128)S(1)} %get-tuple-element.62), channel_id=1, source_target_pairs={{0,1},{1,2},{2,3},{3,4},{4,5},{5,6},{6,7},{8,9},{9,10},{10,11},{11... | collective-permute-start | bytes 786440 | tf_op jit(solution)/shard_map/ppermute | solution.py:30
  56.7 3.4 %collective-permute-start.11 = (f32[2,128,128]{2,1,0:T(8,128)S(1)}, f32[2,128,128]{2,1,0:T(8,128)S(1)}, u32[]{:S(2)}, u32[]{:S(2)}) collective-permute-start(f32[2,128,128]{2,1,0:T(8,128)S(1)} %get-tuple-element.63), channel_id=1, source_target_pairs={{0,9},{1,10},{2,11},{3,12},{4,13},{5,14},{6,15},{8,17},{9,18},{10,... | collective-permute-start | bytes 393224 | tf_op jit(solution)/shard_map/ppermute | solution.py:30
  60.1 4.3 %collective-permute-done.11.diag_ref = f32[2,128,128]{2,1,0:T(8,128)S(1)} collective-permute-done((f32[2,128,128]{2,1,0:T(8,128)S(1)}, f32[2,128,128]{2,1,0:T(8,128)S(1)}, u32[]{:S(2)}, u32[]{:S(2)}) %collective-permute-start.11) | collective-permute-done | bytes 131104 | tf_op jit(solution)/shard_map/ppermute | solution.py:30
  64.4 1.1 %shard_map.76 = (f32[2,256,256]{2,1,0:T(8,128)}, f32[2,256,256]{2,1,0:T(8,128)}) custom-call(f32[2,256,128]{2,1,0:T(8,128)S(1)} %get-tuple-element.49.left_ref.refs_1_, f32[2,256,128]{2,1,0:T(8,128)S(1)} %get-tuple-element.50.right_ref.refs_2_, f32[2,256,128]{2,1,0:T(8,128)S(1)} %get-tuple-element.51.vl_ref, f32[2,256,128]{2,1,0:T(8,128)S(1)} %get-tuple-element.52.vr_ref, ...), custom_call_target="tpu_custom_call" | custom-call | flops 1000000 | bytes 1000000 | tf_op jit(solution)/shard_map/pallas_call | solution.py:352
  (12 shorter events, 0.0 us)
Async XLA Ops:
  0.6 1.0 %copy-start = (f32[2,256,256]{2,1,0:T(8,128)S(1)}, f32[2,256,256]{2,1,0:T(8,128)}, u32[]{:S(2)}) copy-start(f32[2,256,256]{2,1,0:T(8,128)} %obj_ref.1) | copy-start | bytes 1572868
  1.7 7.0 %copy-start.1 = (f32[2,256,256]{2,1,0:T(8,128)S(1)}, f32[2,256,256]{2,1,0:T(8,128)}, u32[]{:S(2)}) copy-start(f32[2,256,256]{2,1,0:T(8,128)} %probe_ref.1) | copy-start | bytes 1572868
  1.7 6.9 %copy-start.3 = (f32[1,1,1,256,256]{4,3,2,1,0:T(8,128)S(1)}, f32[1,1,1,256,256]{4,3,2,1,0:T(8,128)}, u32[]{:S(2)}) copy-start(f32[1,1,1,256,256]{4,3,2,1,0:T(8,128)} %param.8) | copy-start | bytes 786436
  1.7 9.4 %collective-permute-start.1 = (f32[2,256,128]{2,1,0:T(8,128)S(1)}, f32[2,256,128]{2,1,0:T(8,128)S(1)}, u32[]{:S(2)}, u32[]{:S(2)}) collective-permute-start(f32[2,256,128]{2,1,0:T(8,128)S(1)} %get-tuple-element.36), channel_id=1, source_target_pairs={{1,0},{2,1},{3,2},{4,3},{5,4},{6,5},{7,6},{9,8},{10,9},{11,10},{12... | collective-permute-start | bytes 786440 | tf_op jit(solution)/shard_map/ppermute | solution.py:30
  4.5 12.0 %collective-permute-start = (f32[2,128,256]{2,1,0:T(8,128)S(1)}, f32[2,128,256]{2,1,0:T(8,128)S(1)}, u32[]{:S(2)}, u32[]{:S(2)}) collective-permute-start(f32[2,128,256]{2,1,0:T(8,128)S(1)} %slice.3), channel_id=1, source_target_pairs={{8,0},{9,1},{10,2},{11,3},{12,4},{13,5},{14,6},{15,7},{16,8},{17,9... | collective-permute-start | bytes 786440 | tf_op jit(solution)/shard_map/ppermute | solution.py:30
  6.7 8.9 %collective-permute-start.2 = (f32[2,128,128]{2,1,0:T(8,128)S(1)}, f32[2,128,128]{2,1,0:T(8,128)S(1)}, u32[]{:S(2)}, u32[]{:S(2)}) collective-permute-start(f32[2,128,128]{2,1,0:T(8,128)S(1)} %get-tuple-element.37), channel_id=1, source_target_pairs={{9,0},{10,1},{11,2},{12,3},{13,4},{14,5},{15,6},{17,8},{18,9},{19,... | collective-permute-start | bytes 393224 | tf_op jit(solution)/shard_map/ppermute | solution.py:30
  8.6 0.7 %copy-start.4 = (s32[1,1,1,2]{3,2,1,0:T(1,128)S(1)}, s32[1,1,1,2]{3,2,1,0:T(1,128)}, u32[]{:S(2)}) copy-start(s32[1,1,1,2]{3,2,1,0:T(1,128)} %param.7) | copy-start | bytes 28
  18.3 11.6 %collective-permute-start.3 = (f32[264,256]{1,0:T(8,128)S(1)}, f32[264,256]{1,0:T(8,128)S(1)}, u32[]{:S(2)}, u32[]{:S(2)}) collective-permute-start(f32[264,256]{1,0:T(8,128)S(1)} %get-tuple-element.47), channel_id=1, source_target_pairs={{0,8},{1,9},{2,10},{3,11},{4,12},{5,13},{6,14},{7,15},{8,16},{9,17... | collective-permute-start | bytes 811016 | tf_op jit(solution)/shard_map/ppermute | solution.py:30
  21.3 8.5 %copy-start.2 = (f32[2,256,256]{2,1,0:T(8,128)S(1)}, f32[2,256,256]{2,1,0:T(8,128)}, u32[]{:S(2)}) copy-start(f32[2,256,256]{2,1,0:T(8,128)} %vel_ref.1) | copy-start | bytes 1572868
  21.6 8.2 %collective-permute-start.4 = (f32[520,128]{1,0:T(8,128)S(1)}, f32[520,128]{1,0:T(8,128)S(1)}, u32[]{:S(2)}, u32[]{:S(2)}) collective-permute-start(f32[520,128]{1,0:T(8,128)S(1)} %get-tuple-element.48), channel_id=1, source_target_pairs={{0,1},{1,2},{2,3},{3,4},{4,5},{5,6},{6,7},{8,9},{9,10},{10,11},{11... | collective-permute-start | bytes 798728 | tf_op jit(solution)/shard_map/ppermute | solution.py:30
  30.0 12.5 %collective-permute-start.7 = (f32[2,256,128]{2,1,0:T(8,128)S(1)}, f32[2,256,128]{2,1,0:T(8,128)S(1)}, u32[]{:S(2)}, u32[]{:S(2)}) collective-permute-start(f32[2,256,128]{2,1,0:T(8,128)S(1)} %get-tuple-element.57), channel_id=1, source_target_pairs={{1,0},{2,1},{3,2},{4,3},{5,4},{6,5},{7,6},{9,8},{10,9},{11,10},{12... | collective-permute-start | bytes 786440 | tf_op jit(solution)/shard_map/ppermute | solution.py:30
  33.2 15.6 %collective-permute-start.6 = (f32[2,128,256]{2,1,0:T(8,128)S(1)}, f32[2,128,256]{2,1,0:T(8,128)S(1)}, u32[]{:S(2)}, u32[]{:S(2)}) collective-permute-start(f32[2,128,256]{2,1,0:T(8,128)S(1)} %get-tuple-element.54), channel_id=1, source_target_pairs={{8,0},{9,1},{10,2},{11,3},{12,4},{13,5},{14,6},{15,7},{16,8},{17,9... | collective-permute-start | bytes 786440 | tf_op jit(solution)/shard_map/ppermute | solution.py:30
  36.3 8.0 %collective-permute-start.5 = (f32[2,128,128]{2,1,0:T(8,128)S(1)}, f32[2,128,128]{2,1,0:T(8,128)S(1)}, u32[]{:S(2)}, u32[]{:S(2)}) collective-permute-start(f32[2,128,128]{2,1,0:T(8,128)S(1)} %get-tuple-element.53), channel_id=1, source_target_pairs={{0,9},{1,10},{2,11},{3,12},{4,13},{5,14},{6,15},{8,17},{9,18},{10,... | collective-permute-start | bytes 393224 | tf_op jit(solution)/shard_map/ppermute | solution.py:30
  40.6 8.2 %collective-permute-start.8 = (f32[2,128,128]{2,1,0:T(8,128)S(1)}, f32[2,128,128]{2,1,0:T(8,128)S(1)}, u32[]{:S(2)}, u32[]{:S(2)}) collective-permute-start(f32[2,128,128]{2,1,0:T(8,128)S(1)} %get-tuple-element.58), channel_id=1, source_target_pairs={{9,0},{10,1},{11,2},{12,3},{13,4},{14,5},{15,6},{17,8},{18,9},{19,... | collective-permute-start | bytes 393224 | tf_op jit(solution)/shard_map/ppermute | solution.py:30
  50.6 13.8 %collective-permute-start.9 = (f32[2,128,256]{2,1,0:T(8,128)S(1)}, f32[2,128,256]{2,1,0:T(8,128)S(1)}, u32[]{:S(2)}, u32[]{:S(2)}) collective-permute-start(f32[2,128,256]{2,1,0:T(8,128)S(1)} %get-tuple-element.61), channel_id=1, source_target_pairs={{0,8},{1,9},{2,10},{3,11},{4,12},{5,13},{6,14},{7,15},{8,16},{9,17... | collective-permute-start | bytes 786440 | tf_op jit(solution)/shard_map/ppermute | solution.py:30
  54.6 9.9 %collective-permute-start.10 = (f32[2,256,128]{2,1,0:T(8,128)S(1)}, f32[2,256,128]{2,1,0:T(8,128)S(1)}, u32[]{:S(2)}, u32[]{:S(2)}) collective-permute-start(f32[2,256,128]{2,1,0:T(8,128)S(1)} %get-tuple-element.62), channel_id=1, source_target_pairs={{0,1},{1,2},{2,3},{3,4},{4,5},{5,6},{6,7},{8,9},{9,10},{10,11},{11... | collective-permute-start | bytes 786440 | tf_op jit(solution)/shard_map/ppermute | solution.py:30
  56.7 7.7 %collective-permute-start.11 = (f32[2,128,128]{2,1,0:T(8,128)S(1)}, f32[2,128,128]{2,1,0:T(8,128)S(1)}, u32[]{:S(2)}, u32[]{:S(2)}) collective-permute-start(f32[2,128,128]{2,1,0:T(8,128)S(1)} %get-tuple-element.63), channel_id=1, source_target_pairs={{0,9},{1,10},{2,11},{3,12},{4,13},{5,14},{6,15},{8,17},{9,18},{10,... | collective-permute-start | bytes 393224 | tf_op jit(solution)/shard_map/ppermute | solution.py:30

commit v6 on v5

--- a/solution.py
+++ b/solution.py
@@ -240,31 +240,43 @@
     return obj - step_size * vel, vel
 
 
+def arrived(above_ref, before_ref):
+    row_id = lax.broadcasted_iota(jnp.int32, (H, H), 0).astype(jnp.float32)
+    return above_ref[2 * H : 2 * H + 1, :H] < 0.5, row_id >= before_ref[2 * N : 2 * N + 1]
+
+
+def gradients(part, masks_of, top_ref, bottom_ref, above_ref, before_ref):
+    ours_above, ours_before = masks_of
+    above, before = above_ref[part * H : (part + 1) * H], before_ref[part * N : (part + 1) * N]
+    g00 = (top_ref[part, :, :H] + jnp.where(ours_above, above[:, :H], 0.0)) + jnp.where(ours_before, before[:H], 0.0)
+    return g00, top_ref[part, :, H:] + above[:, H:], bottom_ref[part, :, :H] + before[H:], bottom_ref[part, :, H:]
+
+
+def send_kernel(left_ref, right_ref, vel_ref, top_ref, bottom_ref, above_ref, before_ref, up_out, corner_out, send_out):
+    ours = arrived(above_ref, before_ref)
+    for part in range(2):
+        g00, g01, g10, _ = gradients(part, ours, top_ref, bottom_ref, above_ref, before_ref)
+        obj, _ = stepped(left_ref[part, :H], vel_ref[part, :H, :H], g00)
+        up_out[part, :, :H], corner_out[part], send_out[part, :H] = obj, obj, obj
+        up_out[part, :, H:], _ = stepped(right_ref[part, :H], vel_ref[part, :H, H:], g01)
+        send_out[part, H:], _ = stepped(left_ref[part, H:], vel_ref[part, H:, :H], g10)
+
+
 def update_kernel(
     mask_ref, left_ref, right_ref, vel_ref, top_ref, bottom_ref, above_ref, before_ref,
-    left_out, right_out, vl_out, vr_out, up_out, corner_out, send_out, fix_out,
+    left_out, right_out, vl_out, vr_out, fix_out,
 ):
-    row_id = lax.broadcasted_iota(jnp.int32, (H, H), 0).astype(jnp.float32)
-    ours_above = above_ref[2 * H : 2 * H + 1, :H] < 0.5
-    ours_before = row_id >= before_ref[2 * N : 2 * N + 1]
-    for part in range(2):
-        above, before = above_ref[part * H : (part + 1) * H], before_ref[part * N : (part + 1) * N]
-        g00 = (top_ref[part, :, :H] + jnp.where(ours_above, above[:, :H], 0.0)) + jnp.where(ours_before, before[:H], 0.0)
-        g01 = top_ref[part, :, H:] + above[:, H:]
-        g10 = bottom_ref[part, :, :H] + before[H:]
-        g11 = bottom_ref[part, :, H:]
-        obj, vel = stepped(left_ref[part, :H], vel_ref[part, :H, :H], g00)
-        left_out[part, :H], vl_out[part, :H] = obj, vel
-        up_out[part, :, :H], corner_out[part], send_out[part, :H] = obj, obj, obj
-        obj, vel = stepped(right_ref[part, :H], vel_ref[part, :H, H:], g01)
-        right_out[part, :H], vr_out[part, :H], up_out[part, :, H:] = obj, vel, obj
-        obj, vel = stepped(left_ref[part, H:], vel_ref[part, H:, :H], g10)
-        left_out[part, H:], vl_out[part, H:], send_out[part, H:] = obj, vel, obj
+    ours_above, ours_before = ours = arrived(above_ref, before_ref)
+    for part in range(2):
+        g00, g01, g10, g11 = gradients(part, ours, top_ref, bottom_ref, above_ref, before_ref)
+        left_out[part, :H], vl_out[part, :H] = stepped(left_ref[part, :H], vel_ref[part, :H, :H], g00)
+        left_out[part, H:], vl_out[part, H:] = stepped(left_ref[part, H:], vel_ref[part, H:, :H], g10)
+        right_out[part, :H], vr_out[part, :H] = stepped(right_ref[part, :H], vel_ref[part, :H, H:], g01)
         right_out[part, H:], vr_out[part, H:] = stepped(right_ref[part, H:], vel_ref[part, H:, H:], g11)
         scale = mask_ref[2].astype(jnp.float32) * step_size
-        fix_out[part, :, :H] = scale * jnp.where(ours_before, 0.0, before[:H])
+        fix_out[part, :, :H] = scale * jnp.where(ours_before, 0.0, before_ref[part * N : part * N + H])
         scale = mask_ref[3].astype(jnp.float32) * step_size
-        fix_out[part, :, H:] = scale * jnp.where(ours_above, 0.0, above[:, :H])
+        fix_out[part, :, H:] = scale * jnp.where(ours_above, 0.0, above_ref[part * H : (part + 1) * H, :H])
 
 
 def final_kernel(
@@ -336,15 +348,18 @@
     )
     before = shifted(right_part, 0, 1)
     late = shifted(diag, 1, 1)
-    left, right, vel_left, vel_right, q00, q00_corner, left_send, fix = kernel(
-        update_kernel, 10**6, 0, 8, (half, half, half, half, strip, quad, half, strip)
+    up_send, q00, left_send = kernel(send_kernel, 10**6, 0, 7, (strip, quad, half))(
+        left, right, velocity, top, bottom, above, before
+    )
+    lower = shifted(up_send, -1, 0)
+    beside = shifted(left_send, 0, -1)
+    corner = shifted(q00, -1, -1)
+    left, right, vel_left, vel_right, fix = kernel(
+        update_kernel, 10**6, 0, 8, (half, half, half, half, strip)
     )(mask, left, right, velocity, top, bottom, above, before)
-    up00 = shifted(q00, -1, 0)
-    corner = shifted(q00_corner, -1, -1)
-    beside = shifted(left_send, 0, -1)
     top, down, diag, bottom, right_part = main(
         lambda *refs: main_kernel(False, *refs), (strip, strip, quad, strip, half),
-        left, right, up00, kept, fix, late, beside, corner,
+        left, right, lower, kept, fix, late, beside, corner,
     )
     above = shifted(down, 1, 0)
     before = shifted(right_part, 0, 1)

time: 66.1 us -> 66 us (level)
  no operation moved by 1% of the time
where the time goes in v6:
time: 66 us; the launch traced here: 65.5 us
  starting transfers between devices  36.6 us (55%)
  waiting for transfers between devices  18.5 us (28%)
  Pallas kernels  7.75 us (12%)
  local copies, waits for them, and re-layouts  1.7 us (3%)
  between operations  0.86 us (1%)
    ppermute x12, starting transfers between devices, shifted(): return lax.ppermute(value, ('row', 'col'), pairs)  36.6 us
    ppermute x12, waiting for transfers between devices, shifted(): return lax.ppermute(value, ('row', 'col'), pairs)  18.5 us
    pallas_call x2, Pallas kernels, main(): kernel(body, 10 ** 9, 0, 1 + len(arrays) + len(rest), outs)  3.48 us
    pallas_call x1, Pallas kernels, steps(): kernel(prep_kernel, 10 ** 8, 3, 2, (shape(2, N, N), rows, shape(4, H, H,...  1.85 us
    unnamed x10, local copies, waits for them, and re-layouts  1.68 us
  transfers between devices with their start and end apart: 12, of which 6 were waited for; matrix products, arithmetic and copies ran while one was open for 0% of the time, Pallas kernels for 4%

profile of v6, /device:TPU:11, one launch (start us, length us, event | category | flops | bytes accessed | tf_op | source)
XLA Modules:
  0.0 65.5 jit_solution(11772160259794224276)
XLA Ops:
  0.6 1.0 %copy-done.1 = f32[2,256,256]{2,1,0:T(8,128)S(1)} copy-done((f32[2,256,256]{2,1,0:T(8,128)S(1)}, f32[2,256,256]{2,1,0:T(8,128)}, u32[]{:S(2)}) %copy-start.1) | copy-done | bytes 524312
  1.7 0.1 shard_map.69
  1.7 0.0 copy-start.3
  1.7 2.7 %collective-permute-start.1 = (f32[2,256,128]{2,1,0:T(8,128)S(1)}, f32[2,256,128]{2,1,0:T(8,128)S(1)}, u32[]{:S(2)}, u32[]{:S(2)}) collective-permute-start(f32[2,256,128]{2,1,0:T(8,128)S(1)} %get-tuple-element.36), channel_id=1, source_target_pairs={{1,0},{2,1},{3,2},{4,3},{5,4},{6,5},{7,6},{9,8},{10,9},{11,10},{12... | collective-permute-start | bytes 786440 | tf_op jit(solution)/shard_map/ppermute | solution.py:30
  4.5 2.2 %collective-permute-start = (f32[2,128,256]{2,1,0:T(8,128)S(1)}, f32[2,128,256]{2,1,0:T(8,128)S(1)}, u32[]{:S(2)}, u32[]{:S(2)}) collective-permute-start(f32[2,128,256]{2,1,0:T(8,128)S(1)} %slice.3), channel_id=1, source_target_pairs={{8,0},{9,1},{10,2},{11,3},{12,4},{13,5},{14,6},{15,7},{16,8},{17,9... | collective-permute-start | bytes 786440 | tf_op jit(solution)/shard_map/ppermute | solution.py:30
  6.7 1.9 %collective-permute-start.2 = (f32[2,128,128]{2,1,0:T(8,128)S(1)}, f32[2,128,128]{2,1,0:T(8,128)S(1)}, u32[]{:S(2)}, u32[]{:S(2)}) collective-permute-start(f32[2,128,128]{2,1,0:T(8,128)S(1)} %get-tuple-element.37), channel_id=1, source_target_pairs={{9,0},{10,1},{11,2},{12,3},{13,4},{14,5},{15,6},{17,8},{18,9},{19,... | collective-permute-start | bytes 393224 | tf_op jit(solution)/shard_map/ppermute | solution.py:30
  8.6 0.0 copy-start.4
  8.6 0.6 copy-done.4
  9.3 1.9 %shard_map.68 = (f32[2,256,256]{2,1,0:T(8,128)S(1)}, f32[256,256]{1,0:T(8,128)S(1)}, s32[4,128,128]{2,1,0:T(8,128)S(1)}, bf16[4,256,256]{2,1,0:T(8,128)(2,1)S(1)...) custom-call(s32[2]{0:T(128)S(1)} %bitcast.5, s32[1]{0:T(128)} %bitcast.1.below_ref, s32[1]{0:T(128)} %bitcast.2.beside_ref, ...), custom_call_target="tpu_custom_call" | custom-call | flops 100000000 | bytes 1000000 | tf_op jit(solution)/shard_map/pallas_call | solution.py:324
  11.1 0.3 shard_map.70.refs_8_
  11.4 4.2 %collective-permute-done.2.refs_5_ = f32[2,128,128]{2,1,0:T(8,128)S(1)} collective-permute-done((f32[2,128,128]{2,1,0:T(8,128)S(1)}, f32[2,128,128]{2,1,0:T(8,128)S(1)}, u32[]{:S(2)}, u32[]{:S(2)}) %collective-permute-start.2) | collective-permute-done | bytes 131104 | tf_op jit(solution)/shard_map/ppermute | solution.py:30
  15.6 1.0 %collective-permute-done.refs_3_ = f32[2,128,256]{2,1,0:T(8,128)S(1)} collective-permute-done((f32[2,128,256]{2,1,0:T(8,128)S(1)}, f32[2,128,256]{2,1,0:T(8,128)S(1)}, u32[]{:S(2)}, u32[]{:S(2)}) %collective-permute-start) | collective-permute-done | bytes 262176 | tf_op jit(solution)/shard_map/ppermute | solution.py:30
  16.5 1.7 %shard_map.71 = (f32[2,128,256]{2,1,0:T(8,128)S(1)}, f32[264,256]{1,0:T(8,128)S(1)}, f32[2,128,128]{2,1,0:T(8,128)S(1)}, f32[2,128,128]{2,1,0:T(8,128)S(1)}, f32...) custom-call(s32[4,128,128]{2,1,0:T(8,128)S(1)} %get-tuple-element.33.mask_ref.refs_0_, ...), custom_call_target="tpu_custom_call" | custom-call | flops 1000000000 | bytes 1000000 | tf_op jit(solution)/shard_map/pallas_call | solution.py:339
  18.3 3.1 %collective-permute-start.3 = (f32[264,256]{1,0:T(8,128)S(1)}, f32[264,256]{1,0:T(8,128)S(1)}, u32[]{:S(2)}, u32[]{:S(2)}) collective-permute-start(f32[264,256]{1,0:T(8,128)S(1)} %get-tuple-element.47), channel_id=1, source_target_pairs={{0,8},{1,9},{2,10},{3,11},{4,12},{5,13},{6,14},{7,15},{8,16},{9,17... | collective-permute-start | bytes 811016 | tf_op jit(solution)/shard_map/ppermute | solution.py:30
  21.3 0.3 shard_map.72
  21.7 4.8 %collective-permute-start.4 = (f32[520,128]{1,0:T(8,128)S(1)}, f32[520,128]{1,0:T(8,128)S(1)}, u32[]{:S(2)}, u32[]{:S(2)}) collective-permute-start(f32[520,128]{1,0:T(8,128)S(1)} %get-tuple-element.48), channel_id=1, source_target_pairs={{0,1},{1,2},{2,3},{3,4},{4,5},{5,6},{6,7},{8,9},{9,10},{10,11},{11... | collective-permute-start | bytes 798728 | tf_op jit(solution)/shard_map/ppermute | solution.py:30
  26.5 3.3 %collective-permute-done.4.before_ref = f32[520,128]{1,0:T(8,128)S(1)} collective-permute-done((f32[520,128]{1,0:T(8,128)S(1)}, f32[520,128]{1,0:T(8,128)S(1)}, u32[]{:S(2)}, u32[]{:S(2)}) %collective-permute-start.4) | collective-permute-done | bytes 266272 | tf_op jit(solution)/shard_map/ppermute | solution.py:30
  29.8 0.1 shard_map.74
  29.9 3.2 %collective-permute-start.7 = (f32[2,256,128]{2,1,0:T(8,128)S(1)}, f32[2,256,128]{2,1,0:T(8,128)S(1)}, u32[]{:S(2)}, u32[]{:S(2)}) collective-permute-start(f32[2,256,128]{2,1,0:T(8,128)S(1)} %get-tuple-element.57), channel_id=1, source_target_pairs={{1,0},{2,1},{3,2},{4,3},{5,4},{6,5},{7,6},{9,8},{10,9},{11,10},{12... | collective-permute-start | bytes 786440 | tf_op jit(solution)/shard_map/ppermute | solution.py:30
  33.2 3.1 %collective-permute-start.6 = (f32[2,128,256]{2,1,0:T(8,128)S(1)}, f32[2,128,256]{2,1,0:T(8,128)S(1)}, u32[]{:S(2)}, u32[]{:S(2)}) collective-permute-start(f32[2,128,256]{2,1,0:T(8,128)S(1)} %get-tuple-element.54), channel_id=1, source_target_pairs={{8,0},{9,1},{10,2},{11,3},{12,4},{13,5},{14,6},{15,7},{16,8},{17,9... | collective-permute-start | bytes 786440 | tf_op jit(solution)/shard_map/ppermute | solution.py:30
  36.2 4.3 %collective-permute-start.5 = (f32[2,128,128]{2,1,0:T(8,128)S(1)}, f32[2,128,128]{2,1,0:T(8,128)S(1)}, u32[]{:S(2)}, u32[]{:S(2)}) collective-permute-start(f32[2,128,128]{2,1,0:T(8,128)S(1)} %get-tuple-element.53), channel_id=1, source_target_pairs={{0,9},{1,10},{2,11},{3,12},{4,13},{5,14},{6,15},{8,17},{9,18},{10,... | collective-permute-start | bytes 393224 | tf_op jit(solution)/shard_map/ppermute | solution.py:30
  40.5 1.9 %collective-permute-start.8 = (f32[2,128,128]{2,1,0:T(8,128)S(1)}, f32[2,128,128]{2,1,0:T(8,128)S(1)}, u32[]{:S(2)}, u32[]{:S(2)}) collective-permute-start(f32[2,128,128]{2,1,0:T(8,128)S(1)} %get-tuple-element.58), channel_id=1, source_target_pairs={{9,0},{10,1},{11,2},{12,3},{13,4},{14,5},{15,6},{17,8},{18,9},{19,... | collective-permute-start | bytes 393224 | tf_op jit(solution)/shard_map/ppermute | solution.py:30
  42.5 0.2 shard_map.73
  42.7 0.3 shard_map.75.refs_11_
  43.0 1.2 %collective-permute-done.5.refs_6_.late_ref = f32[2,128,128]{2,1,0:T(8,128)S(1)} collective-permute-done((f32[2,128,128]{2,1,0:T(8,128)S(1)}, f32[2,128,128]{2,1,0:T(8,128)S(1)}, u32[]{:S(2)}, u32[]{:S(2)}) %collective-permute-start.5) | collective-permute-done | bytes 131104 | tf_op jit(solution)/shard_map/ppermute | solution.py:30
  44.2 4.5 %collective-permute-done.8.refs_8_ = f32[2,128,128]{2,1,0:T(8,128)S(1)} collective-permute-done((f32[2,128,128]{2,1,0:T(8,128)S(1)}, f32[2,128,128]{2,1,0:T(8,128)S(1)}, u32[]{:S(2)}, u32[]{:S(2)}) %collective-permute-start.8) | collective-permute-done | bytes 131104 | tf_op jit(solution)/shard_map/ppermute | solution.py:30
  48.7 1.8 %shard_map.76 = (f32[2,128,256]{2,1,0:T(8,128)S(1)}, f32[2,128,256]{2,1,0:T(8,128)S(1)}, f32[2,128,128]{2,1,0:T(8,128)S(1)}, f32[2,128,256]{2,1,0:T(8,128)S(1)}, f32[2,256,128]{2,1,0:T(8,128)S(1)}) custom-call(s32[4,128,128]{2,1,0:T(8,128)S(1)} %get-tuple-element.33.mask_ref.refs_0_, f32[2,256,128]{2,1,0:T(8,128)S(1)} %get-tuple-element.49.left_ref.refs_1_, ...), custom_call_target="tpu_custom_call" | custom-call | flops 1000000000 | bytes 1000000 | tf_op jit(solution)/shard_map/pallas_call | solution.py:339
  50.5 3.9 %collective-permute-start.9 = (f32[2,128,256]{2,1,0:T(8,128)S(1)}, f32[2,128,256]{2,1,0:T(8,128)S(1)}, u32[]{:S(2)}, u32[]{:S(2)}) collective-permute-start(f32[2,128,256]{2,1,0:T(8,128)S(1)} %get-tuple-element.61), channel_id=1, source_target_pairs={{0,8},{1,9},{2,10},{3,11},{4,12},{5,13},{6,14},{7,15},{8,16},{9,17... | collective-permute-start | bytes 786440 | tf_op jit(solution)/shard_map/ppermute | solution.py:30
  54.5 2.2 %collective-permute-start.10 = (f32[2,256,128]{2,1,0:T(8,128)S(1)}, f32[2,256,128]{2,1,0:T(8,128)S(1)}, u32[]{:S(2)}, u32[]{:S(2)}) collective-permute-start(f32[2,256,128]{2,1,0:T(8,128)S(1)} %get-tuple-element.62), channel_id=1, source_target_pairs={{0,1},{1,2},{2,3},{3,4},{4,5},{5,6},{6,7},{8,9},{9,10},{10,11},{11... | collective-permute-start | bytes 786440 | tf_op jit(solution)/shard_map/ppermute | solution.py:30
  56.6 3.4 %collective-permute-start.11 = (f32[2,128,128]{2,1,0:T(8,128)S(1)}, f32[2,128,128]{2,1,0:T(8,128)S(1)}, u32[]{:S(2)}, u32[]{:S(2)}) collective-permute-start(f32[2,128,128]{2,1,0:T(8,128)S(1)} %get-tuple-element.63), channel_id=1, source_target_pairs={{0,9},{1,10},{2,11},{3,12},{4,13},{5,14},{6,15},{8,17},{9,18},{10,... | collective-permute-start | bytes 393224 | tf_op jit(solution)/shard_map/ppermute | solution.py:30
  60.0 4.3 %collective-permute-done.11.diag_ref = f32[2,128,128]{2,1,0:T(8,128)S(1)} collective-permute-done((f32[2,128,128]{2,1,0:T(8,128)S(1)}, f32[2,128,128]{2,1,0:T(8,128)S(1)}, u32[]{:S(2)}, u32[]{:S(2)}) %collective-permute-start.11) | collective-permute-done | bytes 131104 | tf_op jit(solution)/shard_map/ppermute | solution.py:30
  64.3 1.1 %shard_map.77 = (f32[2,256,256]{2,1,0:T(8,128)}, f32[2,256,256]{2,1,0:T(8,128)}) custom-call(f32[2,256,128]{2,1,0:T(8,128)S(1)} %get-tuple-element.49.left_ref.refs_1_, f32[2,256,128]{2,1,0:T(8,128)S(1)} %get-tuple-element.50.right_ref.refs_2_, f32[2,256,128]{2,1,0:T(8,128)S(1)} %get-tuple-element.51.vl_ref, f32[2,256,128]{2,1,0:T(8,128)S(1)} %get-tuple-element.52.vr_ref, ...), custom_call_target="tpu_custom_call" | custom-call | flops 1000000 | bytes 1000000 | tf_op jit(solution)/shard_map/pallas_call | solution.py:367
  (13 shorter events, 0.0 us)
Async XLA Ops:
  0.6 1.0 %copy-start.1 = (f32[2,256,256]{2,1,0:T(8,128)S(1)}, f32[2,256,256]{2,1,0:T(8,128)}, u32[]{:S(2)}) copy-start(f32[2,256,256]{2,1,0:T(8,128)} %obj_ref.1) | copy-start | bytes 1572868
  1.7 7.0 %copy-start.2 = (f32[2,256,256]{2,1,0:T(8,128)S(1)}, f32[2,256,256]{2,1,0:T(8,128)}, u32[]{:S(2)}) copy-start(f32[2,256,256]{2,1,0:T(8,128)} %probe_ref.1) | copy-start | bytes 1572868
  1.7 6.9 %copy-start.3 = (f32[1,1,1,256,256]{4,3,2,1,0:T(8,128)S(1)}, f32[1,1,1,256,256]{4,3,2,1,0:T(8,128)}, u32[]{:S(2)}) copy-start(f32[1,1,1,256,256]{4,3,2,1,0:T(8,128)} %param.8) | copy-start | bytes 786436
  1.7 9.4 %collective-permute-start.1 = (f32[2,256,128]{2,1,0:T(8,128)S(1)}, f32[2,256,128]{2,1,0:T(8,128)S(1)}, u32[]{:S(2)}, u32[]{:S(2)}) collective-permute-start(f32[2,256,128]{2,1,0:T(8,128)S(1)} %get-tuple-element.36), channel_id=1, source_target_pairs={{1,0},{2,1},{3,2},{4,3},{5,4},{6,5},{7,6},{9,8},{10,9},{11,10},{12... | collective-permute-start | bytes 786440 | tf_op jit(solution)/shard_map/ppermute | solution.py:30
  4.5 12.0 %collective-permute-start = (f32[2,128,256]{2,1,0:T(8,128)S(1)}, f32[2,128,256]{2,1,0:T(8,128)S(1)}, u32[]{:S(2)}, u32[]{:S(2)}) collective-permute-start(f32[2,128,256]{2,1,0:T(8,128)S(1)} %slice.3), channel_id=1, source_target_pairs={{8,0},{9,1},{10,2},{11,3},{12,4},{13,5},{14,6},{15,7},{16,8},{17,9... | collective-permute-start | bytes 786440 | tf_op jit(solution)/shard_map/ppermute | solution.py:30
  6.7 8.9 %collective-permute-start.2 = (f32[2,128,128]{2,1,0:T(8,128)S(1)}, f32[2,128,128]{2,1,0:T(8,128)S(1)}, u32[]{:S(2)}, u32[]{:S(2)}) collective-permute-start(f32[2,128,128]{2,1,0:T(8,128)S(1)} %get-tuple-element.37), channel_id=1, source_target_pairs={{9,0},{10,1},{11,2},{12,3},{13,4},{14,5},{15,6},{17,8},{18,9},{19,... | collective-permute-start | bytes 393224 | tf_op jit(solution)/shard_map/ppermute | solution.py:30
  8.6 0.7 %copy-start.4 = (s32[1,1,1,2]{3,2,1,0:T(1,128)S(1)}, s32[1,1,1,2]{3,2,1,0:T(1,128)}, u32[]{:S(2)}) copy-start(s32[1,1,1,2]{3,2,1,0:T(1,128)} %param.7) | copy-start | bytes 28
  18.3 11.6 %collective-permute-start.3 = (f32[264,256]{1,0:T(8,128)S(1)}, f32[264,256]{1,0:T(8,128)S(1)}, u32[]{:S(2)}, u32[]{:S(2)}) collective-permute-start(f32[264,256]{1,0:T(8,128)S(1)} %get-tuple-element.47), channel_id=1, source_target_pairs={{0,8},{1,9},{2,10},{3,11},{4,12},{5,13},{6,14},{7,15},{8,16},{9,17... | collective-permute-start | bytes 811016 | tf_op jit(solution)/shard_map/ppermute | solution.py:30
  21.3 8.5 %copy-start = (f32[2,256,256]{2,1,0:T(8,128)S(1)}, f32[2,256,256]{2,1,0:T(8,128)}, u32[]{:S(2)}) copy-start(f32[2,256,256]{2,1,0:T(8,128)} %vel_ref.3) | copy-start | bytes 1572868
  21.7 8.2 %collective-permute-start.4 = (f32[520,128]{1,0:T(8,128)S(1)}, f32[520,128]{1,0:T(8,128)S(1)}, u32[]{:S(2)}, u32[]{:S(2)}) collective-permute-start(f32[520,128]{1,0:T(8,128)S(1)} %get-tuple-element.48), channel_id=1, source_target_pairs={{0,1},{1,2},{2,3},{3,4},{4,5},{5,6},{6,7},{8,9},{9,10},{10,11},{11... | collective-permute-start | bytes 798728 | tf_op jit(solution)/shard_map/ppermute | solution.py:30
  29.9 12.7 %collective-permute-start.7 = (f32[2,256,128]{2,1,0:T(8,128)S(1)}, f32[2,256,128]{2,1,0:T(8,128)S(1)}, u32[]{:S(2)}, u32[]{:S(2)}) collective-permute-start(f32[2,256,128]{2,1,0:T(8,128)S(1)} %get-tuple-element.57), channel_id=1, source_target_pairs={{1,0},{2,1},{3,2},{4,3},{5,4},{6,5},{7,6},{9,8},{10,9},{11,10},{12... | collective-permute-start | bytes 786440 | tf_op jit(solution)/shard_map/ppermute | solution.py:30
  33.2 15.6 %collective-permute-start.6 = (f32[2,128,256]{2,1,0:T(8,128)S(1)}, f32[2,128,256]{2,1,0:T(8,128)S(1)}, u32[]{:S(2)}, u32[]{:S(2)}) collective-permute-start(f32[2,128,256]{2,1,0:T(8,128)S(1)} %get-tuple-element.54), channel_id=1, source_target_pairs={{8,0},{9,1},{10,2},{11,3},{12,4},{13,5},{14,6},{15,7},{16,8},{17,9... | collective-permute-start | bytes 786440 | tf_op jit(solution)/shard_map/ppermute | solution.py:30
  36.2 8.0 %collective-permute-start.5 = (f32[2,128,128]{2,1,0:T(8,128)S(1)}, f32[2,128,128]{2,1,0:T(8,128)S(1)}, u32[]{:S(2)}, u32[]{:S(2)}) collective-permute-start(f32[2,128,128]{2,1,0:T(8,128)S(1)} %get-tuple-element.53), channel_id=1, source_target_pairs={{0,9},{1,10},{2,11},{3,12},{4,13},{5,14},{6,15},{8,17},{9,18},{10,... | collective-permute-start | bytes 393224 | tf_op jit(solution)/shard_map/ppermute | solution.py:30
  40.5 8.2 %collective-permute-start.8 = (f32[2,128,128]{2,1,0:T(8,128)S(1)}, f32[2,128,128]{2,1,0:T(8,128)S(1)}, u32[]{:S(2)}, u32[]{:S(2)}) collective-permute-start(f32[2,128,128]{2,1,0:T(8,128)S(1)} %get-tuple-element.58), channel_id=1, source_target_pairs={{9,0},{10,1},{11,2},{12,3},{13,4},{14,5},{15,6},{17,8},{18,9},{19,... | collective-permute-start | bytes 393224 | tf_op jit(solution)/shard_map/ppermute | solution.py:30
  50.5 13.8 %collective-permute-start.9 = (f32[2,128,256]{2,1,0:T(8,128)S(1)}, f32[2,128,256]{2,1,0:T(8,128)S(1)}, u32[]{:S(2)}, u32[]{:S(2)}) collective-permute-start(f32[2,128,256]{2,1,0:T(8,128)S(1)} %get-tuple-element.61), channel_id=1, source_target_pairs={{0,8},{1,9},{2,10},{3,11},{4,12},{5,13},{6,14},{7,15},{8,16},{9,17... | collective-permute-start | bytes 786440 | tf_op jit(solution)/shard_map/ppermute | solution.py:30
  54.5 9.9 %collective-permute-start.10 = (f32[2,256,128]{2,1,0:T(8,128)S(1)}, f32[2,256,128]{2,1,0:T(8,128)S(1)}, u32[]{:S(2)}, u32[]{:S(2)}) collective-permute-start(f32[2,256,128]{2,1,0:T(8,128)S(1)} %get-tuple-element.62), channel_id=1, source_target_pairs={{0,1},{1,2},{2,3},{3,4},{4,5},{5,6},{6,7},{8,9},{9,10},{10,11},{11... | collective-permute-start | bytes 786440 | tf_op jit(solution)/shard_map/ppermute | solution.py:30
  56.6 7.7 %collective-permute-start.11 = (f32[2,128,128]{2,1,0:T(8,128)S(1)}, f32[2,128,128]{2,1,0:T(8,128)S(1)}, u32[]{:S(2)}, u32[]{:S(2)}) collective-permute-start(f32[2,128,128]{2,1,0:T(8,128)S(1)} %get-tuple-element.63), channel_id=1, source_target_pairs={{0,9},{1,10},{2,11},{3,12},{4,13},{5,14},{6,15},{8,17},{9,18},{10,... | collective-permute-start | bytes 393224 | tf_op jit(solution)/shard_map/ppermute | solution.py:30
